TPU v7x, 256 devices: a whole 4x4x8 slice. The times are simulated.
256 devices in a mesh: src: 64 (over x, z, core), grp: 4 (over y).
Axes of the slice: x: 4, y: 4, z: 8, core: 2. Of those that a mesh axis runs over, the one named last changes fastest.
Arguments:
- currents: bfloat16 [524288, 1024], P(('src', 'grp')), may hold values from -6 to 6
- leaf_basis: bfloat16 [2, 40, 524288], P(None, None, ('src', 'grp')), may hold values from -6 to 6
- leaf_box: int32 [524288], P(('src', 'grp')), may hold values from 0 to 7, as said below
- box_count: int32 [2048], P(('src', 'grp')), may hold values from 1 to 2041, as said below
- merge_factor: bfloat16 [2, 2560, 81920], P(None, None, ('src', 'grp')), may hold values from -0.25 to 0.25
- angle_factor: bfloat16 [4096, 4, 2, 2560], P('src'), may hold values from -0.0390625 to 0.0390625
Outputs:
- normalized: float32 [4096, 512], P('src', 'grp')
- peak_value: float32 [512], P('grp')
Inputs may be any that keep to these rules, and one draw needn't show every extreme that they name: `leaf_box`: every source block of 2048 currents holds one or more currents of each of its 8 leaf boxes; some blocks put all but 7 of their currents into one box. box_count[k * 8 + b] is the number of currents of source block k whose leaf_box is b.
All inputs are finite; a program needn't handle non-finite values.
Results may differ from a plain program's by a relative error of at most 0.0057.
Values may be sent and summed in bfloat16 or wider, within the bound.
No kernel may reach another device: no remote copies, remote signals or barrier semaphores. Data moves between devices by JAX's collectives and lax.ppermute only.
A program may use at most 128 MiB of HBM per device.

v0:
```python
import jax
import jax.numpy as jnp
from jax import lax
from jax.experimental import pallas as pl
from jax.experimental.pallas import tpu as pltpu
from jax.sharding import Mesh
from jax.sharding import PartitionSpec as P


F32, BF16 = jnp.float32, jnp.bfloat16
NX, NZ, NC, NY = 4, 8, 2, 4
R, LEAF, S_DEV, NE, A = 40, 8, 2048, 512, 64
Q = NE // NY
LEAF_STEPS = 2
ZS = 2
SIZES = {"x": NX, "z": NZ, "c": NC, "y": NY}


def shift(v, axis, k):
    n = SIZES[axis]
    return lax.ppermute(v, axis, [(i, (i + k) % n) for i in range(n)])


def params(*sem):
    return pltpu.CompilerParams(dimension_semantics=sem, vmem_limit_bytes=56 * 2**20)


def source_kernel(count, me, box, basis, x_re, x_im, m, keep, send, op, stacked):
    step = pl.program_id(0)
    half = LEAF * R

    @pl.when(step == 0)
    def _():
        boxes = box[...]
        for part in range(2):
            wide = basis[part].astype(F32)
            for pair in range(LEAF // 2):
                rows = []
                for b in (2 * pair, 2 * pair + 1):
                    scale = lax.rsqrt(jnp.full((1, S_DEV), count[b].astype(F32), F32))
                    rows.append(wide * jnp.where(boxes == b, scale, 0.0))
                at = part * half + pair * 2 * R
                op[at : at + 2 * R, :] = jnp.concatenate(rows, axis=0).astype(BF16)

    width = NE // LEAF_STEPS
    for k in range(LEAF_STEPS):

        @pl.when(step == k)
        def _(k=k):
            first = jnp.dot(op[...], x_re[...], preferred_element_type=F32)
            second = jnp.dot(op[...], x_im[...], preferred_element_type=F32)
            re = first[:half] - second[half:]
            im = second[:half] + first[half:]
            left, right = pl.ds(k * width, width), pl.ds(NE + k * width, width)
            stacked[:half, left] = re.astype(BF16)
            stacked[half:, left] = (-im).astype(BF16)
            stacked[:half, right] = im.astype(BF16)
            stacked[half:, right] = re.astype(BF16)

    @pl.when(step >= LEAF_STEPS)
    def _():
        rows = m[...].reshape(2 * half, NZ * NC * R).T
        out = jnp.dot(rows, stacked[...], preferred_element_type=F32)

        def write(own):
            for z in range(NZ):
                for c in range(NC):
                    g = (z * NC + c) * R
                    tile = [out[g : g + R, :NE], out[g : g + R, NE:]]
                    (keep if c == own else send)[0, z] = jnp.concatenate(tile, axis=0).astype(BF16)

        for own in range(NC):
            pl.when(me[2] == own)(lambda own=own: write(own))


def source(count, me, box, basis, currents, m):
    out = jax.ShapeDtypeStruct((NX, NZ, 2 * R, NE), BF16)
    width = NE // LEAF_STEPS

    def leaf_at(i):
        return jnp.minimum(i, LEAF_STEPS - 1)

    def merge_at(i):
        return jnp.maximum(i - LEAF_STEPS, 0)

    return pl.pallas_call(
        source_kernel,
        grid_spec=pltpu.PrefetchScalarGridSpec(
            num_scalar_prefetch=2,
            grid=(LEAF_STEPS + NX,),
            in_specs=[
                pl.BlockSpec((1, S_DEV), lambda i, *n: (0, 0)),
                pl.BlockSpec((2, R, S_DEV), lambda i, *n: (0, 0, 0)),
                pl.BlockSpec((S_DEV, width), lambda i, *n: (0, leaf_at(i))),
                pl.BlockSpec((S_DEV, width), lambda i, *n: (0, leaf_at(i) + LEAF_STEPS)),
                pl.BlockSpec((2, LEAF * R, NZ * NC * R), lambda i, *n: (0, 0, merge_at(i))),
            ],
            out_specs=[pl.BlockSpec((1, NZ, 2 * R, NE), lambda i, *n: (merge_at(i), 0, 0, 0))] * 2,
            scratch_shapes=[
                pltpu.VMEM((2 * LEAF * R, S_DEV), BF16),
                pltpu.VMEM((2 * LEAF * R, 2 * NE), BF16),
            ],
        ),
        out_shape=[out, out],
        compiler_params=params("arbitrary"),
        name="source",
    )(count, me, box, basis, currents, currents, m)


def turn_kernel(f, out):
    out[...] = f[...].T


def turn(f):
    return pl.pallas_call(
        turn_kernel, out_shape=jax.ShapeDtypeStruct(f.shape[::-1], f.dtype), name="turn"
    )(f)


def factor_kernel(me, f, out):
    for z in range(NZ):
        both = f[0, z].astype(F32)
        first, second = both[:R], both[R:]
        own = jnp.where(me[2] == 0, first, second)
        other = jnp.where(me[2] == 0, second, first)
        rows = []
        for v in (own, other):
            rows += [v, jnp.concatenate([-v[:, A:], v[:, :A]], axis=1)]
        out[0, z] = jnp.concatenate(rows, axis=0).T.astype(BF16)


def factors(me, f):
    return pl.pallas_call(
        factor_kernel,
        grid_spec=pltpu.PrefetchScalarGridSpec(
            num_scalar_prefetch=1,
            grid=(NX,),
            in_specs=[pl.BlockSpec((1, NZ, 2 * R, 2 * A), lambda i, n: (i, 0, 0, 0))],
            out_specs=pl.BlockSpec((1, NZ, 2 * A, 4 * R), lambda i, n: (i, 0, 0, 0)),
        ),
        out_shape=jax.ShapeDtypeStruct((NX, NZ, 2 * A, 4 * R), BF16),
        compiler_params=params("arbitrary"),
        name="factors",
    )(me, f)


def pattern_kernel(me, keep, recv, fac, *refs):
    by_x, by_y, row = refs[:NX], refs[NX : NX + NY], refs[NX + NY]
    step = pl.program_id(0)

    def product(x, z):
        right = jnp.concatenate([keep[x, z], recv[x, z]], axis=0)
        return jnp.dot(fac[x, z], right, preferred_element_type=F32).astype(BF16)

    @pl.when(step < NZ // 2 // ZS)
    def _():
        for z in range(ZS):
            pieces = [product(lax.rem(me[0] + k, NX), z) for k in range(NX)]
            for k in range(NX):
                by_x[k][z] = pieces[k]

    @pl.when(step >= NZ // 2 // ZS)
    def _():
        for z in range(ZS):
            for x in range(NX):
                row[z, x] = product(x, z)
        for k in range(NY):
            at = pl.multiple_of(lax.rem(me[3] + k, NY) * Q, Q)
            by_y[k][...] = row[:, :, :, pl.ds(at, Q)]


def pattern(me, keep, recv, fac):
    h = NZ // 2 // ZS
    wide = pl.BlockSpec((ZS, 2 * A, NE), lambda i, n: (jnp.minimum(i, h - 1), 0, 0))
    cut = pl.BlockSpec((ZS, NX, 2 * A, Q), lambda i, n: (jnp.maximum(i - h, 0), 0, 0, 0))
    return pl.pallas_call(
        pattern_kernel,
        grid_spec=pltpu.PrefetchScalarGridSpec(
            num_scalar_prefetch=1,
            grid=(NZ // ZS,),
            in_specs=[
                pl.BlockSpec((NX, ZS, 2 * R, NE), lambda i, n: (0, i, 0, 0)),
                pl.BlockSpec((NX, ZS, 2 * R, NE), lambda i, n: (0, i, 0, 0)),
                pl.BlockSpec((NX, ZS, 2 * A, 4 * R), lambda i, n: (0, i, 0, 0)),
            ],
            out_specs=[wide] * NX + [cut] * NY,
            scratch_shapes=[pltpu.VMEM((ZS, NX, 2 * A, NE), BF16)],
        ),
        out_shape=[jax.ShapeDtypeStruct((NZ // 2, 2 * A, NE), BF16)] * NX
        + [jax.ShapeDtypeStruct((NZ // 2, NX, 2 * A, Q), BF16)] * NY,
        compiler_params=params("arbitrary"),
        name="pattern",
    )(me, keep, recv, fac)


def second_kernel(me, *refs):
    wide, cut = refs[:NX], refs[NX : NX + NY]
    by_y, by_x = refs[NX + NY : NX + 2 * NY], refs[NX + 2 * NY :]
    for z in range(NZ // 2):
        for k in range(NY):
            at = pl.multiple_of(lax.rem(me[3] + k, NY) * Q, Q)
            by_y[k][z] = sum(r[z, :, pl.ds(at, Q)].astype(F32) for r in wide).astype(BF16)
        for k in range(NX):
            x = lax.rem(me[0] + k, NX)
            by_x[k][z] = sum(r[z, x].astype(F32) for r in cut).astype(BF16)


def second(me, wide, cut):
    out = jax.ShapeDtypeStruct((NZ // 2, 2 * A, Q), BF16)
    vmem = pl.BlockSpec(memory_space=pltpu.VMEM)
    return pl.pallas_call(
        second_kernel,
        in_specs=[pl.BlockSpec(memory_space=pltpu.SMEM)] + [vmem] * (NX + NY),
        out_specs=[vmem] * (NY + NX),
        out_shape=[out] * (NY + NX),
        compiler_params=params(),
        name="second",
    )(me, *wide, *cut)


def third_kernel(*refs):
    out = refs[-1]
    h = NZ // 2
    out[:h] = sum(r[...].astype(F32) for r in refs[:NY]).astype(BF16)
    out[h:] = sum(r[...].astype(F32) for r in refs[NY:-1]).astype(BF16)


def third(parts):
    return pl.pallas_call(
        third_kernel,
        out_shape=jax.ShapeDtypeStruct((NZ, 2 * A, Q), BF16),
        name="third",
    )(*parts)


def last_kernel(parts, intensity, top):
    total = jnp.sum(parts[...].astype(F32), axis=0)
    value = total[:A] * total[:A] + total[A:] * total[A:]
    intensity[...] = value
    top[...] = jnp.max(value, axis=0, keepdims=True)


def last(parts):
    return pl.pallas_call(
        last_kernel,
        out_shape=[jax.ShapeDtypeStruct((A, Q), F32), jax.ShapeDtypeStruct((1, Q), F32)],
        name="last",
    )(parts)


def body(currents, leaf_basis, leaf_box, box_count, merge_factor, angle_factor):
    me = jnp.stack([lax.axis_index(a).astype(jnp.int32) for a in ("x", "z", "c", "y")])
    own = lax.dynamic_index_in_dim(angle_factor, lax.axis_index("y"), 1, keepdims=False)
    own = turn(own.transpose(1, 0, 2).reshape(2 * A, NX * NZ * NC * R))
    own = own.reshape(NX * NZ, NC * R, 2 * A)
    spread = lax.all_to_all(own, ("x", "z"), 0, 0, tiled=True)
    box = leaf_box.reshape(1, S_DEV)
    coefs = merge_factor.swapaxes(1, 2)
    keep, send = source(box_count, me, box, leaf_basis, currents, coefs)
    fac = factors(me, spread.reshape(NX, NZ, NC * R, 2 * A))
    recv = shift(send, "c", 1)
    cuts = pattern(me, keep, recv, fac)
    wide = [cuts[0]] + [shift(cuts[k], "x", k) for k in range(1, NX)]
    cut = [cuts[NX]] + [shift(cuts[NX + k], "y", k) for k in range(1, NY)]
    cuts = second(me, wide, cut)
    parts = [cuts[0]] + [shift(cuts[k], "y", k) for k in range(1, NY)]
    parts += [cuts[NY]] + [shift(cuts[NY + k], "x", k) for k in range(1, NX)]
    parts = lax.all_to_all(third(parts), "z", 0, 0, tiled=True)
    intensity, top = last(parts)
    tops = jnp.broadcast_to(top[None], (NX * NZ * NC, 1, Q))
    tops = lax.all_to_all(tops, ("x", "z", "c"), 0, 0, tiled=True)
    peak = jnp.max(tops, axis=(0, 1))
    return intensity / (peak[None, :] + 1.0), peak


def solution(mesh):
    split = Mesh(mesh.devices.reshape(NX, NZ, NC, NY), ("x", "z", "c", "y"))
    src, every = ("x", "z", "c"), ("x", "z", "c", "y")
    in_specs = (
        P(every, None),
        P(None, None, every),
        P(every),
        P(every),
        P(None, None, every),
        P(src, None, None, None),
    )
    out_specs = (P(src, "y"), P("y"))
    return jax.shard_map(body, mesh=split, in_specs=in_specs, out_specs=out_specs, check_vma=False)
```

profile of v0, /device:TPU:1, one launch (start us, length us, event | category | flops | bytes accessed | tf_op | source)
XLA Modules:
  0.0 151.9 jit_solution(5140822471724575895)
XLA Ops:
  0.6 0.0 copy-start
  0.7 0.6 pad_add_fusion.me
  1.3 13.1 %source.1 = (bf16[4,8,80,512]{3,2,1,0:T(8,128)(2,1)}, bf16[4,8,80,512]{3,2,1,0:T(8,128)(2,1)}) custom-call(s32[8]{0:T(128)} %count.1, s32[4]{0:T(128)} %pad_add_fusion.me, s32[1,2048]{1,0:T(1,128)} %bitcast.20, bf16[2,40,2048]{2,1,0:T(8,128)(2,1)} %basis.1, bf16[2048,1024]{1,0:T(8,128)(2,1)} %x_im.1, bf16[2048,1024]{1,0:T(8,128)(2,1)} %x_im.1, ...), custom_call_target="tpu_custom_call" | custom-call | tf_op jit(solution)/shard_map/source/pallas_call | solution.py:86
  14.4 3.2 %collective-permute-start = (bf16[4,8,80,512]{3,2,1,0:T(8,128)(2,1)}, bf16[4,8,80,512]{3,2,1,0:T(8,128)(2,1)}, u32[]{:S(2)}, u32[]{:S(2)}) collective-permute-start(bf16[4,8,80,512]{3,2,1,0:T(8,128)(2,1)} %get-tuple-element.23), channel_id=1, source_target_pairs={{0,4},{4,0},{1,5},{5,1},{2,6},{6,2},{3,7},{7,3},{8,12},{12,8},{9,1... | collective-permute-start | bytes 7864328 | tf_op jit(solution)/shard_map/ppermute | solution.py:21
  17.6 0.0 copy-done
  17.6 0.5 constant_dynamic-slice_fusion
  18.1 1.0 copy.12
  19.0 2.2 %turn.1 = bf16[2560,128]{1,0:T(8,128)(2,1)} custom-call(bf16[128,2560]{1,0:T(8,128)(2,1)} %bitcast.16), custom_call_target="tpu_custom_call" | custom-call | tf_op jit(solution)/shard_map/turn/pallas_call | solution.py:115
  21.2 26.6 %all_to_all.15 = bf16[32,80,128]{2,1,0:T(8,128)(2,1)} all-to-all(bf16[32,80,128]{2,1,0:T(8,128)(2,1)} %bitcast.17), channel_id=1, replica_groups=mesh['x'=4,'z'=8,'c'=2,'y'=4] {'x','z'}, dimensions={0} | all-to-all | bytes 1310720 | tf_op jit(solution)/shard_map/all_to_all | solution.py:256
  47.8 5.0 %factors.1.fac = bf16[4,8,128,160]{3,2,1,0:T(8,128)(2,1)} custom-call(s32[4]{0:T(128)} %pad_add_fusion.me, bf16[4,8,80,128]{3,2,1,0:T(8,128)(2,1)} %bitcast.18), custom_call_target="tpu_custom_call" | custom-call | tf_op jit(solution)/shard_map/factors/pallas_call | solution.py:133
  52.8 0.0 collective-permute-done.recv
  52.8 7.3 %pattern.1 = (bf16[4,128,512]{2,1,0:T(8,128)(2,1)}, bf16[4,128,512]{2,1,0:T(8,128)(2,1)}, bf16[4,128,512]{2,1,0:T(8,128)(2,1)}, bf16[4,128,512]{2,1,0:T(8,128)(2...) custom-call(s32[4]{0:T(128)} %pad_add_fusion.me, ...), custom_call_target="tpu_custom_call" | custom-call | tf_op jit(solution)/shard_map/pattern/pallas_call | solution.py:176
  60.1 0.6 collective-permute-start.1
  60.7 2.4 %collective-permute-start.2 = (bf16[4,128,512]{2,1,0:T(8,128)(2,1)}, bf16[4,128,512]{2,1,0:T(8,128)(2,1)S(1)}, u32[]{:S(2)}, u32[]{:S(2)}) collective-permute-start(bf16[4,128,512]{2,1,0:T(8,128)(2,1)} %get-tuple-element.26), channel_id=1, source_target_pairs={{0,128},{64,192},{128,0},{192,64},{1,129},{65,193},{129,1},{193,65... | collective-permute-start | bytes 1572872 | tf_op jit(solution)/shard_map/ppermute | solution.py:21
  63.1 1.2 collective-permute-start.3
  64.3 1.3 collective-permute-start.4
  65.6 2.6 %collective-permute-start.5 = (bf16[4,4,128,128]{3,2,1,0:T(8,128)(2,1)}, bf16[4,4,128,128]{3,2,1,0:T(8,128)(2,1)S(1)}, u32[]{:S(2)}, u32[]{:S(2)}) collective-permute-start(bf16[4,4,128,128]{3,2,1,0:T(8,128)(2,1)} %get-tuple-element.30), channel_id=1, source_target_pairs={{0,2},{1,3},{2,0},{3,1},{4,6},{5,7},{6,4},{7,5},{8,10},{9,11},{10,... | collective-permute-start | bytes 1572872 | tf_op jit(solution)/shard_map/ppermute | solution.py:21
  68.2 3.4 %collective-permute-done.1.refs_1_ = bf16[4,128,512]{2,1,0:T(8,128)(2,1)S(1)} collective-permute-done((bf16[4,128,512]{2,1,0:T(8,128)(2,1)}, bf16[4,128,512]{2,1,0:T(8,128)(2,1)S(1)}, u32[]{:S(2)}, u32[]{:S(2)}) %collective-permute-start.1) | collective-permute-done | bytes 524320 | tf_op jit(solution)/shard_map/ppermute | solution.py:21
  71.7 0.0 copy-start.1
  71.7 2.7 %collective-permute-start.6 = (bf16[4,4,128,128]{3,2,1,0:T(8,128)(2,1)}, bf16[4,4,128,128]{3,2,1,0:T(8,128)(2,1)S(1)}, u32[]{:S(2)}, u32[]{:S(2)}) collective-permute-start(bf16[4,4,128,128]{3,2,1,0:T(8,128)(2,1)} %get-tuple-element.31), channel_id=1, source_target_pairs={{0,3},{1,0},{2,1},{3,2},{4,7},{5,4},{6,5},{7,6},{8,11},{9,8},{10,9... | collective-permute-start | bytes 1572872 | tf_op jit(solution)/shard_map/ppermute | solution.py:21
  74.4 10.0 %collective-permute-done.2.refs_2_ = bf16[4,128,512]{2,1,0:T(8,128)(2,1)S(1)} collective-permute-done((bf16[4,128,512]{2,1,0:T(8,128)(2,1)}, bf16[4,128,512]{2,1,0:T(8,128)(2,1)S(1)}, u32[]{:S(2)}, u32[]{:S(2)}) %collective-permute-start.2) | collective-permute-done | bytes 524320 | tf_op jit(solution)/shard_map/ppermute | solution.py:21
  84.4 0.0 copy-start.2
  84.4 1.8 %collective-permute-done.3.refs_3_ = bf16[4,128,512]{2,1,0:T(8,128)(2,1)S(1)} collective-permute-done((bf16[4,128,512]{2,1,0:T(8,128)(2,1)}, bf16[4,128,512]{2,1,0:T(8,128)(2,1)S(1)}, u32[]{:S(2)}, u32[]{:S(2)}) %collective-permute-start.3) | collective-permute-done | bytes 524320 | tf_op jit(solution)/shard_map/ppermute | solution.py:21
  86.3 0.0 copy-start.3
  86.3 0.0 collective-permute-done.4.refs_5_
  86.3 0.0 copy-start.4
  86.3 2.2 %collective-permute-done.5.refs_6_ = bf16[4,4,128,128]{3,2,1,0:T(8,128)(2,1)S(1)} collective-permute-done((bf16[4,4,128,128]{3,2,1,0:T(8,128)(2,1)}, bf16[4,4,128,128]{3,2,1,0:T(8,128)(2,1)S(1)}, u32[]{:S(2)}, u32[]{:S(2)}) %collective-permute-start.5) | collective-permute-done | bytes 524320 | tf_op jit(solution)/shard_map/ppermute | solution.py:21
  88.5 0.0 copy-start.5
  88.5 0.0 collective-permute-done.6.refs_7_
  88.5 0.0 copy-start.6
  88.5 0.0 copy-done.1
  88.5 0.0 copy-done.2
  88.5 0.0 copy-done.3
  88.5 0.0 copy-done.4
  88.5 0.8 copy-done.5
  89.3 0.2 copy-done.6
  89.5 3.6 %second.1 = (bf16[4,128,128]{2,1,0:T(8,128)(2,1)}, bf16[4,128,128]{2,1,0:T(8,128)(2,1)}, bf16[4,128,128]{2,1,0:T(8,128)(2,1)}, bf16[4,128,128]{2,1,0:T(8,128)(2,...) custom-call(s32[4]{0:T(128)} %pad_add_fusion.me, ...), custom_call_target="tpu_custom_call" | custom-call | tf_op jit(solution)/shard_map/second/pallas_call | solution.py:211
  93.1 3.2 %collective-permute-start.7 = (bf16[4,128,128]{2,1,0:T(8,128)(2,1)}, bf16[4,128,128]{2,1,0:T(8,128)(2,1)S(1)}, u32[]{:S(2)}, u32[]{:S(2)}) collective-permute-start(bf16[4,128,128]{2,1,0:T(8,128)(2,1)} %get-tuple-element.33), channel_id=1, source_target_pairs={{0,1},{1,2},{2,3},{3,0},{4,5},{5,6},{6,7},{7,4},{8,9},{9,10},{10,1... | collective-permute-start | bytes 393224 | tf_op jit(solution)/shard_map/ppermute | solution.py:21
  96.3 0.1 collective-permute-start.8
  96.4 2.4 %collective-permute-start.9 = (bf16[4,128,128]{2,1,0:T(8,128)(2,1)}, bf16[4,128,128]{2,1,0:T(8,128)(2,1)S(1)}, u32[]{:S(2)}, u32[]{:S(2)}) collective-permute-start(bf16[4,128,128]{2,1,0:T(8,128)(2,1)} %get-tuple-element.35), channel_id=1, source_target_pairs={{0,3},{1,0},{2,1},{3,2},{4,7},{5,4},{6,5},{7,6},{8,11},{9,8},{10,9... | collective-permute-start | bytes 393224 | tf_op jit(solution)/shard_map/ppermute | solution.py:21
  98.7 0.3 collective-permute-start.10
  99.1 1.8 %collective-permute-start.11 = (bf16[4,128,128]{2,1,0:T(8,128)(2,1)}, bf16[4,128,128]{2,1,0:T(8,128)(2,1)S(1)}, u32[]{:S(2)}, u32[]{:S(2)}) collective-permute-start(bf16[4,128,128]{2,1,0:T(8,128)(2,1)} %get-tuple-element.38), channel_id=1, source_target_pairs={{0,128},{64,192},{128,0},{192,64},{1,129},{65,193},{129,1},{193,65... | collective-permute-start | bytes 393224 | tf_op jit(solution)/shard_map/ppermute | solution.py:21
  100.8 0.0 collective-permute-done.7.refs_1_
  100.8 0.0 copy-start.7
  100.8 0.7 collective-permute-start.12
  101.5 0.3 collective-permute-done.8.refs_2_
  101.9 0.0 copy-start.8
  101.9 0.0 collective-permute-done.9.refs_3_
  101.9 3.5 %collective-permute-done.10.refs_5_ = bf16[4,128,128]{2,1,0:T(8,128)(2,1)S(1)} collective-permute-done((bf16[4,128,128]{2,1,0:T(8,128)(2,1)}, bf16[4,128,128]{2,1,0:T(8,128)(2,1)S(1)}, u32[]{:S(2)}, u32[]{:S(2)}) %collective-permute-start.10) | collective-permute-done | bytes 131104 | tf_op jit(solution)/shard_map/ppermute | solution.py:21
  105.4 0.0 collective-permute-done.11.refs_6_
  105.4 0.6 collective-permute-done.12.refs_7_
  106.0 0.0 copy-done.7
  106.0 0.0 copy-done.8
  106.0 0.0 copy-done.9
  106.0 0.0 copy-done.10
  106.0 0.0 copy-done.11
  106.1 0.6 copy-done.12
  106.7 2.1 %third.1 = bf16[8,128,128]{2,1,0:T(8,128)(2,1)} custom-call(bf16[4,128,128]{2,1,0:T(8,128)(2,1)} %get-tuple-element.32.refs_0_, bf16[4,128,128]{2,1,0:T(8,128)(2,1)} %copy-done.7, bf16[4,128,128]{2,1,0:T(8,128)(2,1)} %copy-done.8, bf16[4,128,128]{2,1,0:T(8,128)(2,1)} %copy-done.9, bf16[4,128,128]{2,1,0:T(8,128)(2,1)} %get-tuple-element.36.refs_4_, ...), custom_call_target="tpu_custom_call" | custom-call | tf_op jit(solution)/shard_map/third/pallas_call | solution.py:229
  108.8 17.8 %all_to_all.16.parts = bf16[8,128,128]{2,1,0:T(8,128)(2,1)} all-to-all(bf16[8,128,128]{2,1,0:T(8,128)(2,1)} %third.1), channel_id=1, replica_groups=mesh['x'=4,'z'=8,'c'=2,'y'=4] {'z'}, dimensions={0} | all-to-all | bytes 524288 | tf_op jit(solution)/shard_map/all_to_all | solution.py:268
  126.5 1.6 %last.1 = (f32[64,128]{1,0:T(8,128)}, f32[1,128]{1,0:T(1,128)}) custom-call(bf16[8,128,128]{2,1,0:T(8,128)(2,1)} %all_to_all.16.parts), custom_call_target="tpu_custom_call" | custom-call | tf_op jit(solution)/shard_map/last/pallas_call | solution.py:244
  128.2 0.7 broadcast_in_dim.10
  128.8 21.7 %all_to_all.17 = f32[64,1,128]{2,1,0:T(1,128)S(1)} all-to-all(f32[64,1,128]{2,1,0:T(1,128)S(1)} %broadcast_in_dim.10), channel_id=1, replica_groups=mesh['x'=4,'z'=8,'c'=2,'y'=4] {'x','z','c'}, dimensions={0} | all-to-all | bytes 65536 | tf_op jit(solution)/shard_map/all_to_all | solution.py:271
  150.6 1.4 broadcast_divide_fusion
  151.9 0.0 copy-done.13
  (7 shorter events, 0.0 us)
Async XLA Ops:
  0.6 17.0 %copy-start = (bf16[64,4,2,2560]{3,2,1,0:T(2,128)(2,1)S(1)}, bf16[64,4,2,2560]{3,2,1,0:T(2,128)(2,1)}, u32[]{:S(2)}) copy-start(bf16[64,4,2,2560]{3,2,1,0:T(2,128)(2,1)} %param.11) | copy-start | bytes 7864324
  14.4 38.4 %collective-permute-start = (bf16[4,8,80,512]{3,2,1,0:T(8,128)(2,1)}, bf16[4,8,80,512]{3,2,1,0:T(8,128)(2,1)}, u32[]{:S(2)}, u32[]{:S(2)}) collective-permute-start(bf16[4,8,80,512]{3,2,1,0:T(8,128)(2,1)} %get-tuple-element.23), channel_id=1, source_target_pairs={{0,4},{4,0},{1,5},{5,1},{2,6},{6,2},{3,7},{7,3},{8,12},{12,8},{9,1... | collective-permute-start | bytes 7864328 | tf_op jit(solution)/shard_map/ppermute | solution.py:21
  60.1 11.6 %collective-permute-start.1 = (bf16[4,128,512]{2,1,0:T(8,128)(2,1)}, bf16[4,128,512]{2,1,0:T(8,128)(2,1)S(1)}, u32[]{:S(2)}, u32[]{:S(2)}) collective-permute-start(bf16[4,128,512]{2,1,0:T(8,128)(2,1)} %get-tuple-element.25), channel_id=1, source_target_pairs={{0,64},{64,128},{128,192},{192,0},{1,65},{65,129},{129,193},{193,1... | collective-permute-start | bytes 1572872 | tf_op jit(solution)/shard_map/ppermute | solution.py:21
  60.7 23.7 %collective-permute-start.2 = (bf16[4,128,512]{2,1,0:T(8,128)(2,1)}, bf16[4,128,512]{2,1,0:T(8,128)(2,1)S(1)}, u32[]{:S(2)}, u32[]{:S(2)}) collective-permute-start(bf16[4,128,512]{2,1,0:T(8,128)(2,1)} %get-tuple-element.26), channel_id=1, source_target_pairs={{0,128},{64,192},{128,0},{192,64},{1,129},{65,193},{129,1},{193,65... | collective-permute-start | bytes 1572872 | tf_op jit(solution)/shard_map/ppermute | solution.py:21
  63.1 23.1 %collective-permute-start.3 = (bf16[4,128,512]{2,1,0:T(8,128)(2,1)}, bf16[4,128,512]{2,1,0:T(8,128)(2,1)S(1)}, u32[]{:S(2)}, u32[]{:S(2)}) collective-permute-start(bf16[4,128,512]{2,1,0:T(8,128)(2,1)} %get-tuple-element.27), channel_id=1, source_target_pairs={{0,192},{64,0},{128,64},{192,128},{1,193},{65,1},{129,65},{193,129... | collective-permute-start | bytes 1572872 | tf_op jit(solution)/shard_map/ppermute | solution.py:21
  64.3 22.0 %collective-permute-start.4 = (bf16[4,4,128,128]{3,2,1,0:T(8,128)(2,1)}, bf16[4,4,128,128]{3,2,1,0:T(8,128)(2,1)S(1)}, u32[]{:S(2)}, u32[]{:S(2)}) collective-permute-start(bf16[4,4,128,128]{3,2,1,0:T(8,128)(2,1)} %get-tuple-element.29), channel_id=1, source_target_pairs={{0,1},{1,2},{2,3},{3,0},{4,5},{5,6},{6,7},{7,4},{8,9},{9,10},{10,1... | collective-permute-start | bytes 1572872 | tf_op jit(solution)/shard_map/ppermute | solution.py:21
  65.6 22.9 %collective-permute-start.5 = (bf16[4,4,128,128]{3,2,1,0:T(8,128)(2,1)}, bf16[4,4,128,128]{3,2,1,0:T(8,128)(2,1)S(1)}, u32[]{:S(2)}, u32[]{:S(2)}) collective-permute-start(bf16[4,4,128,128]{3,2,1,0:T(8,128)(2,1)} %get-tuple-element.30), channel_id=1, source_target_pairs={{0,2},{1,3},{2,0},{3,1},{4,6},{5,7},{6,4},{7,5},{8,10},{9,11},{10,... | collective-permute-start | bytes 1572872 | tf_op jit(solution)/shard_map/ppermute | solution.py:21
  71.7 16.8 %copy-start.1 = (bf16[4,128,512]{2,1,0:T(8,128)(2,1)}, bf16[4,128,512]{2,1,0:T(8,128)(2,1)S(1)}, u32[]{:S(2)}) copy-start(bf16[4,128,512]{2,1,0:T(8,128)(2,1)S(1)} %collective-permute-done.1.refs_1_) | copy-start | bytes 1572868
  71.7 16.8 %collective-permute-start.6 = (bf16[4,4,128,128]{3,2,1,0:T(8,128)(2,1)}, bf16[4,4,128,128]{3,2,1,0:T(8,128)(2,1)S(1)}, u32[]{:S(2)}, u32[]{:S(2)}) collective-permute-start(bf16[4,4,128,128]{3,2,1,0:T(8,128)(2,1)} %get-tuple-element.31), channel_id=1, source_target_pairs={{0,3},{1,0},{2,1},{3,2},{4,7},{5,4},{6,5},{7,6},{8,11},{9,8},{10,9... | collective-permute-start | bytes 1572872 | tf_op jit(solution)/shard_map/ppermute | solution.py:21
  84.4 4.1 %copy-start.2 = (bf16[4,128,512]{2,1,0:T(8,128)(2,1)}, bf16[4,128,512]{2,1,0:T(8,128)(2,1)S(1)}, u32[]{:S(2)}) copy-start(bf16[4,128,512]{2,1,0:T(8,128)(2,1)S(1)} %collective-permute-done.2.refs_2_) | copy-start | bytes 1572868
  86.3 2.2 %copy-start.3 = (bf16[4,128,512]{2,1,0:T(8,128)(2,1)}, bf16[4,128,512]{2,1,0:T(8,128)(2,1)S(1)}, u32[]{:S(2)}) copy-start(bf16[4,128,512]{2,1,0:T(8,128)(2,1)S(1)} %collective-permute-done.3.refs_3_) | copy-start | bytes 1572868
  86.3 2.2 %copy-start.4 = (bf16[4,4,128,128]{3,2,1,0:T(8,128)(2,1)}, bf16[4,4,128,128]{3,2,1,0:T(8,128)(2,1)S(1)}, u32[]{:S(2)}) copy-start(bf16[4,4,128,128]{3,2,1,0:T(8,128)(2,1)S(1)} %collective-permute-done.4.refs_5_) | copy-start | bytes 1572868
  88.5 0.8 copy-start.5
  88.5 1.0 copy-start.6
  93.1 7.8 %collective-permute-start.7 = (bf16[4,128,128]{2,1,0:T(8,128)(2,1)}, bf16[4,128,128]{2,1,0:T(8,128)(2,1)S(1)}, u32[]{:S(2)}, u32[]{:S(2)}) collective-permute-start(bf16[4,128,128]{2,1,0:T(8,128)(2,1)} %get-tuple-element.33), channel_id=1, source_target_pairs={{0,1},{1,2},{2,3},{3,0},{4,5},{5,6},{6,7},{7,4},{8,9},{9,10},{10,1... | collective-permute-start | bytes 393224 | tf_op jit(solution)/shard_map/ppermute | solution.py:21
  96.3 5.6 %collective-permute-start.8 = (bf16[4,128,128]{2,1,0:T(8,128)(2,1)}, bf16[4,128,128]{2,1,0:T(8,128)(2,1)S(1)}, u32[]{:S(2)}, u32[]{:S(2)}) collective-permute-start(bf16[4,128,128]{2,1,0:T(8,128)(2,1)} %get-tuple-element.34), channel_id=1, source_target_pairs={{0,2},{1,3},{2,0},{3,1},{4,6},{5,7},{6,4},{7,5},{8,10},{9,11},{10,... | collective-permute-start | bytes 393224 | tf_op jit(solution)/shard_map/ppermute | solution.py:21
  96.4 5.5 %collective-permute-start.9 = (bf16[4,128,128]{2,1,0:T(8,128)(2,1)}, bf16[4,128,128]{2,1,0:T(8,128)(2,1)S(1)}, u32[]{:S(2)}, u32[]{:S(2)}) collective-permute-start(bf16[4,128,128]{2,1,0:T(8,128)(2,1)} %get-tuple-element.35), channel_id=1, source_target_pairs={{0,3},{1,0},{2,1},{3,2},{4,7},{5,4},{6,5},{7,6},{8,11},{9,8},{10,9... | collective-permute-start | bytes 393224 | tf_op jit(solution)/shard_map/ppermute | solution.py:21
  98.7 6.6 %collective-permute-start.10 = (bf16[4,128,128]{2,1,0:T(8,128)(2,1)}, bf16[4,128,128]{2,1,0:T(8,128)(2,1)S(1)}, u32[]{:S(2)}, u32[]{:S(2)}) collective-permute-start(bf16[4,128,128]{2,1,0:T(8,128)(2,1)} %get-tuple-element.37), channel_id=1, source_target_pairs={{0,64},{64,128},{128,192},{192,0},{1,65},{65,129},{129,193},{193,1... | collective-permute-start | bytes 393224 | tf_op jit(solution)/shard_map/ppermute | solution.py:21
  99.1 6.3 %collective-permute-start.11 = (bf16[4,128,128]{2,1,0:T(8,128)(2,1)}, bf16[4,128,128]{2,1,0:T(8,128)(2,1)S(1)}, u32[]{:S(2)}, u32[]{:S(2)}) collective-permute-start(bf16[4,128,128]{2,1,0:T(8,128)(2,1)} %get-tuple-element.38), channel_id=1, source_target_pairs={{0,128},{64,192},{128,0},{192,64},{1,129},{65,193},{129,1},{193,65... | collective-permute-start | bytes 393224 | tf_op jit(solution)/shard_map/ppermute | solution.py:21
  100.8 5.2 %copy-start.7 = (bf16[4,128,128]{2,1,0:T(8,128)(2,1)}, bf16[4,128,128]{2,1,0:T(8,128)(2,1)S(1)}, u32[]{:S(2)}) copy-start(bf16[4,128,128]{2,1,0:T(8,128)(2,1)S(1)} %collective-permute-done.7.refs_1_) | copy-start | bytes 393220
  100.8 5.2 %collective-permute-start.12 = (bf16[4,128,128]{2,1,0:T(8,128)(2,1)}, bf16[4,128,128]{2,1,0:T(8,128)(2,1)S(1)}, u32[]{:S(2)}, u32[]{:S(2)}) collective-permute-start(bf16[4,128,128]{2,1,0:T(8,128)(2,1)} %get-tuple-element.39), channel_id=1, source_target_pairs={{0,192},{64,0},{128,64},{192,128},{1,193},{65,1},{129,65},{193,129... | collective-permute-start | bytes 393224 | tf_op jit(solution)/shard_map/ppermute | solution.py:21
  101.9 4.2 %copy-start.8 = (bf16[4,128,128]{2,1,0:T(8,128)(2,1)}, bf16[4,128,128]{2,1,0:T(8,128)(2,1)S(1)}, u32[]{:S(2)}) copy-start(bf16[4,128,128]{2,1,0:T(8,128)(2,1)S(1)} %collective-permute-done.8.refs_2_) | copy-start | bytes 393220
  101.9 4.2 %copy-start.9 = (bf16[4,128,128]{2,1,0:T(8,128)(2,1)}, bf16[4,128,128]{2,1,0:T(8,128)(2,1)S(1)}, u32[]{:S(2)}) copy-start(bf16[4,128,128]{2,1,0:T(8,128)(2,1)S(1)} %collective-permute-done.9.refs_3_) | copy-start | bytes 393220
  105.4 0.6 copy-start.10
  105.4 0.7 copy-start.11
  106.0 0.7 copy-start.12
  150.5 1.4 copy-start.13
where the time goes:
time: 153 us; the launch traced here: 152 us
  blocking collectives  66 us (43%)
  Pallas kernels  35 us (23%)
  starting transfers between devices  22.5 us (15%)
  waiting for transfers between devices  22 us (14%)
  local copies, waits for them, and re-layouts  3.71 us (2%)
  other arithmetic  2.03 us (1%)
    all_to_all x1, blocking collectives, body(): spread = lax.all_to_all(own, ('x', 'z'), 0, 0, tiled=True)  26.6 us
    ppermute x13, starting transfers between devices, shift(): return lax.ppermute(v, axis, [(i, (i + k) % n) for i in range(n)])  22.5 us
    ppermute x13, waiting for transfers between devices, shift(): return lax.ppermute(v, axis, [(i, (i + k) % n) for i in range(n)])  22 us
    all_to_all x1, blocking collectives, body(): tops = lax.all_to_all(tops, ('x', 'z', 'c'), 0, 0, tiled=True)  21.7 us
    all_to_all x1, blocking collectives, body(): parts = lax.all_to_all(third(parts), 'z', 0, 0, tiled=True)  17.8 us
    pallas_call x1, Pallas kernels, source(): pl.pallas_call(source_kernel, grid_spec=pltpu.PrefetchScalarGridSpec(num_...  13.1 us
    pallas_call x1, Pallas kernels, pattern(): pl.pallas_call(pattern_kernel, grid_spec=pltpu.PrefetchScalarGridSpec(num...  7.25 us
    pallas_call x1, Pallas kernels, factors(): pl.pallas_call(factor_kernel, grid_spec=pltpu.PrefetchScalarGridSpec(num_...  5.04 us
  transfers between devices with their start and end apart: 13, of which 7 were waited for; matrix products, arithmetic and copies ran while one was open for 1% of the time, Pallas kernels for 5%

commit v1 on v0

--- a/solution.py
+++ b/solution.py
@@ -12,7 +12,8 @@
 R, LEAF, S_DEV, NE, A = 40, 8, 2048, 512, 64
 Q = NE // NY
 LEAF_STEPS = 2
-ZS = 2
+CHUNKS = 2
+ORDER = (2, 1, 3)
 SIZES = {"x": NX, "z": NZ, "c": NC, "y": NY}
 
 
@@ -107,96 +108,87 @@
     )(count, me, box, basis, currents, currents, m)
 
 
-def turn_kernel(f, out):
-    out[...] = f[...].T
-
-
-def turn(f):
-    return pl.pallas_call(
-        turn_kernel, out_shape=jax.ShapeDtypeStruct(f.shape[::-1], f.dtype), name="turn"
-    )(f)
-
-
-def factor_kernel(me, f, out):
-    for z in range(NZ):
-        both = f[0, z].astype(F32)
-        first, second = both[:R], both[R:]
-        own = jnp.where(me[2] == 0, first, second)
-        other = jnp.where(me[2] == 0, second, first)
-        rows = []
-        for v in (own, other):
-            rows += [v, jnp.concatenate([-v[:, A:], v[:, :A]], axis=1)]
-        out[0, z] = jnp.concatenate(rows, axis=0).T.astype(BF16)
-
-
-def factors(me, f):
-    return pl.pallas_call(
-        factor_kernel,
+def turn_kernel(me, f, out):
+    wide = f[:, 0].astype(F32)
+    out[...] = jnp.concatenate([wide[:, 0], wide[:, 1]], axis=0).astype(BF16).T
+
+
+def turn(me, factor):
+    steps, columns = 4, factor.shape[3]
+    width = columns // steps
+    return pl.pallas_call(
+        turn_kernel,
         grid_spec=pltpu.PrefetchScalarGridSpec(
             num_scalar_prefetch=1,
-            grid=(NX,),
-            in_specs=[pl.BlockSpec((1, NZ, 2 * R, 2 * A), lambda i, n: (i, 0, 0, 0))],
-            out_specs=pl.BlockSpec((1, NZ, 2 * A, 4 * R), lambda i, n: (i, 0, 0, 0)),
-        ),
-        out_shape=jax.ShapeDtypeStruct((NX, NZ, 2 * A, 4 * R), BF16),
-        compiler_params=params("arbitrary"),
-        name="factors",
-    )(me, f)
+            grid=(steps,),
+            in_specs=[pl.BlockSpec((A, 1, 2, width), lambda i, n: (0, n[3], 0, i))],
+            out_specs=pl.BlockSpec((width, 2 * A), lambda i, n: (i, 0)),
+        ),
+        out_shape=jax.ShapeDtypeStruct((columns, 2 * A), BF16),
+        compiler_params=params("arbitrary"),
+        name="turn",
+    )(me, factor)
 
 
 def pattern_kernel(me, keep, recv, fac, *refs):
     by_x, by_y, row = refs[:NX], refs[NX : NX + NY], refs[NX + NY]
-    step = pl.program_id(0)
-
-    def product(x, z):
-        right = jnp.concatenate([keep[x, z], recv[x, z]], axis=0)
-        return jnp.dot(fac[x, z], right, preferred_element_type=F32).astype(BF16)
-
-    @pl.when(step < NZ // 2 // ZS)
-    def _():
-        for z in range(ZS):
-            pieces = [product(lax.rem(me[0] + k, NX), z) for k in range(NX)]
-            for k in range(NX):
-                by_x[k][z] = pieces[k]
-
-    @pl.when(step >= NZ // 2 // ZS)
-    def _():
-        for z in range(ZS):
-            for x in range(NX):
-                row[z, x] = product(x, z)
-        for k in range(NY):
-            at = pl.multiple_of(lax.rem(me[3] + k, NY) * Q, Q)
-            by_y[k][...] = row[:, :, :, pl.ds(at, Q)]
-
-
-def pattern(me, keep, recv, fac):
-    h = NZ // 2 // ZS
-    wide = pl.BlockSpec((ZS, 2 * A, NE), lambda i, n: (jnp.minimum(i, h - 1), 0, 0))
-    cut = pl.BlockSpec((ZS, NX, 2 * A, Q), lambda i, n: (jnp.maximum(i - h, 0), 0, 0, 0))
+    first = me[2] == 0
+
+    def product(x, part):
+        both = fac[x, part, 0].astype(F32)
+        turned = jnp.concatenate([-both[:, A:], both[:, :A]], axis=1)
+        left = jnp.concatenate([both[:R], turned[:R], both[R:], turned[R:]], axis=0).astype(BF16)
+        own, other = keep[x, part, 0], recv[x, part, 0]
+        right = jnp.concatenate(
+            [jnp.where(first, own, other), jnp.where(first, other, own)], axis=0
+        )
+        return jnp.dot(left.T, right, preferred_element_type=F32).astype(BF16)
+
+    pieces = [product(lax.rem(me[0] + k, NX), 0) for k in range(NX)]
+    for k in range(NX):
+        by_x[k][0] = pieces[k]
+    for x in range(NX):
+        row[x] = product(x, 1)
+    for k in range(NY):
+        at = pl.multiple_of(lax.rem(me[3] + k, NY) * Q, Q)
+        by_y[k][0] = row[:, :, pl.ds(at, Q)]
+
+
+def pattern(me, keep, recv, fac, chunk):
+    steps = NZ // 2 // CHUNKS
+
+    def halves(v):
+        return v.reshape((NX, 2, NZ // 2) + v.shape[2:])
+
+    def at(i, n):
+        return (0, 0, chunk * steps + i, 0, 0)
+
+    wide = pl.BlockSpec((1, 2 * A, NE), lambda i, n: (i, 0, 0))
+    cut = pl.BlockSpec((1, NX, 2 * A, Q), lambda i, n: (i, 0, 0, 0))
     return pl.pallas_call(
         pattern_kernel,
         grid_spec=pltpu.PrefetchScalarGridSpec(
             num_scalar_prefetch=1,
-            grid=(NZ // ZS,),
+            grid=(steps,),
             in_specs=[
-                pl.BlockSpec((NX, ZS, 2 * R, NE), lambda i, n: (0, i, 0, 0)),
-                pl.BlockSpec((NX, ZS, 2 * R, NE), lambda i, n: (0, i, 0, 0)),
-                pl.BlockSpec((NX, ZS, 2 * A, 4 * R), lambda i, n: (0, i, 0, 0)),
+                pl.BlockSpec((NX, 2, 1, 2 * R, NE), at),
+                pl.BlockSpec((NX, 2, 1, 2 * R, NE), at),
+                pl.BlockSpec((NX, 2, 1, 2 * R, 2 * A), at),
             ],
             out_specs=[wide] * NX + [cut] * NY,
-            scratch_shapes=[pltpu.VMEM((ZS, NX, 2 * A, NE), BF16)],
-        ),
-        out_shape=[jax.ShapeDtypeStruct((NZ // 2, 2 * A, NE), BF16)] * NX
-        + [jax.ShapeDtypeStruct((NZ // 2, NX, 2 * A, Q), BF16)] * NY,
+            scratch_shapes=[pltpu.VMEM((NX, 2 * A, NE), BF16)],
+        ),
+        out_shape=[jax.ShapeDtypeStruct((steps, 2 * A, NE), BF16)] * NX
+        + [jax.ShapeDtypeStruct((steps, NX, 2 * A, Q), BF16)] * NY,
         compiler_params=params("arbitrary"),
         name="pattern",
-    )(me, keep, recv, fac)
+    )(me, halves(keep), halves(recv), halves(fac))
 
 
 def second_kernel(me, *refs):
     wide, cut = refs[:NX], refs[NX : NX + NY]
-    by_y, by_x = refs[NX + NY : NX + 2 * NY], refs[NX + 2 * NY :]
-    for z in range(NZ // 2):
+    by_y, by_x = refs[-NY - NX : -NX], refs[-NX:]
+    for z in range(NZ // 2 // CHUNKS):
         for k in range(NY):
             at = pl.multiple_of(lax.rem(me[3] + k, NY) * Q, Q)
             by_y[k][z] = sum(r[z, :, pl.ds(at, Q)].astype(F32) for r in wide).astype(BF16)
@@ -205,17 +197,25 @@
             by_x[k][z] = sum(r[z, x].astype(F32) for r in cut).astype(BF16)
 
 
-def second(me, wide, cut):
+def second(me, wide, cut, chunk, earlier):
+    rows = NZ // 2 // CHUNKS
+    pieces = NY + NX
     out = jax.ShapeDtypeStruct((NZ // 2, 2 * A, Q), BF16)
-    vmem = pl.BlockSpec(memory_space=pltpu.VMEM)
     return pl.pallas_call(
         second_kernel,
-        in_specs=[pl.BlockSpec(memory_space=pltpu.SMEM)] + [vmem] * (NX + NY),
-        out_specs=[vmem] * (NY + NX),
-        out_shape=[out] * (NY + NX),
-        compiler_params=params(),
+        grid_spec=pltpu.PrefetchScalarGridSpec(
+            num_scalar_prefetch=1,
+            grid=(1,),
+            in_specs=[pl.BlockSpec((rows, 2 * A, NE), lambda i, n: (0, 0, 0))] * NX
+            + [pl.BlockSpec((rows, NX, 2 * A, Q), lambda i, n: (0, 0, 0, 0))] * NY
+            + [pl.BlockSpec(memory_space=pl.ANY)] * len(earlier),
+            out_specs=[pl.BlockSpec((rows, 2 * A, Q), lambda i, n: (chunk, 0, 0))] * pieces,
+        ),
+        out_shape=[out] * pieces,
+        input_output_aliases={1 + pieces + i: i for i in range(len(earlier))},
+        compiler_params=params("arbitrary"),
         name="second",
-    )(me, *wide, *cut)
+    )(me, *wide, *cut, *earlier)
 
 
 def third_kernel(*refs):
@@ -237,37 +237,48 @@
     total = jnp.sum(parts[...].astype(F32), axis=0)
     value = total[:A] * total[:A] + total[A:] * total[A:]
     intensity[...] = value
-    top[...] = jnp.max(value, axis=0, keepdims=True)
+    top[...] = jnp.broadcast_to(jnp.max(value, axis=0, keepdims=True)[None], top.shape)
 
 
 def last(parts):
     return pl.pallas_call(
         last_kernel,
-        out_shape=[jax.ShapeDtypeStruct((A, Q), F32), jax.ShapeDtypeStruct((1, Q), F32)],
+        out_shape=[
+            jax.ShapeDtypeStruct((A, Q), F32),
+            jax.ShapeDtypeStruct((NX * NZ * NC, 1, Q), F32),
+        ],
         name="last",
     )(parts)
 
 
+def exchange(first, second, axes):
+    firsts, seconds = [first[0]] + [None] * (NX - 1), [second[0]] + [None] * (NY - 1)
+    for k in ORDER:
+        firsts[k] = shift(first[k], axes[0], k)
+        seconds[k] = shift(second[k], axes[1], k)
+    return firsts, seconds
+
+
 def body(currents, leaf_basis, leaf_box, box_count, merge_factor, angle_factor):
     me = jnp.stack([lax.axis_index(a).astype(jnp.int32) for a in ("x", "z", "c", "y")])
-    own = lax.dynamic_index_in_dim(angle_factor, lax.axis_index("y"), 1, keepdims=False)
-    own = turn(own.transpose(1, 0, 2).reshape(2 * A, NX * NZ * NC * R))
+    own = turn(me, angle_factor)
     own = own.reshape(NX * NZ, NC * R, 2 * A)
     spread = lax.all_to_all(own, ("x", "z"), 0, 0, tiled=True)
     box = leaf_box.reshape(1, S_DEV)
     coefs = merge_factor.swapaxes(1, 2)
     keep, send = source(box_count, me, box, leaf_basis, currents, coefs)
-    fac = factors(me, spread.reshape(NX, NZ, NC * R, 2 * A))
+    fac = spread.reshape(NX, NZ, NC * R, 2 * A)
     recv = shift(send, "c", 1)
-    cuts = pattern(me, keep, recv, fac)
-    wide = [cuts[0]] + [shift(cuts[k], "x", k) for k in range(1, NX)]
-    cut = [cuts[NX]] + [shift(cuts[NX + k], "y", k) for k in range(1, NY)]
-    cuts = second(me, wide, cut)
-    parts = [cuts[0]] + [shift(cuts[k], "y", k) for k in range(1, NY)]
-    parts += [cuts[NY]] + [shift(cuts[NY + k], "x", k) for k in range(1, NX)]
-    parts = lax.all_to_all(third(parts), "z", 0, 0, tiled=True)
-    intensity, top = last(parts)
-    tops = jnp.broadcast_to(top[None], (NX * NZ * NC, 1, Q))
+    sent = []
+    for chunk in range(CHUNKS):
+        pieces = pattern(me, keep, recv, fac, chunk)
+        sent.append(exchange(pieces[:NX], pieces[NX:], ("x", "y")))
+    pieces = []
+    for chunk in range(CHUNKS):
+        pieces = second(me, *sent[chunk], chunk, pieces)
+    firsts, seconds = exchange(pieces[:NY], pieces[NY:], ("y", "x"))
+    parts = lax.all_to_all(third(firsts + seconds), "z", 0, 0, tiled=True)
+    intensity, tops = last(parts)
     tops = lax.all_to_all(tops, ("x", "z", "c"), 0, 0, tiled=True)
     peak = jnp.max(tops, axis=(0, 1))
     return intensity / (peak[None, :] + 1.0), peak

time: 153 us -> 152 us (level)
  waiting for transfers between devices: 22 us -> 18.7 us
  starting transfers between devices: 22.5 us -> 24.1 us
    ppermute x13 -> x19, waiting for transfers between devices: 22 us -> 18.7 us  [shift(): return lax.ppermute(v, axis, [(i, (i + k) % n) for i in range(n)])]
    all_to_all x1, blocking collectives: 21.7 us -> 19.2 us  [body(): tops = lax.all_to_all(tops, ('x', 'z', 'c'), 0, 0, tiled=True)]
    all_to_all x1, blocking collectives: 17.8 us -> 19.8 us  [body(): parts = lax.all_to_all(third(firsts + seconds), 'z', 0, 0, tiled=True)]
    pallas_call x1 -> x2, Pallas kernels: 7.25 us -> 9.11 us  [pattern(): pl.pallas_call(pattern_kernel, grid_spec=pltpu.PrefetchScalarGridSpec(num...]
    ppermute x13 -> x19, starting transfers between devices: 22.5 us -> 24.1 us  [shift(): return lax.ppermute(v, axis, [(i, (i + k) % n) for i in range(n)])]
  transfers between devices with their start and end apart: 13 -> 19, of which waited for: 7 -> 9; matrix products, arithmetic and copies ran while one was open for 1% -> 0% of each run, Pallas kernels for 5% -> 8%
where the time goes in v1:
time: 152 us; the launch traced here: 151 us
  blocking collectives  65.7 us (43%)
  Pallas kernels  36.4 us (24%)
  starting transfers between devices  24.1 us (16%)
  waiting for transfers between devices  18.7 us (12%)
  local copies, waits for them, and re-layouts  2.91 us (2%)
  other arithmetic  2.08 us (1%)
    all_to_all x1, blocking collectives, body(): spread = lax.all_to_all(own, ('x', 'z'), 0, 0, tiled=True)  26.7 us
    ppermute x19, starting transfers between devices, shift(): return lax.ppermute(v, axis, [(i, (i + k) % n) for i in range(n)])  24.1 us
    all_to_all x1, blocking collectives, body(): parts = lax.all_to_all(third(firsts + seconds), 'z', 0, 0, tiled=True)  19.8 us
    all_to_all x1, blocking collectives, body(): tops = lax.all_to_all(tops, ('x', 'z', 'c'), 0, 0, tiled=True)  19.2 us
    ppermute x19, waiting for transfers between devices, shift(): return lax.ppermute(v, axis, [(i, (i + k) % n) for i in range(n)])  18.7 us
    pallas_call x1, Pallas kernels, source(): pl.pallas_call(source_kernel, grid_spec=pltpu.PrefetchScalarGridSpec(num_...  13 us
    pallas_call x2, Pallas kernels, pattern(): pl.pallas_call(pattern_kernel, grid_spec=pltpu.PrefetchScalarGridSpec(num...  9.11 us
    pallas_call x2, Pallas kernels, second(): pl.pallas_call(second_kernel, grid_spec=pltpu.PrefetchScalarGridSpec(num_...  6.26 us
  transfers between devices with their start and end apart: 19, of which 9 were waited for; matrix products, arithmetic and copies ran while one was open for 0% of the time, Pallas kernels for 8%

profile of v1, /device:TPU:1, one launch (start us, length us, event | category | flops | bytes accessed | tf_op | source)
XLA Modules:
  0.0 150.8 jit_solution(8798285828071492577)
XLA Ops:
  0.6 0.6 pad_add_fusion.me
  1.2 13.0 %source.1 = (bf16[4,8,80,512]{3,2,1,0:T(8,128)(2,1)}, bf16[4,8,80,512]{3,2,1,0:T(8,128)(2,1)}) custom-call(s32[8]{0:T(128)} %count.1, s32[4]{0:T(128)} %pad_add_fusion.me, s32[1,2048]{1,0:T(1,128)} %bitcast.18, bf16[2,40,2048]{2,1,0:T(8,128)(2,1)} %basis.1, bf16[2048,1024]{1,0:T(8,128)(2,1)} %x_im.1, bf16[2048,1024]{1,0:T(8,128)(2,1)} %x_im.1, ...), custom_call_target="tpu_custom_call" | custom-call | tf_op jit(solution)/shard_map/source/pallas_call | solution.py:87
  14.3 3.2 %collective-permute-start = (bf16[4,8,80,512]{3,2,1,0:T(8,128)(2,1)}, bf16[4,8,80,512]{3,2,1,0:T(8,128)(2,1)S(1)}, u32[]{:S(2)}, u32[]{:S(2)}) collective-permute-start(bf16[4,8,80,512]{3,2,1,0:T(8,128)(2,1)} %get-tuple-element.39), channel_id=1, source_target_pairs={{0,4},{4,0},{1,5},{5,1},{2,6},{6,2},{3,7},{7,3},{8,12},{12,8},{9,1... | collective-permute-start | bytes 7864328 | tf_op jit(solution)/shard_map/ppermute | solution.py:22
  17.5 4.3 %turn.1 = bf16[2560,128]{1,0:T(8,128)(2,1)} custom-call(s32[4]{0:T(128)} %pad_add_fusion.me, bf16[64,4,2,2560]{3,2,1,0:T(2,128)(2,1)} %f.1), custom_call_target="tpu_custom_call" | custom-call | tf_op jit(solution)/shard_map/turn/pallas_call | solution.py:119
  21.8 26.7 %all_to_all.15 = bf16[32,80,128]{2,1,0:T(8,128)(2,1)} all-to-all(bf16[32,80,128]{2,1,0:T(8,128)(2,1)} %bitcast.17), channel_id=1, replica_groups=mesh['x'=4,'z'=8,'c'=2,'y'=4] {'x','z'}, dimensions={0} | all-to-all | bytes 1310720 | tf_op jit(solution)/shard_map/all_to_all | solution.py:266
  48.5 0.0 collective-permute-done
  48.5 1.5 copy-done
  50.0 4.6 %pattern.3 = (bf16[2,128,512]{2,1,0:T(8,128)(2,1)}, bf16[2,128,512]{2,1,0:T(8,128)(2,1)}, bf16[2,128,512]{2,1,0:T(8,128)(2,1)}, bf16[2,128,512]{2,1,0:T(8,128)(2...) custom-call(s32[4]{0:T(128)} %pad_add_fusion.me, ...), custom_call_target="tpu_custom_call" | custom-call | tf_op jit(solution)/shard_map/pattern/pallas_call | solution.py:168
  54.6 1.3 collective-permute-start.10
  55.9 2.6 %collective-permute-start.11 = (bf16[2,4,128,128]{3,2,1,0:T(8,128)(2,1)}, bf16[2,4,128,128]{3,2,1,0:T(8,128)(2,1)S(1)}, u32[]{:S(2)}, u32[]{:S(2)}) collective-permute-start(bf16[2,4,128,128]{3,2,1,0:T(8,128)(2,1)} %get-tuple-element.54), channel_id=1, source_target_pairs={{0,2},{1,3},{2,0},{3,1},{4,6},{5,7},{6,4},{7,5},{8,10},{9,11},{10,... | collective-permute-start | bytes 786440 | tf_op jit(solution)/shard_map/ppermute | solution.py:22
  58.5 1.1 collective-permute-start.12
  59.6 0.5 collective-permute-start.7
  60.1 4.5 %pattern.2 = (bf16[2,128,512]{2,1,0:T(8,128)(2,1)}, bf16[2,128,512]{2,1,0:T(8,128)(2,1)}, bf16[2,128,512]{2,1,0:T(8,128)(2,1)}, bf16[2,128,512]{2,1,0:T(8,128)(2...) custom-call(s32[4]{0:T(128)} %pad_add_fusion.me, ...), custom_call_target="tpu_custom_call" | custom-call | tf_op jit(solution)/shard_map/pattern/pallas_call | solution.py:168
  64.6 0.0 copy-done.21
  64.6 2.5 %collective-permute-start.8 = (bf16[2,128,512]{2,1,0:T(8,128)(2,1)S(1)}, bf16[2,128,512]{2,1,0:T(8,128)(2,1)S(1)}, u32[]{:S(2)}, u32[]{:S(2)}) collective-permute-start(bf16[2,128,512]{2,1,0:T(8,128)(2,1)S(1)} %copy-done.21), channel_id=1, source_target_pairs={{0,128},{64,192},{128,0},{192,64},{1,129},{65,193},{129,1},{193,65... | collective-permute-start | bytes 786440 | tf_op jit(solution)/shard_map/ppermute | solution.py:22
  67.1 0.0 collective-permute-done.10.refs_5_
  67.1 0.0 copy-done.20
  67.1 1.2 collective-permute-start.9
  68.4 0.0 collective-permute-done.11.refs_6_
  68.4 0.3 collective-permute-start.1
  68.7 0.0 collective-permute-done.12.refs_7_
  68.7 2.8 %collective-permute-start.2 = (bf16[2,128,512]{2,1,0:T(8,128)(2,1)}, bf16[2,128,512]{2,1,0:T(8,128)(2,1)S(1)}, u32[]{:S(2)}, u32[]{:S(2)}) collective-permute-start(bf16[2,128,512]{2,1,0:T(8,128)(2,1)} %get-tuple-element.42), channel_id=1, source_target_pairs={{0,128},{64,192},{128,0},{192,64},{1,129},{65,193},{129,1},{193,65... | collective-permute-start | bytes 786440 | tf_op jit(solution)/shard_map/ppermute | solution.py:22
  71.5 0.0 collective-permute-done.7.refs_1_
  71.5 0.7 collective-permute-start.3
  72.2 0.6 collective-permute-done.8.refs_2_
  72.9 1.3 collective-permute-start.4
  74.2 4.4 %collective-permute-done.9.refs_3_ = bf16[2,128,512]{2,1,0:T(8,128)(2,1)S(1)} collective-permute-done((bf16[2,128,512]{2,1,0:T(8,128)(2,1)S(1)}, bf16[2,128,512]{2,1,0:T(8,128)(2,1)S(1)}, u32[]{:S(2)}, u32[]{:S(2)}) %collective-permute-start.9) | collective-permute-done | bytes 262176 | tf_op jit(solution)/shard_map/ppermute | solution.py:22
  78.6 0.0 collective-permute-start.5
  78.6 4.8 %collective-permute-done.1.refs_1_ = bf16[2,128,512]{2,1,0:T(8,128)(2,1)S(1)} collective-permute-done((bf16[2,128,512]{2,1,0:T(8,128)(2,1)}, bf16[2,128,512]{2,1,0:T(8,128)(2,1)S(1)}, u32[]{:S(2)}, u32[]{:S(2)}) %collective-permute-start.1) | collective-permute-done | bytes 262176 | tf_op jit(solution)/shard_map/ppermute | solution.py:22
  83.3 0.0 collective-permute-start.6
  83.3 0.0 copy-done.1
  83.4 0.0 copy-done.2
  83.4 0.0 copy-done.3
  83.4 3.1 %second.2 = (bf16[4,128,128]{2,1,0:T(8,128)(2,1)}, bf16[4,128,128]{2,1,0:T(8,128)(2,1)}, bf16[4,128,128]{2,1,0:T(8,128)(2,1)}, bf16[4,128,128]{2,1,0:T(8,128)(2,...) custom-call(s32[4]{0:T(128)} %pad_add_fusion.me, ...), custom_call_target="tpu_custom_call" | custom-call | tf_op jit(solution)/shard_map/second/pallas_call | solution.py:204
  86.5 0.0 collective-permute-done.2.refs_2_
  86.5 1.3 collective-permute-done.3.refs_3_
  87.8 0.0 collective-permute-done.4.refs_5_
  87.9 0.0 collective-permute-done.5.refs_6_
  87.9 3.1 %collective-permute-done.6.refs_7_ = bf16[2,4,128,128]{3,2,1,0:T(8,128)(2,1)S(1)} collective-permute-done((bf16[2,4,128,128]{3,2,1,0:T(8,128)(2,1)}, bf16[2,4,128,128]{3,2,1,0:T(8,128)(2,1)S(1)}, u32[]{:S(2)}, u32[]{:S(2)}) %collective-permute-start.6) | collective-permute-done | bytes 262176 | tf_op jit(solution)/shard_map/ppermute | solution.py:22
  91.0 0.0 copy-done.8
  91.0 0.0 copy-done.10
  91.0 0.0 copy-done.11
  91.0 0.7 copy-done.12
  91.7 3.1 %second.3 = (bf16[4,128,128]{2,1,0:T(8,128)(2,1)}, bf16[4,128,128]{2,1,0:T(8,128)(2,1)}, bf16[4,128,128]{2,1,0:T(8,128)(2,1)}, bf16[4,128,128]{2,1,0:T(8,128)(2,...) custom-call(s32[4]{0:T(128)} %pad_add_fusion.me, ...), custom_call_target="tpu_custom_call", output_to_operand_aliasing={{0}: (9, {}), {1}: (10, {}), {2}: (11, {}), {3}: (12, {}), ... | custom-call | tf_op jit(solution)/shard_map/second/pallas_call | solution.py:204
  94.8 0.0 collective-permute-start.13
  94.9 1.2 collective-permute-start.14
  96.1 1.5 collective-permute-start.15
  97.5 1.2 collective-permute-start.16
  98.7 2.0 %collective-permute-start.17 = (bf16[4,128,128]{2,1,0:T(8,128)(2,1)}, bf16[4,128,128]{2,1,0:T(8,128)(2,1)S(1)}, u32[]{:S(2)}, u32[]{:S(2)}) collective-permute-start(bf16[4,128,128]{2,1,0:T(8,128)(2,1)} %get-tuple-element.70), channel_id=1, source_target_pairs={{0,128},{64,192},{128,0},{192,64},{1,129},{65,193},{129,1},{193,65... | collective-permute-start | bytes 393224 | tf_op jit(solution)/shard_map/ppermute | solution.py:22
  100.7 0.8 collective-permute-done.13.refs_1_
  101.5 0.6 collective-permute-start.18
  102.1 0.0 collective-permute-done.14.refs_2_
  102.1 0.0 collective-permute-done.15.refs_3_
  102.1 0.7 collective-permute-done.16.refs_5_
  102.8 1.9 %collective-permute-done.17.refs_6_ = bf16[4,128,128]{2,1,0:T(8,128)(2,1)S(1)} collective-permute-done((bf16[4,128,128]{2,1,0:T(8,128)(2,1)}, bf16[4,128,128]{2,1,0:T(8,128)(2,1)S(1)}, u32[]{:S(2)}, u32[]{:S(2)}) %collective-permute-start.17) | collective-permute-done | bytes 131104 | tf_op jit(solution)/shard_map/ppermute | solution.py:22
  104.7 1.2 collective-permute-done.18.refs_7_
  105.9 0.6 copy-done.18
  106.5 2.1 %third.1 = bf16[8,128,128]{2,1,0:T(8,128)(2,1)} custom-call(bf16[4,128,128]{2,1,0:T(8,128)(2,1)} %get-tuple-element.64.refs_0_, bf16[4,128,128]{2,1,0:T(8,128)(2,1)} %copy-done.13, bf16[4,128,128]{2,1,0:T(8,128)(2,1)} %copy-done.14, bf16[4,128,128]{2,1,0:T(8,128)(2,1)} %copy-done.15, bf16[4,128,128]{2,1,0:T(8,128)(2,1)} %get-tuple-element.68.refs_4_, ...), custom_call_target="tpu_custom_call" | custom-call | tf_op jit(solution)/shard_map/third/pallas_call | solution.py:229
  108.6 19.8 %all_to_all.16.parts = bf16[8,128,128]{2,1,0:T(8,128)(2,1)} all-to-all(bf16[8,128,128]{2,1,0:T(8,128)(2,1)} %third.1), channel_id=1, replica_groups=mesh['x'=4,'z'=8,'c'=2,'y'=4] {'z'}, dimensions={0} | all-to-all | bytes 524288 | tf_op jit(solution)/shard_map/all_to_all | solution.py:280
  128.4 1.6 %last.1 = (f32[64,128]{1,0:T(8,128)}, f32[64,1,128]{2,1,0:T(1,128)}) custom-call(bf16[8,128,128]{2,1,0:T(8,128)(2,1)} %all_to_all.16.parts), custom_call_target="tpu_custom_call" | custom-call | tf_op jit(solution)/shard_map/last/pallas_call | solution.py:244
  130.1 19.2 %all_to_all.17 = f32[64,1,128]{2,1,0:T(1,128)S(1)} all-to-all(f32[64,1,128]{2,1,0:T(1,128)} %get-tuple-element.73), channel_id=1, replica_groups=mesh['x'=4,'z'=8,'c'=2,'y'=4] {'x','z','c'}, dimensions={0} | all-to-all | bytes 65536 | tf_op jit(solution)/shard_map/all_to_all | solution.py:282
  149.3 0.1 reduce_max.9
  149.4 1.4 broadcast_divide_fusion
  150.8 0.0 copy-done.19
  (33 shorter events, 0.1 us)
Async XLA Ops:
  14.3 34.2 %collective-permute-start = (bf16[4,8,80,512]{3,2,1,0:T(8,128)(2,1)}, bf16[4,8,80,512]{3,2,1,0:T(8,128)(2,1)S(1)}, u32[]{:S(2)}, u32[]{:S(2)}) collective-permute-start(bf16[4,8,80,512]{3,2,1,0:T(8,128)(2,1)} %get-tuple-element.39), channel_id=1, source_target_pairs={{0,4},{4,0},{1,5},{5,1},{2,6},{6,2},{3,7},{7,3},{8,12},{12,8},{9,1... | collective-permute-start | bytes 7864328 | tf_op jit(solution)/shard_map/ppermute | solution.py:22
  48.5 1.5 %copy-start = (bf16[4,8,80,512]{3,2,1,0:T(8,128)(2,1)}, bf16[4,8,80,512]{3,2,1,0:T(8,128)(2,1)S(1)}, u32[]{:S(2)}) copy-start(bf16[4,8,80,512]{3,2,1,0:T(8,128)(2,1)S(1)} %collective-permute-done) | copy-start | bytes 7864324
  54.6 12.6 %collective-permute-start.10 = (bf16[2,4,128,128]{3,2,1,0:T(8,128)(2,1)}, bf16[2,4,128,128]{3,2,1,0:T(8,128)(2,1)S(1)}, u32[]{:S(2)}, u32[]{:S(2)}) collective-permute-start(bf16[2,4,128,128]{3,2,1,0:T(8,128)(2,1)} %get-tuple-element.53), channel_id=1, source_target_pairs={{0,1},{1,2},{2,3},{3,0},{4,5},{5,6},{6,7},{7,4},{8,9},{9,10},{10,1... | collective-permute-start | bytes 786440 | tf_op jit(solution)/shard_map/ppermute | solution.py:22
  55.9 12.5 %collective-permute-start.11 = (bf16[2,4,128,128]{3,2,1,0:T(8,128)(2,1)}, bf16[2,4,128,128]{3,2,1,0:T(8,128)(2,1)S(1)}, u32[]{:S(2)}, u32[]{:S(2)}) collective-permute-start(bf16[2,4,128,128]{3,2,1,0:T(8,128)(2,1)} %get-tuple-element.54), channel_id=1, source_target_pairs={{0,2},{1,3},{2,0},{3,1},{4,6},{5,7},{6,4},{7,5},{8,10},{9,11},{10,... | collective-permute-start | bytes 786440 | tf_op jit(solution)/shard_map/ppermute | solution.py:22
  58.5 10.2 %collective-permute-start.12 = (bf16[2,4,128,128]{3,2,1,0:T(8,128)(2,1)}, bf16[2,4,128,128]{3,2,1,0:T(8,128)(2,1)S(1)}, u32[]{:S(2)}, u32[]{:S(2)}) collective-permute-start(bf16[2,4,128,128]{3,2,1,0:T(8,128)(2,1)} %get-tuple-element.55), channel_id=1, source_target_pairs={{0,3},{1,0},{2,1},{3,2},{4,7},{5,4},{6,5},{7,6},{8,11},{9,8},{10,9... | collective-permute-start | bytes 786440 | tf_op jit(solution)/shard_map/ppermute | solution.py:22
  59.6 5.0 %copy-start.21 = (bf16[2,128,512]{2,1,0:T(8,128)(2,1)S(1)}, bf16[2,128,512]{2,1,0:T(8,128)(2,1)}, u32[]{:S(2)}) copy-start(bf16[2,128,512]{2,1,0:T(8,128)(2,1)} %get-tuple-element.50) | copy-start | bytes 786436
  59.6 7.6 %copy-start.20 = (bf16[2,128,512]{2,1,0:T(8,128)(2,1)S(1)}, bf16[2,128,512]{2,1,0:T(8,128)(2,1)}, u32[]{:S(2)}) copy-start(bf16[2,128,512]{2,1,0:T(8,128)(2,1)} %get-tuple-element.51) | copy-start | bytes 786436
  59.6 11.9 %collective-permute-start.7 = (bf16[2,128,512]{2,1,0:T(8,128)(2,1)}, bf16[2,128,512]{2,1,0:T(8,128)(2,1)S(1)}, u32[]{:S(2)}, u32[]{:S(2)}) collective-permute-start(bf16[2,128,512]{2,1,0:T(8,128)(2,1)} %get-tuple-element.49), channel_id=1, source_target_pairs={{0,64},{64,128},{128,192},{192,0},{1,65},{65,129},{129,193},{193,1... | collective-permute-start | bytes 786440 | tf_op jit(solution)/shard_map/ppermute | solution.py:22
  64.6 8.2 %collective-permute-start.8 = (bf16[2,128,512]{2,1,0:T(8,128)(2,1)S(1)}, bf16[2,128,512]{2,1,0:T(8,128)(2,1)S(1)}, u32[]{:S(2)}, u32[]{:S(2)}) collective-permute-start(bf16[2,128,512]{2,1,0:T(8,128)(2,1)S(1)} %copy-done.21), channel_id=1, source_target_pairs={{0,128},{64,192},{128,0},{192,64},{1,129},{65,193},{129,1},{193,65... | collective-permute-start | bytes 786440 | tf_op jit(solution)/shard_map/ppermute | solution.py:22
  67.1 16.2 %copy-start.1 = (bf16[2,4,128,128]{3,2,1,0:T(8,128)(2,1)}, bf16[2,4,128,128]{3,2,1,0:T(8,128)(2,1)S(1)}, u32[]{:S(2)}) copy-start(bf16[2,4,128,128]{3,2,1,0:T(8,128)(2,1)S(1)} %collective-permute-done.10.refs_5_) | copy-start | bytes 786436
  67.1 11.4 %collective-permute-start.9 = (bf16[2,128,512]{2,1,0:T(8,128)(2,1)S(1)}, bf16[2,128,512]{2,1,0:T(8,128)(2,1)S(1)}, u32[]{:S(2)}, u32[]{:S(2)}) collective-permute-start(bf16[2,128,512]{2,1,0:T(8,128)(2,1)S(1)} %copy-done.20), channel_id=1, source_target_pairs={{0,192},{64,0},{128,64},{192,128},{1,193},{65,1},{129,65},{193,129... | collective-permute-start | bytes 786440 | tf_op jit(solution)/shard_map/ppermute | solution.py:22
  68.4 15.0 %copy-start.2 = (bf16[2,4,128,128]{3,2,1,0:T(8,128)(2,1)}, bf16[2,4,128,128]{3,2,1,0:T(8,128)(2,1)S(1)}, u32[]{:S(2)}) copy-start(bf16[2,4,128,128]{3,2,1,0:T(8,128)(2,1)S(1)} %collective-permute-done.11.refs_6_) | copy-start | bytes 786436
  68.4 15.0 %collective-permute-start.1 = (bf16[2,128,512]{2,1,0:T(8,128)(2,1)}, bf16[2,128,512]{2,1,0:T(8,128)(2,1)S(1)}, u32[]{:S(2)}, u32[]{:S(2)}) collective-permute-start(bf16[2,128,512]{2,1,0:T(8,128)(2,1)} %get-tuple-element.41), channel_id=1, source_target_pairs={{0,64},{64,128},{128,192},{192,0},{1,65},{65,129},{129,193},{193,1... | collective-permute-start | bytes 786440 | tf_op jit(solution)/shard_map/ppermute | solution.py:22
  68.7 14.7 %copy-start.3 = (bf16[2,4,128,128]{3,2,1,0:T(8,128)(2,1)}, bf16[2,4,128,128]{3,2,1,0:T(8,128)(2,1)S(1)}, u32[]{:S(2)}) copy-start(bf16[2,4,128,128]{3,2,1,0:T(8,128)(2,1)S(1)} %collective-permute-done.12.refs_7_) | copy-start | bytes 786436
  68.7 17.8 %collective-permute-start.2 = (bf16[2,128,512]{2,1,0:T(8,128)(2,1)}, bf16[2,128,512]{2,1,0:T(8,128)(2,1)S(1)}, u32[]{:S(2)}, u32[]{:S(2)}) collective-permute-start(bf16[2,128,512]{2,1,0:T(8,128)(2,1)} %get-tuple-element.42), channel_id=1, source_target_pairs={{0,128},{64,192},{128,0},{192,64},{1,129},{65,193},{129,1},{193,65... | collective-permute-start | bytes 786440 | tf_op jit(solution)/shard_map/ppermute | solution.py:22
  71.5 11.8 %copy-start.4 = (bf16[2,128,512]{2,1,0:T(8,128)(2,1)}, bf16[2,128,512]{2,1,0:T(8,128)(2,1)S(1)}, u32[]{:S(2)}) copy-start(bf16[2,128,512]{2,1,0:T(8,128)(2,1)S(1)} %collective-permute-done.7.refs_1_) | copy-start | bytes 786436
  71.5 16.3 %collective-permute-start.3 = (bf16[2,128,512]{2,1,0:T(8,128)(2,1)}, bf16[2,128,512]{2,1,0:T(8,128)(2,1)S(1)}, u32[]{:S(2)}, u32[]{:S(2)}) collective-permute-start(bf16[2,128,512]{2,1,0:T(8,128)(2,1)} %get-tuple-element.43), channel_id=1, source_target_pairs={{0,192},{64,0},{128,64},{192,128},{1,193},{65,1},{129,65},{193,129... | collective-permute-start | bytes 786440 | tf_op jit(solution)/shard_map/ppermute | solution.py:22
  72.9 10.5 %copy-start.5 = (bf16[2,128,512]{2,1,0:T(8,128)(2,1)}, bf16[2,128,512]{2,1,0:T(8,128)(2,1)S(1)}, u32[]{:S(2)}) copy-start(bf16[2,128,512]{2,1,0:T(8,128)(2,1)S(1)} %collective-permute-done.8.refs_2_) | copy-start | bytes 786436
  72.9 15.0 %collective-permute-start.4 = (bf16[2,4,128,128]{3,2,1,0:T(8,128)(2,1)}, bf16[2,4,128,128]{3,2,1,0:T(8,128)(2,1)S(1)}, u32[]{:S(2)}, u32[]{:S(2)}) collective-permute-start(bf16[2,4,128,128]{3,2,1,0:T(8,128)(2,1)} %get-tuple-element.45), channel_id=1, source_target_pairs={{0,1},{1,2},{2,3},{3,0},{4,5},{5,6},{6,7},{7,4},{8,9},{9,10},{10,1... | collective-permute-start | bytes 786440 | tf_op jit(solution)/shard_map/ppermute | solution.py:22
  78.6 4.8 %copy-start.6 = (bf16[2,128,512]{2,1,0:T(8,128)(2,1)}, bf16[2,128,512]{2,1,0:T(8,128)(2,1)S(1)}, u32[]{:S(2)}) copy-start(bf16[2,128,512]{2,1,0:T(8,128)(2,1)S(1)} %collective-permute-done.9.refs_3_) | copy-start | bytes 786436
  78.6 9.3 %collective-permute-start.5 = (bf16[2,4,128,128]{3,2,1,0:T(8,128)(2,1)}, bf16[2,4,128,128]{3,2,1,0:T(8,128)(2,1)S(1)}, u32[]{:S(2)}, u32[]{:S(2)}) collective-permute-start(bf16[2,4,128,128]{3,2,1,0:T(8,128)(2,1)} %get-tuple-element.46), channel_id=1, source_target_pairs={{0,2},{1,3},{2,0},{3,1},{4,6},{5,7},{6,4},{7,5},{8,10},{9,11},{10,... | collective-permute-start | bytes 786440 | tf_op jit(solution)/shard_map/ppermute | solution.py:22
  83.3 7.6 %copy-start.7 = (bf16[2,128,512]{2,1,0:T(8,128)(2,1)}, bf16[2,128,512]{2,1,0:T(8,128)(2,1)S(1)}, u32[]{:S(2)}) copy-start(bf16[2,128,512]{2,1,0:T(8,128)(2,1)S(1)} %collective-permute-done.1.refs_1_) | copy-start | bytes 786436
  83.3 7.6 %collective-permute-start.6 = (bf16[2,4,128,128]{3,2,1,0:T(8,128)(2,1)}, bf16[2,4,128,128]{3,2,1,0:T(8,128)(2,1)S(1)}, u32[]{:S(2)}, u32[]{:S(2)}) collective-permute-start(bf16[2,4,128,128]{3,2,1,0:T(8,128)(2,1)} %get-tuple-element.47), channel_id=1, source_target_pairs={{0,3},{1,0},{2,1},{3,2},{4,7},{5,4},{6,5},{7,6},{8,11},{9,8},{10,9... | collective-permute-start | bytes 786440 | tf_op jit(solution)/shard_map/ppermute | solution.py:22
  86.5 4.5 %copy-start.8 = (bf16[2,128,512]{2,1,0:T(8,128)(2,1)}, bf16[2,128,512]{2,1,0:T(8,128)(2,1)S(1)}, u32[]{:S(2)}) copy-start(bf16[2,128,512]{2,1,0:T(8,128)(2,1)S(1)} %collective-permute-done.2.refs_2_) | copy-start | bytes 786436
  87.8 3.1 %copy-start.9 = (bf16[2,128,512]{2,1,0:T(8,128)(2,1)}, bf16[2,128,512]{2,1,0:T(8,128)(2,1)S(1)}, u32[]{:S(2)}) copy-start(bf16[2,128,512]{2,1,0:T(8,128)(2,1)S(1)} %collective-permute-done.3.refs_3_) | copy-start | bytes 786436
  87.8 3.1 %copy-start.10 = (bf16[2,4,128,128]{3,2,1,0:T(8,128)(2,1)}, bf16[2,4,128,128]{3,2,1,0:T(8,128)(2,1)S(1)}, u32[]{:S(2)}) copy-start(bf16[2,4,128,128]{3,2,1,0:T(8,128)(2,1)S(1)} %collective-permute-done.4.refs_5_) | copy-start | bytes 786436
  87.9 3.1 %copy-start.11 = (bf16[2,4,128,128]{3,2,1,0:T(8,128)(2,1)}, bf16[2,4,128,128]{3,2,1,0:T(8,128)(2,1)S(1)}, u32[]{:S(2)}) copy-start(bf16[2,4,128,128]{3,2,1,0:T(8,128)(2,1)S(1)} %collective-permute-done.5.refs_6_) | copy-start | bytes 786436
  91.0 0.7 copy-start.12
  94.8 6.7 %collective-permute-start.13 = (bf16[4,128,128]{2,1,0:T(8,128)(2,1)}, bf16[4,128,128]{2,1,0:T(8,128)(2,1)S(1)}, u32[]{:S(2)}, u32[]{:S(2)}) collective-permute-start(bf16[4,128,128]{2,1,0:T(8,128)(2,1)} %get-tuple-element.65), channel_id=1, source_target_pairs={{0,1},{1,2},{2,3},{3,0},{4,5},{5,6},{6,7},{7,4},{8,9},{9,10},{10,1... | collective-permute-start | bytes 393224 | tf_op jit(solution)/shard_map/ppermute | solution.py:22
  94.9 7.2 %collective-permute-start.14 = (bf16[4,128,128]{2,1,0:T(8,128)(2,1)}, bf16[4,128,128]{2,1,0:T(8,128)(2,1)S(1)}, u32[]{:S(2)}, u32[]{:S(2)}) collective-permute-start(bf16[4,128,128]{2,1,0:T(8,128)(2,1)} %get-tuple-element.66), channel_id=1, source_target_pairs={{0,2},{1,3},{2,0},{3,1},{4,6},{5,7},{6,4},{7,5},{8,10},{9,11},{10,... | collective-permute-start | bytes 393224 | tf_op jit(solution)/shard_map/ppermute | solution.py:22
  96.1 6.0 %collective-permute-start.15 = (bf16[4,128,128]{2,1,0:T(8,128)(2,1)}, bf16[4,128,128]{2,1,0:T(8,128)(2,1)S(1)}, u32[]{:S(2)}, u32[]{:S(2)}) collective-permute-start(bf16[4,128,128]{2,1,0:T(8,128)(2,1)} %get-tuple-element.67), channel_id=1, source_target_pairs={{0,3},{1,0},{2,1},{3,2},{4,7},{5,4},{6,5},{7,6},{8,11},{9,8},{10,9... | collective-permute-start | bytes 393224 | tf_op jit(solution)/shard_map/ppermute | solution.py:22
  97.5 5.2 %collective-permute-start.16 = (bf16[4,128,128]{2,1,0:T(8,128)(2,1)}, bf16[4,128,128]{2,1,0:T(8,128)(2,1)S(1)}, u32[]{:S(2)}, u32[]{:S(2)}) collective-permute-start(bf16[4,128,128]{2,1,0:T(8,128)(2,1)} %get-tuple-element.69), channel_id=1, source_target_pairs={{0,64},{64,128},{128,192},{192,0},{1,65},{65,129},{129,193},{193,1... | collective-permute-start | bytes 393224 | tf_op jit(solution)/shard_map/ppermute | solution.py:22
  98.7 5.9 %collective-permute-start.17 = (bf16[4,128,128]{2,1,0:T(8,128)(2,1)}, bf16[4,128,128]{2,1,0:T(8,128)(2,1)S(1)}, u32[]{:S(2)}, u32[]{:S(2)}) collective-permute-start(bf16[4,128,128]{2,1,0:T(8,128)(2,1)} %get-tuple-element.70), channel_id=1, source_target_pairs={{0,128},{64,192},{128,0},{192,64},{1,129},{65,193},{129,1},{193,65... | collective-permute-start | bytes 393224 | tf_op jit(solution)/shard_map/ppermute | solution.py:22
  101.5 4.3 %copy-start.13 = (bf16[4,128,128]{2,1,0:T(8,128)(2,1)}, bf16[4,128,128]{2,1,0:T(8,128)(2,1)S(1)}, u32[]{:S(2)}) copy-start(bf16[4,128,128]{2,1,0:T(8,128)(2,1)S(1)} %collective-permute-done.13.refs_1_) | copy-start | bytes 393220
  101.5 4.3 %collective-permute-start.18 = (bf16[4,128,128]{2,1,0:T(8,128)(2,1)}, bf16[4,128,128]{2,1,0:T(8,128)(2,1)S(1)}, u32[]{:S(2)}, u32[]{:S(2)}) collective-permute-start(bf16[4,128,128]{2,1,0:T(8,128)(2,1)} %get-tuple-element.71), channel_id=1, source_target_pairs={{0,192},{64,0},{128,64},{192,128},{1,193},{65,1},{129,65},{193,129... | collective-permute-start | bytes 393224 | tf_op jit(solution)/shard_map/ppermute | solution.py:22
  102.1 3.7 %copy-start.14 = (bf16[4,128,128]{2,1,0:T(8,128)(2,1)}, bf16[4,128,128]{2,1,0:T(8,128)(2,1)S(1)}, u32[]{:S(2)}) copy-start(bf16[4,128,128]{2,1,0:T(8,128)(2,1)S(1)} %collective-permute-done.14.refs_2_) | copy-start | bytes 393220
  102.1 3.7 %copy-start.15 = (bf16[4,128,128]{2,1,0:T(8,128)(2,1)}, bf16[4,128,128]{2,1,0:T(8,128)(2,1)S(1)}, u32[]{:S(2)}) copy-start(bf16[4,128,128]{2,1,0:T(8,128)(2,1)S(1)} %collective-permute-done.15.refs_3_) | copy-start | bytes 393220
  102.8 3.1 %copy-start.16 = (bf16[4,128,128]{2,1,0:T(8,128)(2,1)}, bf16[4,128,128]{2,1,0:T(8,128)(2,1)S(1)}, u32[]{:S(2)}) copy-start(bf16[4,128,128]{2,1,0:T(8,128)(2,1)S(1)} %collective-permute-done.16.refs_5_) | copy-start | bytes 393220
  104.7 1.2 copy-start.17
  105.8 0.7 copy-start.18
  149.4 1.4 copy-start.19

commit v2 on v1

--- a/solution.py
+++ b/solution.py
@@ -13,7 +13,7 @@
 Q = NE // NY
 LEAF_STEPS = 2
 CHUNKS = 2
-ORDER = (2, 1, 3)
+ORDER = (1, 3, 2)
 SIZES = {"x": NX, "z": NZ, "c": NC, "y": NY}
 
 
@@ -22,8 +22,8 @@
     return lax.ppermute(v, axis, [(i, (i + k) % n) for i in range(n)])
 
 
-def params(*sem):
-    return pltpu.CompilerParams(dimension_semantics=sem, vmem_limit_bytes=56 * 2**20)
+def params(*sem, mb=16):
+    return pltpu.CompilerParams(dimension_semantics=sem, vmem_limit_bytes=mb * 2**20)
 
 
 def source_kernel(count, me, box, basis, x_re, x_im, m, keep, send, op, stacked):
@@ -103,7 +103,7 @@
             ],
         ),
         out_shape=[out, out],
-        compiler_params=params("arbitrary"),
+        compiler_params=params("arbitrary", mb=28),
         name="source",
     )(count, me, box, basis, currents, currents, m)
 
@@ -229,6 +229,7 @@
     return pl.pallas_call(
         third_kernel,
         out_shape=jax.ShapeDtypeStruct((NZ, 2 * A, Q), BF16),
+        compiler_params=params(mb=4),
         name="third",
     )(*parts)
 
@@ -247,6 +248,7 @@
             jax.ShapeDtypeStruct((A, Q), F32),
             jax.ShapeDtypeStruct((NX * NZ * NC, 1, Q), F32),
         ],
+        compiler_params=params(mb=4),
         name="last",
     )(parts)
 

time: 152 us -> 136 us (0.89)
  Pallas kernels: 36.4 us -> 18.4 us
  local copies, waits for them, and re-layouts: 2.91 us -> 6.45 us
  starting transfers between devices: 24.1 us -> 26.4 us
    pallas_call x2, Pallas kernels: 6.26 us -> 1.63 us  [second(): pl.pallas_call(second_kernel, grid_spec=pltpu.PrefetchScalarGridSpec(num_...]
    pallas_call x2, Pallas kernels: 9.11 us -> 4.95 us  [pattern(): pl.pallas_call(pattern_kernel, grid_spec=pltpu.PrefetchScalarGridSpec(num...]
    unnamed x44 -> x14, local copies, waits for them, and re-layouts: 2.91 us -> 6.45 us
    pallas_call x1, Pallas kernels: 13 us -> 10 us  [source(): pl.pallas_call(source_kernel, grid_spec=pltpu.PrefetchScalarGridSpec(num_...]
    pallas_call x1, Pallas kernels: 4.31 us -> 1.6 us  [turn(): pl.pallas_call(turn_kernel, grid_spec=pltpu.PrefetchScalarGridSpec(num_sc...]
    ppermute x19, starting transfers between devices: 24.1 us -> 26.4 us  [shift(): return lax.ppermute(v, axis, [(i, (i + k) % n) for i in range(n)])]
    pallas_call x1, Pallas kernels: 2.1 us -> 0.13 us  [third(): pl.pallas_call(third_kernel, out_shape=jax.ShapeDtypeStruct((NZ, 2 * A, Q...]
    pallas_call x1, Pallas kernels: 1.63 us -> 0.07 us  [last(): pl.pallas_call(last_kernel, out_shape=[jax.ShapeDtypeStruct((A, Q), F32),...]
  transfers between devices with their start and end apart: 19 -> 19, of which waited for: 9 -> 8; matrix products, arithmetic and copies ran while one was open for 0% -> 0% of each run, Pallas kernels for 8% -> 4%
where the time goes in v2:
time: 136 us
  blocking collectives  64.5 us (47%)
  starting transfers between devices  26.4 us (19%)
  waiting for transfers between devices  18.5 us (14%)
  Pallas kernels  18.4 us (14%)
  local copies, waits for them, and re-layouts  6.45 us (5%)
    ppermute x19, starting transfers between devices, shift(): return lax.ppermute(v, axis, [(i, (i + k) % n) for i in range(n)])  26.4 us
    all_to_all x1, blocking collectives, body(): spread = lax.all_to_all(own, ('x', 'z'), 0, 0, tiled=True)  26.2 us
    all_to_all x1, blocking collectives, body(): parts = lax.all_to_all(third(firsts + seconds), 'z', 0, 0, tiled=True)  19.9 us
    ppermute x19, waiting for transfers between devices, shift(): return lax.ppermute(v, axis, [(i, (i + k) % n) for i in range(n)])  18.5 us
    all_to_all x1, blocking collectives, body(): tops = lax.all_to_all(tops, ('x', 'z', 'c'), 0, 0, tiled=True)  18.4 us
    pallas_call x1, Pallas kernels, source(): pl.pallas_call(source_kernel, grid_spec=pltpu.PrefetchScalarGridSpec(num_...  10 us
    unnamed x14, local copies, waits for them, and re-layouts  6.45 us
    pallas_call x2, Pallas kernels, pattern(): pl.pallas_call(pattern_kernel, grid_spec=pltpu.PrefetchScalarGridSpec(num...  4.95 us
  transfers between devices with their start and end apart: 19, of which 8 were waited for; matrix products, arithmetic and copies ran while one was open for 0% of the time, Pallas kernels for 4%

profile of v2, /device:TPU:1, one launch (start us, length us, event | category | flops | bytes accessed | tf_op | source)
XLA Modules:
  0.0 135.8 jit_solution(9435505691771548651)
XLA Ops:
  0.6 0.1 pad_add_fusion.me
  0.7 0.0 copy-start
  0.7 2.2 %copy-done = bf16[2048,1024]{1,0:T(8,128)(2,1)S(1)} copy-done((bf16[2048,1024]{1,0:T(8,128)(2,1)S(1)}, bf16[2048,1024]{1,0:T(8,128)(2,1)}, u32[]{:S(2)}) %copy-start) | copy-done | bytes 4194328
  2.9 1.9 %copy-done.1 = bf16[2,2560,320]{1,2,0:T(8,128)(2,1)S(1)} copy-done((bf16[2,2560,320]{1,2,0:T(8,128)(2,1)S(1)}, bf16[2,2560,320]{1,2,0:T(8,128)(2,1)}, u32[]{:S(2)}) %copy-start.1) | copy-done | bytes 3276824
  4.8 0.0 copy-start.3
  4.8 1.0 copy-done.3
  5.8 0.7 copy-done.4
  6.5 0.0 copy-start.5
  6.5 0.7 copy-done.5
  7.2 0.0 copy-start.2
  7.2 10.0 %source.1 = (bf16[4,8,80,512]{3,2,1,0:T(8,128)(2,1)S(1)}, bf16[4,8,80,512]{3,2,1,0:T(8,128)(2,1)S(1)}) custom-call(s32[8]{0:T(128)S(1)} %copy-done.5, s32[4]{0:T(128)S(1)} %pad_add_fusion.me, s32[1,2048]{1,0:T(1,128)S(1)} %bitcast.18, bf16[2,40,2048]{2,1,0:T(8,128)(2,1)S(1)} %copy-done.3, bf16[2048,1024]{1,0:T(8,128)(2,1)S(1)} %copy-done, ...), custom_call_target="tpu_custom_call" | custom-call | tf_op jit(solution)/shard_map/source/pallas_call | solution.py:87
  17.2 3.3 %collective-permute-start = (bf16[4,8,80,512]{3,2,1,0:T(8,128)(2,1)S(1)}, bf16[4,8,80,512]{3,2,1,0:T(8,128)(2,1)S(1)}, u32[]{:S(2)}, u32[]{:S(2)}) collective-permute-start(bf16[4,8,80,512]{3,2,1,0:T(8,128)(2,1)S(1)} %get-tuple-element.39), channel_id=1, source_target_pairs={{0,4},{4,0},{1,5},{5,1},{2,6},{6,2},{3,7},{7,3},{8,12},{12,8},{9,1... | collective-permute-start | bytes 7864328 | tf_op jit(solution)/shard_map/ppermute | solution.py:22
  20.5 0.0 copy-done.2
  20.5 1.6 %turn.1 = bf16[2560,128]{1,0:T(8,128)(2,1)S(1)} custom-call(s32[4]{0:T(128)S(1)} %pad_add_fusion.me, bf16[64,4,2,2560]{3,2,1,0:T(2,128)(2,1)S(1)} %copy-done.2), custom_call_target="tpu_custom_call" | custom-call | tf_op jit(solution)/shard_map/turn/pallas_call | solution.py:119
  22.1 26.2 %all_to_all.15 = bf16[32,80,128]{2,1,0:T(8,128)(2,1)S(1)} all-to-all(bf16[32,80,128]{2,1,0:T(8,128)(2,1)S(1)} %bitcast.17), channel_id=1, replica_groups=mesh['x'=4,'z'=8,'c'=2,'y'=4] {'x','z'}, dimensions={0} | all-to-all | bytes 1310720 | tf_op jit(solution)/shard_map/all_to_all | solution.py:268
  48.3 0.0 collective-permute-done
  48.3 2.5 %pattern.3 = (bf16[2,128,512]{2,1,0:T(8,128)(2,1)S(1)}, bf16[2,128,512]{2,1,0:T(8,128)(2,1)S(1)}, bf16[2,128,512]{2,1,0:T(8,128)(2,1)S(1)}, bf16[2,128,512]{2,1,...) custom-call(s32[4]{0:T(128)S(1)} %pad_add_fusion.me, ...), custom_call_target="tpu_custom_call" | custom-call | tf_op jit(solution)/shard_map/pattern/pallas_call | solution.py:168
  50.8 1.4 %collective-permute-start.10 = (bf16[2,4,128,128]{3,2,1,0:T(8,128)(2,1)S(1)}, bf16[2,4,128,128]{3,2,1,0:T(8,128)(2,1)S(1)}, u32[]{:S(2)}, u32[]{:S(2)}) collective-permute-start(bf16[2,4,128,128]{3,2,1,0:T(8,128)(2,1)S(1)} %get-tuple-element.53), channel_id=1, source_target_pairs={{0,1},{1,2},{2,3},{3,0},{4,5},{5,6},{6,7},{7,4},{8,9},{9,10},{10,1... | collective-permute-start | bytes 786440 | tf_op jit(solution)/shard_map/ppermute | solution.py:22
  52.2 2.6 %collective-permute-start.11 = (bf16[2,4,128,128]{3,2,1,0:T(8,128)(2,1)S(1)}, bf16[2,4,128,128]{3,2,1,0:T(8,128)(2,1)S(1)}, u32[]{:S(2)}, u32[]{:S(2)}) collective-permute-start(bf16[2,4,128,128]{3,2,1,0:T(8,128)(2,1)S(1)} %get-tuple-element.54), channel_id=1, source_target_pairs={{0,2},{1,3},{2,0},{3,1},{4,6},{5,7},{6,4},{7,5},{8,10},{9,11},{10,... | collective-permute-start | bytes 786440 | tf_op jit(solution)/shard_map/ppermute | solution.py:22
  54.8 1.1 collective-permute-start.12
  55.9 0.6 collective-permute-start.7
  56.5 2.5 %pattern.2 = (bf16[2,128,512]{2,1,0:T(8,128)(2,1)S(1)}, bf16[2,128,512]{2,1,0:T(8,128)(2,1)S(1)}, bf16[2,128,512]{2,1,0:T(8,128)(2,1)S(1)}, bf16[2,128,512]{2,1,...) custom-call(s32[4]{0:T(128)S(1)} %pad_add_fusion.me, ...), custom_call_target="tpu_custom_call" | custom-call | tf_op jit(solution)/shard_map/pattern/pallas_call | solution.py:168
  59.0 2.5 %collective-permute-start.8 = (bf16[2,128,512]{2,1,0:T(8,128)(2,1)S(1)}, bf16[2,128,512]{2,1,0:T(8,128)(2,1)S(1)}, u32[]{:S(2)}, u32[]{:S(2)}) collective-permute-start(bf16[2,128,512]{2,1,0:T(8,128)(2,1)S(1)} %get-tuple-element.50), channel_id=1, source_target_pairs={{0,128},{64,192},{128,0},{192,64},{1,129},{65,193},{129,1},{193,65... | collective-permute-start | bytes 786440 | tf_op jit(solution)/shard_map/ppermute | solution.py:22
  61.5 0.0 collective-permute-done.10.refs_5_
  61.5 1.2 collective-permute-start.9
  62.7 0.6 collective-permute-done.11.refs_6_
  63.2 1.0 collective-permute-start.1
  64.3 0.0 collective-permute-done.12.refs_7_
  64.3 3.4 %collective-permute-start.2 = (bf16[2,128,512]{2,1,0:T(8,128)(2,1)S(1)}, bf16[2,128,512]{2,1,0:T(8,128)(2,1)S(1)}, u32[]{:S(2)}, u32[]{:S(2)}) collective-permute-start(bf16[2,128,512]{2,1,0:T(8,128)(2,1)S(1)} %get-tuple-element.42), channel_id=1, source_target_pairs={{0,128},{64,192},{128,0},{192,64},{1,129},{65,193},{129,1},{193,65... | collective-permute-start | bytes 786440 | tf_op jit(solution)/shard_map/ppermute | solution.py:22
  67.7 0.0 collective-permute-done.7.refs_1_
  67.7 0.6 collective-permute-start.3
  68.4 0.0 collective-permute-done.8.refs_2_
  68.4 2.0 %collective-permute-start.4 = (bf16[2,4,128,128]{3,2,1,0:T(8,128)(2,1)S(1)}, bf16[2,4,128,128]{3,2,1,0:T(8,128)(2,1)S(1)}, u32[]{:S(2)}, u32[]{:S(2)}) collective-permute-start(bf16[2,4,128,128]{3,2,1,0:T(8,128)(2,1)S(1)} %get-tuple-element.45), channel_id=1, source_target_pairs={{0,1},{1,2},{2,3},{3,0},{4,5},{5,6},{6,7},{7,4},{8,9},{9,10},{10,1... | collective-permute-start | bytes 786440 | tf_op jit(solution)/shard_map/ppermute | solution.py:22
  70.4 0.0 collective-permute-done.9.refs_3_
  70.4 1.2 collective-permute-start.5
  71.6 7.0 %collective-permute-done.1.refs_1_ = bf16[2,128,512]{2,1,0:T(8,128)(2,1)S(1)} collective-permute-done((bf16[2,128,512]{2,1,0:T(8,128)(2,1)S(1)}, bf16[2,128,512]{2,1,0:T(8,128)(2,1)S(1)}, u32[]{:S(2)}, u32[]{:S(2)}) %collective-permute-start.1) | collective-permute-done | bytes 262176 | tf_op jit(solution)/shard_map/ppermute | solution.py:22
  78.6 0.0 collective-permute-start.6
  78.6 0.8 second.2
  79.4 0.8 collective-permute-done.2.refs_2_
  80.2 0.3 collective-permute-done.3.refs_3_
  80.5 0.0 collective-permute-done.4.refs_5_
  80.5 0.0 collective-permute-done.5.refs_6_
  80.5 4.6 %collective-permute-done.6.refs_7_ = bf16[2,4,128,128]{3,2,1,0:T(8,128)(2,1)S(1)} collective-permute-done((bf16[2,4,128,128]{3,2,1,0:T(8,128)(2,1)S(1)}, bf16[2,4,128,128]{3,2,1,0:T(8,128)(2,1)S(1)}, u32[]{:S(2)}, u32[]{:S(2)}) %collective-permute-start.6) | collective-permute-done | bytes 262176 | tf_op jit(solution)/shard_map/ppermute | solution.py:22
  85.1 0.8 second.3
  85.9 0.1 collective-permute-start.13
  86.0 1.1 collective-permute-start.14
  87.1 1.5 %collective-permute-start.15 = (bf16[4,128,128]{2,1,0:T(8,128)(2,1)S(1)}, bf16[4,128,128]{2,1,0:T(8,128)(2,1)S(1)}, u32[]{:S(2)}, u32[]{:S(2)}) collective-permute-start(bf16[4,128,128]{2,1,0:T(8,128)(2,1)S(1)} %get-tuple-element.67), channel_id=1, source_target_pairs={{0,3},{1,0},{2,1},{3,2},{4,7},{5,4},{6,5},{7,6},{8,11},{9,8},{10,9... | collective-permute-start | bytes 393224 | tf_op jit(solution)/shard_map/ppermute | solution.py:22
  88.7 1.0 collective-permute-start.16
  89.6 1.0 collective-permute-start.17
  90.6 1.8 %collective-permute-done.13.refs_1_ = bf16[4,128,128]{2,1,0:T(8,128)(2,1)S(1)} collective-permute-done((bf16[4,128,128]{2,1,0:T(8,128)(2,1)S(1)}, bf16[4,128,128]{2,1,0:T(8,128)(2,1)S(1)}, u32[]{:S(2)}, u32[]{:S(2)}) %collective-permute-start.13) | collective-permute-done | bytes 131104 | tf_op jit(solution)/shard_map/ppermute | solution.py:22
  92.4 0.7 collective-permute-start.18
  93.1 0.0 collective-permute-done.14.refs_2_
  93.1 0.0 collective-permute-done.15.refs_3_
  93.1 2.0 %collective-permute-done.16.refs_5_ = bf16[4,128,128]{2,1,0:T(8,128)(2,1)S(1)} collective-permute-done((bf16[4,128,128]{2,1,0:T(8,128)(2,1)S(1)}, bf16[4,128,128]{2,1,0:T(8,128)(2,1)S(1)}, u32[]{:S(2)}, u32[]{:S(2)}) %collective-permute-start.16) | collective-permute-done | bytes 131104 | tf_op jit(solution)/shard_map/ppermute | solution.py:22
  95.1 0.0 collective-permute-done.17.refs_6_
  95.1 1.4 %collective-permute-done.18.refs_7_ = bf16[4,128,128]{2,1,0:T(8,128)(2,1)S(1)} collective-permute-done((bf16[4,128,128]{2,1,0:T(8,128)(2,1)S(1)}, bf16[4,128,128]{2,1,0:T(8,128)(2,1)S(1)}, u32[]{:S(2)}, u32[]{:S(2)}) %collective-permute-start.18) | collective-permute-done | bytes 131104 | tf_op jit(solution)/shard_map/ppermute | solution.py:22
  96.5 0.1 third.1
  96.7 19.9 %all_to_all.16.parts = bf16[8,128,128]{2,1,0:T(8,128)(2,1)S(1)} all-to-all(bf16[8,128,128]{2,1,0:T(8,128)(2,1)S(1)} %third.1), channel_id=1, replica_groups=mesh['x'=4,'z'=8,'c'=2,'y'=4] {'z'}, dimensions={0} | all-to-all | bytes 524288 | tf_op jit(solution)/shard_map/all_to_all | solution.py:282
  116.6 0.1 last.1
  116.7 18.4 %all_to_all.17 = f32[64,1,128]{2,1,0:T(1,128)S(1)} all-to-all(f32[64,1,128]{2,1,0:T(1,128)S(1)} %get-tuple-element.73), channel_id=1, replica_groups=mesh['x'=4,'z'=8,'c'=2,'y'=4] {'x','z','c'}, dimensions={0} | all-to-all | bytes 65536 | tf_op jit(solution)/shard_map/all_to_all | solution.py:284
  135.1 0.1 reduce_max.9
  135.1 0.0 copy-start.6
  135.2 0.6 broadcast_divide_fusion
  135.8 0.0 copy-done.6
  (3 shorter events, 0.0 us)
Async XLA Ops:
  0.7 2.2 %copy-start = (bf16[2048,1024]{1,0:T(8,128)(2,1)S(1)}, bf16[2048,1024]{1,0:T(8,128)(2,1)}, u32[]{:S(2)}) copy-start(bf16[2048,1024]{1,0:T(8,128)(2,1)} %x_im.1) | copy-start | bytes 12582916
  2.9 1.9 %copy-start.1 = (bf16[2,2560,320]{1,2,0:T(8,128)(2,1)S(1)}, bf16[2,2560,320]{1,2,0:T(8,128)(2,1)}, u32[]{:S(2)}) copy-start(bf16[2,2560,320]{1,2,0:T(8,128)(2,1)} %param.10) | copy-start | bytes 9830404
  4.8 1.0 copy-start.3
  5.8 0.7 copy-start.4
  6.5 0.7 copy-start.5
  7.2 13.4 %copy-start.2 = (bf16[64,4,2,2560]{3,2,1,0:T(2,128)(2,1)S(1)}, bf16[64,4,2,2560]{3,2,1,0:T(2,128)(2,1)}, u32[]{:S(2)}) copy-start(bf16[64,4,2,2560]{3,2,1,0:T(2,128)(2,1)} %f.1) | copy-start | bytes 7864324
  17.2 31.1 %collective-permute-start = (bf16[4,8,80,512]{3,2,1,0:T(8,128)(2,1)S(1)}, bf16[4,8,80,512]{3,2,1,0:T(8,128)(2,1)S(1)}, u32[]{:S(2)}, u32[]{:S(2)}) collective-permute-start(bf16[4,8,80,512]{3,2,1,0:T(8,128)(2,1)S(1)} %get-tuple-element.39), channel_id=1, source_target_pairs={{0,4},{4,0},{1,5},{5,1},{2,6},{6,2},{3,7},{7,3},{8,12},{12,8},{9,1... | collective-permute-start | bytes 7864328 | tf_op jit(solution)/shard_map/ppermute | solution.py:22
  50.8 10.7 %collective-permute-start.10 = (bf16[2,4,128,128]{3,2,1,0:T(8,128)(2,1)S(1)}, bf16[2,4,128,128]{3,2,1,0:T(8,128)(2,1)S(1)}, u32[]{:S(2)}, u32[]{:S(2)}) collective-permute-start(bf16[2,4,128,128]{3,2,1,0:T(8,128)(2,1)S(1)} %get-tuple-element.53), channel_id=1, source_target_pairs={{0,1},{1,2},{2,3},{3,0},{4,5},{5,6},{6,7},{7,4},{8,9},{9,10},{10,1... | collective-permute-start | bytes 786440 | tf_op jit(solution)/shard_map/ppermute | solution.py:22
  52.2 11.0 %collective-permute-start.11 = (bf16[2,4,128,128]{3,2,1,0:T(8,128)(2,1)S(1)}, bf16[2,4,128,128]{3,2,1,0:T(8,128)(2,1)S(1)}, u32[]{:S(2)}, u32[]{:S(2)}) collective-permute-start(bf16[2,4,128,128]{3,2,1,0:T(8,128)(2,1)S(1)} %get-tuple-element.54), channel_id=1, source_target_pairs={{0,2},{1,3},{2,0},{3,1},{4,6},{5,7},{6,4},{7,5},{8,10},{9,11},{10,... | collective-permute-start | bytes 786440 | tf_op jit(solution)/shard_map/ppermute | solution.py:22
  54.8 9.5 %collective-permute-start.12 = (bf16[2,4,128,128]{3,2,1,0:T(8,128)(2,1)S(1)}, bf16[2,4,128,128]{3,2,1,0:T(8,128)(2,1)S(1)}, u32[]{:S(2)}, u32[]{:S(2)}) collective-permute-start(bf16[2,4,128,128]{3,2,1,0:T(8,128)(2,1)S(1)} %get-tuple-element.55), channel_id=1, source_target_pairs={{0,3},{1,0},{2,1},{3,2},{4,7},{5,4},{6,5},{7,6},{8,11},{9,8},{10,9... | collective-permute-start | bytes 786440 | tf_op jit(solution)/shard_map/ppermute | solution.py:22
  55.9 11.8 %collective-permute-start.7 = (bf16[2,128,512]{2,1,0:T(8,128)(2,1)S(1)}, bf16[2,128,512]{2,1,0:T(8,128)(2,1)S(1)}, u32[]{:S(2)}, u32[]{:S(2)}) collective-permute-start(bf16[2,128,512]{2,1,0:T(8,128)(2,1)S(1)} %get-tuple-element.49), channel_id=1, source_target_pairs={{0,64},{64,128},{128,192},{192,0},{1,65},{65,129},{129,193},{193,1... | collective-permute-start | bytes 786440 | tf_op jit(solution)/shard_map/ppermute | solution.py:22
  59.0 9.4 %collective-permute-start.8 = (bf16[2,128,512]{2,1,0:T(8,128)(2,1)S(1)}, bf16[2,128,512]{2,1,0:T(8,128)(2,1)S(1)}, u32[]{:S(2)}, u32[]{:S(2)}) collective-permute-start(bf16[2,128,512]{2,1,0:T(8,128)(2,1)S(1)} %get-tuple-element.50), channel_id=1, source_target_pairs={{0,128},{64,192},{128,0},{192,64},{1,129},{65,193},{129,1},{193,65... | collective-permute-start | bytes 786440 | tf_op jit(solution)/shard_map/ppermute | solution.py:22
  61.5 8.8 %collective-permute-start.9 = (bf16[2,128,512]{2,1,0:T(8,128)(2,1)S(1)}, bf16[2,128,512]{2,1,0:T(8,128)(2,1)S(1)}, u32[]{:S(2)}, u32[]{:S(2)}) collective-permute-start(bf16[2,128,512]{2,1,0:T(8,128)(2,1)S(1)} %get-tuple-element.51), channel_id=1, source_target_pairs={{0,192},{64,0},{128,64},{192,128},{1,193},{65,1},{129,65},{193,129... | collective-permute-start | bytes 786440 | tf_op jit(solution)/shard_map/ppermute | solution.py:22
  63.2 15.4 %collective-permute-start.1 = (bf16[2,128,512]{2,1,0:T(8,128)(2,1)S(1)}, bf16[2,128,512]{2,1,0:T(8,128)(2,1)S(1)}, u32[]{:S(2)}, u32[]{:S(2)}) collective-permute-start(bf16[2,128,512]{2,1,0:T(8,128)(2,1)S(1)} %get-tuple-element.41), channel_id=1, source_target_pairs={{0,64},{64,128},{128,192},{192,0},{1,65},{65,129},{129,193},{193,1... | collective-permute-start | bytes 786440 | tf_op jit(solution)/shard_map/ppermute | solution.py:22
  64.3 15.9 %collective-permute-start.2 = (bf16[2,128,512]{2,1,0:T(8,128)(2,1)S(1)}, bf16[2,128,512]{2,1,0:T(8,128)(2,1)S(1)}, u32[]{:S(2)}, u32[]{:S(2)}) collective-permute-start(bf16[2,128,512]{2,1,0:T(8,128)(2,1)S(1)} %get-tuple-element.42), channel_id=1, source_target_pairs={{0,128},{64,192},{128,0},{192,64},{1,129},{65,193},{129,1},{193,65... | collective-permute-start | bytes 786440 | tf_op jit(solution)/shard_map/ppermute | solution.py:22
  67.7 12.8 %collective-permute-start.3 = (bf16[2,128,512]{2,1,0:T(8,128)(2,1)S(1)}, bf16[2,128,512]{2,1,0:T(8,128)(2,1)S(1)}, u32[]{:S(2)}, u32[]{:S(2)}) collective-permute-start(bf16[2,128,512]{2,1,0:T(8,128)(2,1)S(1)} %get-tuple-element.43), channel_id=1, source_target_pairs={{0,192},{64,0},{128,64},{192,128},{1,193},{65,1},{129,65},{193,129... | collective-permute-start | bytes 786440 | tf_op jit(solution)/shard_map/ppermute | solution.py:22
  68.4 12.2 %collective-permute-start.4 = (bf16[2,4,128,128]{3,2,1,0:T(8,128)(2,1)S(1)}, bf16[2,4,128,128]{3,2,1,0:T(8,128)(2,1)S(1)}, u32[]{:S(2)}, u32[]{:S(2)}) collective-permute-start(bf16[2,4,128,128]{3,2,1,0:T(8,128)(2,1)S(1)} %get-tuple-element.45), channel_id=1, source_target_pairs={{0,1},{1,2},{2,3},{3,0},{4,5},{5,6},{6,7},{7,4},{8,9},{9,10},{10,1... | collective-permute-start | bytes 786440 | tf_op jit(solution)/shard_map/ppermute | solution.py:22
  70.4 10.2 %collective-permute-start.5 = (bf16[2,4,128,128]{3,2,1,0:T(8,128)(2,1)S(1)}, bf16[2,4,128,128]{3,2,1,0:T(8,128)(2,1)S(1)}, u32[]{:S(2)}, u32[]{:S(2)}) collective-permute-start(bf16[2,4,128,128]{3,2,1,0:T(8,128)(2,1)S(1)} %get-tuple-element.46), channel_id=1, source_target_pairs={{0,2},{1,3},{2,0},{3,1},{4,6},{5,7},{6,4},{7,5},{8,10},{9,11},{10,... | collective-permute-start | bytes 786440 | tf_op jit(solution)/shard_map/ppermute | solution.py:22
  78.6 6.5 %collective-permute-start.6 = (bf16[2,4,128,128]{3,2,1,0:T(8,128)(2,1)S(1)}, bf16[2,4,128,128]{3,2,1,0:T(8,128)(2,1)S(1)}, u32[]{:S(2)}, u32[]{:S(2)}) collective-permute-start(bf16[2,4,128,128]{3,2,1,0:T(8,128)(2,1)S(1)} %get-tuple-element.47), channel_id=1, source_target_pairs={{0,3},{1,0},{2,1},{3,2},{4,7},{5,4},{6,5},{7,6},{8,11},{9,8},{10,9... | collective-permute-start | bytes 786440 | tf_op jit(solution)/shard_map/ppermute | solution.py:22
  85.9 6.5 %collective-permute-start.13 = (bf16[4,128,128]{2,1,0:T(8,128)(2,1)S(1)}, bf16[4,128,128]{2,1,0:T(8,128)(2,1)S(1)}, u32[]{:S(2)}, u32[]{:S(2)}) collective-permute-start(bf16[4,128,128]{2,1,0:T(8,128)(2,1)S(1)} %get-tuple-element.65), channel_id=1, source_target_pairs={{0,1},{1,2},{2,3},{3,0},{4,5},{5,6},{6,7},{7,4},{8,9},{9,10},{10,1... | collective-permute-start | bytes 393224 | tf_op jit(solution)/shard_map/ppermute | solution.py:22
  86.0 7.1 %collective-permute-start.14 = (bf16[4,128,128]{2,1,0:T(8,128)(2,1)S(1)}, bf16[4,128,128]{2,1,0:T(8,128)(2,1)S(1)}, u32[]{:S(2)}, u32[]{:S(2)}) collective-permute-start(bf16[4,128,128]{2,1,0:T(8,128)(2,1)S(1)} %get-tuple-element.66), channel_id=1, source_target_pairs={{0,2},{1,3},{2,0},{3,1},{4,6},{5,7},{6,4},{7,5},{8,10},{9,11},{10,... | collective-permute-start | bytes 393224 | tf_op jit(solution)/shard_map/ppermute | solution.py:22
  87.1 6.0 %collective-permute-start.15 = (bf16[4,128,128]{2,1,0:T(8,128)(2,1)S(1)}, bf16[4,128,128]{2,1,0:T(8,128)(2,1)S(1)}, u32[]{:S(2)}, u32[]{:S(2)}) collective-permute-start(bf16[4,128,128]{2,1,0:T(8,128)(2,1)S(1)} %get-tuple-element.67), channel_id=1, source_target_pairs={{0,3},{1,0},{2,1},{3,2},{4,7},{5,4},{6,5},{7,6},{8,11},{9,8},{10,9... | collective-permute-start | bytes 393224 | tf_op jit(solution)/shard_map/ppermute | solution.py:22
  88.7 6.4 %collective-permute-start.16 = (bf16[4,128,128]{2,1,0:T(8,128)(2,1)S(1)}, bf16[4,128,128]{2,1,0:T(8,128)(2,1)S(1)}, u32[]{:S(2)}, u32[]{:S(2)}) collective-permute-start(bf16[4,128,128]{2,1,0:T(8,128)(2,1)S(1)} %get-tuple-element.69), channel_id=1, source_target_pairs={{0,64},{64,128},{128,192},{192,0},{1,65},{65,129},{129,193},{193,1... | collective-permute-start | bytes 393224 | tf_op jit(solution)/shard_map/ppermute | solution.py:22
  89.6 5.5 %collective-permute-start.17 = (bf16[4,128,128]{2,1,0:T(8,128)(2,1)S(1)}, bf16[4,128,128]{2,1,0:T(8,128)(2,1)S(1)}, u32[]{:S(2)}, u32[]{:S(2)}) collective-permute-start(bf16[4,128,128]{2,1,0:T(8,128)(2,1)S(1)} %get-tuple-element.70), channel_id=1, source_target_pairs={{0,128},{64,192},{128,0},{192,64},{1,129},{65,193},{129,1},{193,65... | collective-permute-start | bytes 393224 | tf_op jit(solution)/shard_map/ppermute | solution.py:22
  92.4 4.1 %collective-permute-start.18 = (bf16[4,128,128]{2,1,0:T(8,128)(2,1)S(1)}, bf16[4,128,128]{2,1,0:T(8,128)(2,1)S(1)}, u32[]{:S(2)}, u32[]{:S(2)}) collective-permute-start(bf16[4,128,128]{2,1,0:T(8,128)(2,1)S(1)} %get-tuple-element.71), channel_id=1, source_target_pairs={{0,192},{64,0},{128,64},{192,128},{1,193},{65,1},{129,65},{193,129... | collective-permute-start | bytes 393224 | tf_op jit(solution)/shard_map/ppermute | solution.py:22
  135.1 0.6 copy-start.6

commit v3 on v2

v3 whole, which is shorter than its diff:
```python
import jax
import jax.numpy as jnp
from jax import lax
from jax.experimental import pallas as pl
from jax.experimental.pallas import tpu as pltpu
from jax.sharding import Mesh
from jax.sharding import PartitionSpec as P


F32, BF16 = jnp.float32, jnp.bfloat16
NX, NZ, NC, NY = 4, 8, 2, 4
R, LEAF, S_DEV, NE, A = 40, 8, 2048, 512, 64
Q = NE // NY
LEAF_STEPS = 2
CHUNKS = 2
NEAR, FAR = (1, 3, 2), (2, 1, 3)


def other_core(v):
    return lax.ppermute(v, "c", [(0, 1), (1, 0)])


def shift(v, x_core, k):
    pairs = []
    for x in range(NX):
        for c in range(NC):
            for y in range(NY):
                to = ((x + k) % NX, y) if c == x_core else (x, (y + k) % NY)
                pairs.append(((x * NC + c) * NY + y, (to[0] * NC + c) * NY + to[1]))
    return lax.ppermute(v, ("x", "c", "y"), pairs)


def in_hbm(v):
    return pltpu.with_memory_space_constraint(v, pltpu.HBM)


def params(*sem, mb=16):
    return pltpu.CompilerParams(dimension_semantics=sem, vmem_limit_bytes=mb * 2**20)


def source_kernel(count, box, basis, x_re, x_im, m, keep, send, op, stacked):
    step = pl.program_id(0)
    half = LEAF * R

    @pl.when(step == 0)
    def _():
        boxes = box[...]
        for part in range(2):
            wide = basis[part].astype(F32)
            for pair in range(LEAF // 2):
                rows = []
                for b in (2 * pair, 2 * pair + 1):
                    scale = lax.rsqrt(jnp.full((1, S_DEV), count[b].astype(F32), F32))
                    rows.append(wide * jnp.where(boxes == b, scale, 0.0))
                at = part * half + pair * 2 * R
                op[at : at + 2 * R, :] = jnp.concatenate(rows, axis=0).astype(BF16)

    width = NE // LEAF_STEPS
    for k in range(LEAF_STEPS):

        @pl.when(step == k)
        def _(k=k):
            first = jnp.dot(op[...], x_re[...], preferred_element_type=F32)
            second = jnp.dot(op[...], x_im[...], preferred_element_type=F32)
            re = first[:half] - second[half:]
            im = second[:half] + first[half:]
            left, right = pl.ds(k * width, width), pl.ds(NE + k * width, width)
            stacked[:half, left] = re.astype(BF16)
            stacked[half:, left] = (-im).astype(BF16)
            stacked[:half, right] = im.astype(BF16)
            stacked[half:, right] = re.astype(BF16)

    @pl.when(step >= LEAF_STEPS)
    def _():
        rows = m[...].reshape(2 * half, NZ * NC * R).T
        out = jnp.dot(rows, stacked[...], preferred_element_type=F32)

        def write(own):
            for z in range(NZ):
                for c in range(NC):
                    g = (z * NC + c) * R
                    tile = [out[g : g + R, :NE], out[g : g + R, NE:]]
                    (keep if c == own else send)[0, z] = jnp.concatenate(tile, axis=0).astype(BF16)

        for own in range(NC):
            pl.when(lax.axis_index("c") == own)(lambda own=own: write(own))


def source(count, box, basis, currents, m):
    out = jax.ShapeDtypeStruct((NX, NZ, 2 * R, NE), BF16)
    width = NE // LEAF_STEPS

    def leaf_at(i):
        return jnp.minimum(i, LEAF_STEPS - 1)

    def merge_at(i):
        return jnp.maximum(i - LEAF_STEPS, 0)

    return pl.pallas_call(
        source_kernel,
        grid_spec=pltpu.PrefetchScalarGridSpec(
            num_scalar_prefetch=1,
            grid=(LEAF_STEPS + NX,),
            in_specs=[
                pl.BlockSpec((1, S_DEV), lambda i, *n: (0, 0)),
                pl.BlockSpec((2, R, S_DEV), lambda i, *n: (0, 0, 0)),
                pl.BlockSpec((S_DEV, width), lambda i, *n: (0, leaf_at(i))),
                pl.BlockSpec((S_DEV, width), lambda i, *n: (0, leaf_at(i) + LEAF_STEPS)),
                pl.BlockSpec((2, LEAF * R, NZ * NC * R), lambda i, *n: (0, 0, merge_at(i))),
            ],
            out_specs=[pl.BlockSpec((1, NZ, 2 * R, NE), lambda i, *n: (merge_at(i), 0, 0, 0))] * 2,
            scratch_shapes=[
                pltpu.VMEM((2 * LEAF * R, S_DEV), BF16),
                pltpu.VMEM((2 * LEAF * R, 2 * NE), BF16),
            ],
        ),
        out_shape=[out, out],
        compiler_params=params("arbitrary", mb=28),
        name="source",
    )(count, box, in_hbm(basis), in_hbm(currents), in_hbm(currents), in_hbm(m))


def turn_kernel(f, out):
    wide = f[:, 0].astype(F32)
    out[...] = jnp.concatenate([wide[:, 0], wide[:, 1]], axis=0).astype(BF16).T


def turn(factor):
    steps, columns = 2, factor.shape[3]
    width = columns // steps
    return pl.pallas_call(
        turn_kernel,
        grid=(steps,),
        in_specs=[pl.BlockSpec((A, 1, 2, width), lambda i: (0, lax.axis_index("y"), 0, i))],
        out_specs=pl.BlockSpec((width, 2 * A), lambda i: (i, 0)),
        out_shape=jax.ShapeDtypeStruct((columns, 2 * A), BF16),
        compiler_params=params("arbitrary"),
        name="turn",
    )(in_hbm(factor))


def pattern_kernel(keep, recv, fac, *refs):
    pieces, row = refs[:NX], refs[NX]
    core, x_own, y_own = (lax.axis_index(a) for a in ("c", "x", "y"))
    first = core == 0

    def product(x):
        both = fac[x, 0].astype(F32)
        turned = jnp.concatenate([-both[:, A:], both[:, :A]], axis=1)
        left = jnp.concatenate([both[:R], turned[:R], both[R:], turned[R:]], axis=0).astype(BF16)
        own, other = keep[x, 0], recv[x, 0]
        right = jnp.concatenate(
            [jnp.where(first, own, other), jnp.where(first, other, own)], axis=0
        )
        return jnp.dot(left.T, right, preferred_element_type=F32).astype(BF16)

    @pl.when(first)
    def _():
        for k in range(NX):
            piece = product(lax.rem(x_own + k, NX))
            for y in range(NY):
                pieces[k][0, y] = piece[:, y * Q : (y + 1) * Q]

    @pl.when(core == 1)
    def _():
        for x in range(NX):
            row[x] = product(x)
        for k in range(NY):
            at = pl.multiple_of(lax.rem(y_own + k, NY) * Q, Q)
            pieces[k][0] = row[:, :, pl.ds(at, Q)]


def pattern(keep, recv, fac, chunk):
    steps = NZ // CHUNKS

    def at(i):
        return (0, chunk * steps + i, 0, 0)

    return pl.pallas_call(
        pattern_kernel,
        grid=(steps,),
        in_specs=[
            pl.BlockSpec((NX, 1, 2 * R, NE), at),
            pl.BlockSpec((NX, 1, 2 * R, NE), at),
            pl.BlockSpec((NX, 1, 2 * R, 2 * A), at),
        ],
        out_specs=[pl.BlockSpec((1, NX, 2 * A, Q), lambda i: (i, 0, 0, 0))] * NX,
        out_shape=[jax.ShapeDtypeStruct((steps, NX, 2 * A, Q), BF16)] * NX,
        scratch_shapes=[pltpu.VMEM((NX, 2 * A, NE), BF16)],
        compiler_params=params("arbitrary"),
        name="pattern",
    )(keep, recv, fac)


def second_kernel(*refs):
    parts, pieces = refs[:NX], refs[-NX:]
    own = jnp.where(lax.axis_index("c") == 0, lax.axis_index("y"), lax.axis_index("x"))
    for k in range(NX):
        at = lax.rem(own + k, NX)
        for z in range(NZ // CHUNKS):
            pieces[k][z] = sum(r[z, at].astype(F32) for r in parts).astype(BF16)


def second(parts, chunk, earlier):
    rows = NZ // CHUNKS
    return pl.pallas_call(
        second_kernel,
        grid=(1,),
        in_specs=[pl.BlockSpec((rows, NX, 2 * A, Q), lambda i: (0, 0, 0, 0))] * NX
        + [pl.BlockSpec(memory_space=pl.ANY)] * len(earlier),
        out_specs=[pl.BlockSpec((rows, 2 * A, Q), lambda i: (chunk, 0, 0))] * NX,
        out_shape=[jax.ShapeDtypeStruct((NZ, 2 * A, Q), BF16)] * NX,
        input_output_aliases={NX + i: i for i in range(len(earlier))},
        compiler_params=params("arbitrary"),
        name="second",
    )(*parts, *earlier)


def third_kernel(*refs):
    refs[-1][...] = sum(r[...].astype(F32) for r in refs[:-1]).astype(BF16)


def third(parts):
    return pl.pallas_call(
        third_kernel,
        out_shape=jax.ShapeDtypeStruct((NZ, 2 * A, Q), BF16),
        compiler_params=params(mb=4),
        name="third",
    )(*parts)


def last_kernel(parts, intensity, top):
    total = jnp.sum(parts[...].astype(F32), axis=0)
    value = total[:A] * total[:A] + total[A:] * total[A:]
    intensity[...] = value
    top[...] = jnp.broadcast_to(jnp.max(value, axis=0, keepdims=True)[None], top.shape)


def last(parts):
    return pl.pallas_call(
        last_kernel,
        out_shape=[
            jax.ShapeDtypeStruct((A, Q), F32),
            jax.ShapeDtypeStruct((NX * NZ * NC, 1, Q), F32),
        ],
        compiler_params=params(mb=4),
        name="last",
    )(parts)


def exchange(pieces, x_core, order):
    parts = [pieces[0]] + [None] * (NX - 1)
    for k in order:
        parts[k] = shift(pieces[k], x_core, k)
    return parts


def body(currents, leaf_basis, leaf_box, box_count, merge_factor, angle_factor):
    own = turn(angle_factor)
    own = own.reshape(NX * NZ, NC * R, 2 * A)
    spread = lax.all_to_all(own, ("x", "z"), 0, 0, tiled=True)
    box = leaf_box.reshape(1, S_DEV)
    coefs = merge_factor.swapaxes(1, 2)
    keep, send = source(box_count, box, leaf_basis, currents, coefs)
    fac = spread.reshape(NX, NZ, NC * R, 2 * A)
    recv = other_core(send)
    sent = []
    for chunk in range(CHUNKS):
        pieces = pattern(keep, recv, fac, chunk)
        sent.append(exchange(pieces, 0, NEAR))
    pieces = []
    for chunk in range(CHUNKS):
        pieces = second(sent[chunk], chunk, pieces)
    parts = third(exchange(pieces, 1, FAR))
    parts = lax.all_to_all(parts, "z", 0, 0, tiled=True)
    intensity, tops = last(parts)
    tops = lax.all_to_all(tops, ("x", "z", "c"), 0, 0, tiled=True)
    peak = jnp.max(tops, axis=(0, 1))
    return intensity / (peak[None, :] + 1.0), peak


def solution(mesh):
    split = Mesh(mesh.devices.reshape(NX, NZ, NC, NY), ("x", "z", "c", "y"))
    src, every = ("x", "z", "c"), ("x", "z", "c", "y")
    in_specs = (
        P(every, None),
        P(None, None, every),
        P(every),
        P(every),
        P(None, None, every),
        P(src, None, None, None),
    )
    out_specs = (P(src, "y"), P("y"))
    return jax.shard_map(body, mesh=split, in_specs=in_specs, out_specs=out_specs, check_vma=False)
```

time: 136 us -> 120 us (0.88)
  starting transfers between devices: 26.4 us -> 15.1 us
  local copies, waits for them, and re-layouts: 6.45 us -> 1.35 us
  blocking collectives: 64.5 us -> 59.5 us
  waiting for transfers between devices: 18.5 us -> 23.3 us
    ppermute x19 -> x10, starting transfers between devices: 26.4 us -> 15.1 us  [the longest x9 11.8 us: shift(): return lax.ppermute(v, ('x', 'c', 'y'), pairs)]
    all_to_all x1, blocking collectives: 19.9 us -> 14.5 us  [body(): parts = lax.all_to_all(parts, 'z', 0, 0, tiled=True)]
    unnamed x14 -> x6, local copies, waits for them, and re-layouts: 6.45 us -> 1.35 us
    ppermute x19 -> x10, waiting for transfers between devices: 18.5 us -> 23.3 us  [the longest x9 23.3 us: shift(): return lax.ppermute(v, ('x', 'c', 'y'), pairs)]
    pallas_call x1, Pallas kernels: 10 us -> 11.5 us  [source(): pl.pallas_call(source_kernel, grid_spec=pltpu.PrefetchScalarGridSpec(num_...]
  transfers between devices with their start and end apart: 19 -> 10, of which waited for: 8 -> 7; matrix products, arithmetic and copies ran while one was open for 0% -> 0% of each run, Pallas kernels for 4% -> 4%
where the time goes in v3:
time: 120 us
  blocking collectives  59.5 us (50%)
  waiting for transfers between devices  23.3 us (19%)
  Pallas kernels  19 us (16%)
  starting transfers between devices  15.1 us (13%)
  local copies, waits for them, and re-layouts  1.35 us (1%)
    all_to_all x1, blocking collectives, body(): spread = lax.all_to_all(own, ('x', 'z'), 0, 0, tiled=True)  26.2 us
    ppermute x9, waiting for transfers between devices, shift(): return lax.ppermute(v, ('x', 'c', 'y'), pairs)  23.3 us
    all_to_all x1, blocking collectives, body(): tops = lax.all_to_all(tops, ('x', 'z', 'c'), 0, 0, tiled=True)  18.9 us
    all_to_all x1, blocking collectives, body(): parts = lax.all_to_all(parts, 'z', 0, 0, tiled=True)  14.5 us
    ppermute x9, starting transfers between devices, shift(): return lax.ppermute(v, ('x', 'c', 'y'), pairs)  11.8 us
    pallas_call x1, Pallas kernels, source(): pl.pallas_call(source_kernel, grid_spec=pltpu.PrefetchScalarGridSpec(num_...  11.5 us
    pallas_call x2, Pallas kernels, pattern(): pl.pallas_call(pattern_kernel, grid=(steps,), in_specs=[pl.BlockSpec((NX,...  5.22 us
    ppermute x1, starting transfers between devices, other_core(): return lax.ppermute(v, 'c', [(0, 1), (1, 0)])  3.3 us
  transfers between devices with their start and end apart: 10, of which 7 were waited for; matrix products, arithmetic and copies ran while one was open for 0% of the time, Pallas kernels for 4%

profile of v3, /device:TPU:1, one launch (start us, length us, event | category | flops | bytes accessed | tf_op | source)
XLA Modules:
  0.0 119.7 jit_solution(15944241463228472986)
XLA Ops:
  0.6 0.0 copy-start
  0.6 0.7 copy-done
  1.3 0.0 copy-start.1
  1.3 0.7 copy-done.1
  2.0 11.5 %source.1 = (bf16[4,8,80,512]{3,2,1,0:T(8,128)(2,1)S(1)}, bf16[4,8,80,512]{3,2,1,0:T(8,128)(2,1)S(1)}) custom-call(s32[8]{0:T(128)S(1)} %copy-done.1, s32[1,2048]{1,0:T(1,128)S(1)} %bitcast.7, bf16[2,40,2048]{2,1,0:T(8,128)(2,1)} %basis.1, bf16[2048,1024]{1,0:T(8,128)(2,1)} %x_im.1, bf16[2048,1024]{1,0:T(8,128)(2,1)} %x_im.1, bf16[2,320,2560]{2,1,0:T(8,128)(2,1)} %bitcast.8), custom_call_target="tpu_custom_call" | custom-call | tf_op jit(solution)/shard_map/source/pallas_call | solution.py:99
  13.5 3.3 %collective-permute-start = (bf16[4,8,80,512]{3,2,1,0:T(8,128)(2,1)S(1)}, bf16[4,8,80,512]{3,2,1,0:T(8,128)(2,1)S(1)}, u32[]{:S(2)}, u32[]{:S(2)}) collective-permute-start(bf16[4,8,80,512]{3,2,1,0:T(8,128)(2,1)S(1)} %get-tuple-element.23), channel_id=1, source_target_pairs={{0,4},{4,0},{1,5},{5,1},{2,6},{6,2},{3,7},{7,3},{8,12},{12,8},{9,1... | collective-permute-start | bytes 7864328 | tf_op jit(solution)/shard_map/ppermute | solution.py:20
  16.7 1.6 %turn.1 = bf16[2560,128]{1,0:T(8,128)(2,1)S(1)} custom-call(bf16[64,4,2,2560]{3,2,1,0:T(2,128)(2,1)} %f.1), custom_call_target="tpu_custom_call" | custom-call | tf_op jit(solution)/shard_map/turn/pallas_call | solution.py:131
  18.4 26.2 %all_to_all.15 = bf16[32,80,128]{2,1,0:T(8,128)(2,1)S(1)} all-to-all(bf16[32,80,128]{2,1,0:T(8,128)(2,1)S(1)} %bitcast.6), channel_id=1, replica_groups=mesh['x'=4,'z'=8,'c'=2,'y'=4] {'x','z'}, dimensions={0} | all-to-all | bytes 1310720 | tf_op jit(solution)/shard_map/all_to_all | solution.py:261
  44.6 0.0 collective-permute-done.recv
  44.6 2.6 %pattern.3 = (bf16[4,4,128,128]{3,2,1,0:T(8,128)(2,1)S(1)}, bf16[4,4,128,128]{3,2,1,0:T(8,128)(2,1)S(1)}, bf16[4,4,128,128]{3,2,1,0:T(8,128)(2,1)S(1)}, bf16[4,4,128,128]{3,2,1,0:T(8,128)(2,1)S(1)}) custom-call(bf16[4,8,80,512]{3,2,1,0:T(8,128)(2,1)S(1)} %get-tuple-element.22.keep, bf16[4,8,80,512]{3,2,1,0:T(8,128)(2,1)S(1)} %collective-permute-done.recv, ...), custom_call_target="tpu_custom_call" | custom-call | tf_op jit(solution)/shard_map/pattern/pallas_call | solution.py:179
  47.2 1.4 %collective-permute-start.4 = (bf16[4,4,128,128]{3,2,1,0:T(8,128)(2,1)S(1)}, bf16[4,4,128,128]{3,2,1,0:T(8,128)(2,1)S(1)}, u32[]{:S(2)}, u32[]{:S(2)}) collective-permute-start(bf16[4,4,128,128]{3,2,1,0:T(8,128)(2,1)S(1)} %get-tuple-element.29), channel_id=1, source_target_pairs={{0,64},{1,65},{2,66},{3,67},{4,5},{5,6},{6,7},{7,4},{64,128},{65,1... | collective-permute-start | bytes 1572872 | tf_op jit(solution)/shard_map/ppermute | solution.py:30
  48.6 2.6 %collective-permute-start.5 = (bf16[4,4,128,128]{3,2,1,0:T(8,128)(2,1)S(1)}, bf16[4,4,128,128]{3,2,1,0:T(8,128)(2,1)S(1)}, u32[]{:S(2)}, u32[]{:S(2)}) collective-permute-start(bf16[4,4,128,128]{3,2,1,0:T(8,128)(2,1)S(1)} %get-tuple-element.30), channel_id=1, source_target_pairs={{0,128},{1,129},{2,130},{3,131},{4,6},{5,7},{6,4},{7,5},{64,192},{... | collective-permute-start | bytes 1572872 | tf_op jit(solution)/shard_map/ppermute | solution.py:30
  51.2 1.1 collective-permute-start.6
  52.3 2.6 %pattern.2 = (bf16[4,4,128,128]{3,2,1,0:T(8,128)(2,1)S(1)}, bf16[4,4,128,128]{3,2,1,0:T(8,128)(2,1)S(1)}, bf16[4,4,128,128]{3,2,1,0:T(8,128)(2,1)S(1)}, bf16[4,4,128,128]{3,2,1,0:T(8,128)(2,1)S(1)}) custom-call(bf16[4,8,80,512]{3,2,1,0:T(8,128)(2,1)S(1)} %get-tuple-element.22.keep, bf16[4,8,80,512]{3,2,1,0:T(8,128)(2,1)S(1)} %collective-permute-done.recv, ...), custom_call_target="tpu_custom_call" | custom-call | tf_op jit(solution)/shard_map/pattern/pallas_call | solution.py:179
  54.9 0.5 collective-permute-start.1
  55.4 0.8 collective-permute-start.2
  56.2 0.7 collective-permute-done.4.refs_1_
  56.9 1.5 %collective-permute-start.3 = (bf16[4,4,128,128]{3,2,1,0:T(8,128)(2,1)S(1)}, bf16[4,4,128,128]{3,2,1,0:T(8,128)(2,1)S(1)}, u32[]{:S(2)}, u32[]{:S(2)}) collective-permute-start(bf16[4,4,128,128]{3,2,1,0:T(8,128)(2,1)S(1)} %get-tuple-element.27), channel_id=1, source_target_pairs={{0,192},{1,193},{2,194},{3,195},{4,7},{5,4},{6,5},{7,6},{64,0},{65... | collective-permute-start | bytes 1572872 | tf_op jit(solution)/shard_map/ppermute | solution.py:30
  58.3 5.4 %collective-permute-done.5.refs_2_ = bf16[4,4,128,128]{3,2,1,0:T(8,128)(2,1)S(1)} collective-permute-done((bf16[4,4,128,128]{3,2,1,0:T(8,128)(2,1)S(1)}, bf16[4,4,128,128]{3,2,1,0:T(8,128)(2,1)S(1)}, u32[]{:S(2)}, u32[]{:S(2)}) %collective-permute-start.5) | collective-permute-done | bytes 524320 | tf_op jit(solution)/shard_map/ppermute | solution.py:30
  63.7 0.0 collective-permute-done.6.refs_3_
  63.7 0.3 second.2
  64.0 5.3 %collective-permute-done.1.refs_1_ = bf16[4,4,128,128]{3,2,1,0:T(8,128)(2,1)S(1)} collective-permute-done((bf16[4,4,128,128]{3,2,1,0:T(8,128)(2,1)S(1)}, bf16[4,4,128,128]{3,2,1,0:T(8,128)(2,1)S(1)}, u32[]{:S(2)}, u32[]{:S(2)}) %collective-permute-start.1) | collective-permute-done | bytes 524320 | tf_op jit(solution)/shard_map/ppermute | solution.py:30
  69.3 5.7 %collective-permute-done.2.refs_2_ = bf16[4,4,128,128]{3,2,1,0:T(8,128)(2,1)S(1)} collective-permute-done((bf16[4,4,128,128]{3,2,1,0:T(8,128)(2,1)S(1)}, bf16[4,4,128,128]{3,2,1,0:T(8,128)(2,1)S(1)}, u32[]{:S(2)}, u32[]{:S(2)}) %collective-permute-start.2) | collective-permute-done | bytes 524320 | tf_op jit(solution)/shard_map/ppermute | solution.py:30
  75.0 0.0 collective-permute-done.3.refs_3_
  75.0 0.3 second.3
  75.2 0.4 collective-permute-start.7
  75.7 2.4 %collective-permute-start.8 = (bf16[8,128,128]{2,1,0:T(8,128)(2,1)S(1)}, bf16[8,128,128]{2,1,0:T(8,128)(2,1)S(1)}, u32[]{:S(2)}, u32[]{:S(2)}) collective-permute-start(bf16[8,128,128]{2,1,0:T(8,128)(2,1)S(1)} %get-tuple-element.38), channel_id=1, source_target_pairs={{0,2},{1,3},{2,0},{3,1},{4,132},{5,133},{6,134},{7,135},{64,66},{6... | collective-permute-start | bytes 786440 | tf_op jit(solution)/shard_map/ppermute | solution.py:30
  78.1 1.2 collective-permute-start.9
  79.2 2.5 %collective-permute-done.7.refs_1_ = bf16[8,128,128]{2,1,0:T(8,128)(2,1)S(1)} collective-permute-done((bf16[8,128,128]{2,1,0:T(8,128)(2,1)S(1)}, bf16[8,128,128]{2,1,0:T(8,128)(2,1)S(1)}, u32[]{:S(2)}, u32[]{:S(2)}) %collective-permute-start.7) | collective-permute-done | bytes 262176 | tf_op jit(solution)/shard_map/ppermute | solution.py:30
  81.7 2.9 %collective-permute-done.8.refs_2_ = bf16[8,128,128]{2,1,0:T(8,128)(2,1)S(1)} collective-permute-done((bf16[8,128,128]{2,1,0:T(8,128)(2,1)S(1)}, bf16[8,128,128]{2,1,0:T(8,128)(2,1)S(1)}, u32[]{:S(2)}, u32[]{:S(2)}) %collective-permute-start.8) | collective-permute-done | bytes 262176 | tf_op jit(solution)/shard_map/ppermute | solution.py:30
  84.6 0.8 collective-permute-done.9.refs_3_
  85.5 0.1 third.1
  85.6 14.5 %all_to_all.16.parts = bf16[8,128,128]{2,1,0:T(8,128)(2,1)S(1)} all-to-all(bf16[8,128,128]{2,1,0:T(8,128)(2,1)S(1)} %third.1), channel_id=1, replica_groups=mesh['x'=4,'z'=8,'c'=2,'y'=4] {'z'}, dimensions={0} | all-to-all | bytes 524288 | tf_op jit(solution)/shard_map/all_to_all | solution.py:275
  100.1 0.1 last.1
  100.1 18.9 %all_to_all.17 = f32[64,1,128]{2,1,0:T(1,128)S(1)} all-to-all(f32[64,1,128]{2,1,0:T(1,128)S(1)} %get-tuple-element.41), channel_id=1, replica_groups=mesh['x'=4,'z'=8,'c'=2,'y'=4] {'x','z','c'}, dimensions={0} | all-to-all | bytes 65536 | tf_op jit(solution)/shard_map/all_to_all | solution.py:277
  119.0 0.1 reduce_max.9
  119.1 0.0 copy-start.2
  119.1 0.6 broadcast_divide_fusion
  119.7 0.0 copy-done.2
  (1 shorter events, 0.0 us)
Async XLA Ops:
  0.6 0.7 copy-start
  1.3 0.7 copy-start.1
  13.5 31.1 %collective-permute-start = (bf16[4,8,80,512]{3,2,1,0:T(8,128)(2,1)S(1)}, bf16[4,8,80,512]{3,2,1,0:T(8,128)(2,1)S(1)}, u32[]{:S(2)}, u32[]{:S(2)}) collective-permute-start(bf16[4,8,80,512]{3,2,1,0:T(8,128)(2,1)S(1)} %get-tuple-element.23), channel_id=1, source_target_pairs={{0,4},{4,0},{1,5},{5,1},{2,6},{6,2},{3,7},{7,3},{8,12},{12,8},{9,1... | collective-permute-start | bytes 7864328 | tf_op jit(solution)/shard_map/ppermute | solution.py:20
  47.2 9.7 %collective-permute-start.4 = (bf16[4,4,128,128]{3,2,1,0:T(8,128)(2,1)S(1)}, bf16[4,4,128,128]{3,2,1,0:T(8,128)(2,1)S(1)}, u32[]{:S(2)}, u32[]{:S(2)}) collective-permute-start(bf16[4,4,128,128]{3,2,1,0:T(8,128)(2,1)S(1)} %get-tuple-element.29), channel_id=1, source_target_pairs={{0,64},{1,65},{2,66},{3,67},{4,5},{5,6},{6,7},{7,4},{64,128},{65,1... | collective-permute-start | bytes 1572872 | tf_op jit(solution)/shard_map/ppermute | solution.py:30
  48.6 15.1 %collective-permute-start.5 = (bf16[4,4,128,128]{3,2,1,0:T(8,128)(2,1)S(1)}, bf16[4,4,128,128]{3,2,1,0:T(8,128)(2,1)S(1)}, u32[]{:S(2)}, u32[]{:S(2)}) collective-permute-start(bf16[4,4,128,128]{3,2,1,0:T(8,128)(2,1)S(1)} %get-tuple-element.30), channel_id=1, source_target_pairs={{0,128},{1,129},{2,130},{3,131},{4,6},{5,7},{6,4},{7,5},{64,192},{... | collective-permute-start | bytes 1572872 | tf_op jit(solution)/shard_map/ppermute | solution.py:30
  51.2 12.5 %collective-permute-start.6 = (bf16[4,4,128,128]{3,2,1,0:T(8,128)(2,1)S(1)}, bf16[4,4,128,128]{3,2,1,0:T(8,128)(2,1)S(1)}, u32[]{:S(2)}, u32[]{:S(2)}) collective-permute-start(bf16[4,4,128,128]{3,2,1,0:T(8,128)(2,1)S(1)} %get-tuple-element.31), channel_id=1, source_target_pairs={{0,192},{1,193},{2,194},{3,195},{4,7},{5,4},{6,5},{7,6},{64,0},{65... | collective-permute-start | bytes 1572872 | tf_op jit(solution)/shard_map/ppermute | solution.py:30
  54.9 14.4 %collective-permute-start.1 = (bf16[4,4,128,128]{3,2,1,0:T(8,128)(2,1)S(1)}, bf16[4,4,128,128]{3,2,1,0:T(8,128)(2,1)S(1)}, u32[]{:S(2)}, u32[]{:S(2)}) collective-permute-start(bf16[4,4,128,128]{3,2,1,0:T(8,128)(2,1)S(1)} %get-tuple-element.25), channel_id=1, source_target_pairs={{0,64},{1,65},{2,66},{3,67},{4,5},{5,6},{6,7},{7,4},{64,128},{65,1... | collective-permute-start | bytes 1572872 | tf_op jit(solution)/shard_map/ppermute | solution.py:30
  55.4 19.6 %collective-permute-start.2 = (bf16[4,4,128,128]{3,2,1,0:T(8,128)(2,1)S(1)}, bf16[4,4,128,128]{3,2,1,0:T(8,128)(2,1)S(1)}, u32[]{:S(2)}, u32[]{:S(2)}) collective-permute-start(bf16[4,4,128,128]{3,2,1,0:T(8,128)(2,1)S(1)} %get-tuple-element.26), channel_id=1, source_target_pairs={{0,128},{1,129},{2,130},{3,131},{4,6},{5,7},{6,4},{7,5},{64,192},{... | collective-permute-start | bytes 1572872 | tf_op jit(solution)/shard_map/ppermute | solution.py:30
  56.9 18.1 %collective-permute-start.3 = (bf16[4,4,128,128]{3,2,1,0:T(8,128)(2,1)S(1)}, bf16[4,4,128,128]{3,2,1,0:T(8,128)(2,1)S(1)}, u32[]{:S(2)}, u32[]{:S(2)}) collective-permute-start(bf16[4,4,128,128]{3,2,1,0:T(8,128)(2,1)S(1)} %get-tuple-element.27), channel_id=1, source_target_pairs={{0,192},{1,193},{2,194},{3,195},{4,7},{5,4},{6,5},{7,6},{64,0},{65... | collective-permute-start | bytes 1572872 | tf_op jit(solution)/shard_map/ppermute | solution.py:30
  75.2 6.5 %collective-permute-start.7 = (bf16[8,128,128]{2,1,0:T(8,128)(2,1)S(1)}, bf16[8,128,128]{2,1,0:T(8,128)(2,1)S(1)}, u32[]{:S(2)}, u32[]{:S(2)}) collective-permute-start(bf16[8,128,128]{2,1,0:T(8,128)(2,1)S(1)} %get-tuple-element.37), channel_id=1, source_target_pairs={{0,1},{1,2},{2,3},{3,0},{4,68},{5,69},{6,70},{7,71},{64,65},{65,66... | collective-permute-start | bytes 786440 | tf_op jit(solution)/shard_map/ppermute | solution.py:30
  75.7 9.0 %collective-permute-start.8 = (bf16[8,128,128]{2,1,0:T(8,128)(2,1)S(1)}, bf16[8,128,128]{2,1,0:T(8,128)(2,1)S(1)}, u32[]{:S(2)}, u32[]{:S(2)}) collective-permute-start(bf16[8,128,128]{2,1,0:T(8,128)(2,1)S(1)} %get-tuple-element.38), channel_id=1, source_target_pairs={{0,2},{1,3},{2,0},{3,1},{4,132},{5,133},{6,134},{7,135},{64,66},{6... | collective-permute-start | bytes 786440 | tf_op jit(solution)/shard_map/ppermute | solution.py:30
  78.1 7.4 %collective-permute-start.9 = (bf16[8,128,128]{2,1,0:T(8,128)(2,1)S(1)}, bf16[8,128,128]{2,1,0:T(8,128)(2,1)S(1)}, u32[]{:S(2)}, u32[]{:S(2)}) collective-permute-start(bf16[8,128,128]{2,1,0:T(8,128)(2,1)S(1)} %get-tuple-element.39), channel_id=1, source_target_pairs={{0,3},{1,0},{2,1},{3,2},{4,196},{5,197},{6,198},{7,199},{64,67},{6... | collective-permute-start | bytes 786440 | tf_op jit(solution)/shard_map/ppermute | solution.py:30
  119.1 0.6 copy-start.2

commit v4 on v3

--- a/solution.py
+++ b/solution.py
@@ -13,7 +13,8 @@
 Q = NE // NY
 LEAF_STEPS = 2
 CHUNKS = 2
-NEAR, FAR = (1, 3, 2), (2, 1, 3)
+FAR = (2, 1, 3)
+PLACE = {0: 0, 1: 1, 3: 2}
 
 
 def other_core(v):
@@ -140,7 +141,7 @@
 
 
 def pattern_kernel(keep, recv, fac, *refs):
-    pieces, row = refs[:NX], refs[NX]
+    pieces, halves, row = refs[:3], refs[3:5], refs[5]
     core, x_own, y_own = (lax.axis_index(a) for a in ("c", "x", "y"))
     first = core == 0
 
@@ -154,20 +155,25 @@
         )
         return jnp.dot(left.T, right, preferred_element_type=F32).astype(BF16)
 
-    @pl.when(first)
+    @pl.when(core == 1)
     def _():
         for k in range(NX):
             piece = product(lax.rem(x_own + k, NX))
             for y in range(NY):
-                pieces[k][0, y] = piece[:, y * Q : (y + 1) * Q]
-
-    @pl.when(core == 1)
+                to = halves[y // 2].at[0, y % 2] if k == 2 else pieces[PLACE[k]].at[0, y]
+                to[...] = piece[:, y * Q : (y + 1) * Q]
+
+    @pl.when(core == 0)
     def _():
         for x in range(NX):
             row[x] = product(x)
         for k in range(NY):
             at = pl.multiple_of(lax.rem(y_own + k, NY) * Q, Q)
-            pieces[k][0] = row[:, :, pl.ds(at, Q)]
+            if k == 2:
+                for half in range(2):
+                    halves[half][0] = row[2 * half : 2 * half + 2, :, pl.ds(at, Q)]
+            else:
+                pieces[PLACE[k]][0] = row[:, :, pl.ds(at, Q)]
 
 
 def pattern(keep, recv, fac, chunk):
@@ -184,17 +190,37 @@
             pl.BlockSpec((NX, 1, 2 * R, NE), at),
             pl.BlockSpec((NX, 1, 2 * R, 2 * A), at),
         ],
-        out_specs=[pl.BlockSpec((1, NX, 2 * A, Q), lambda i: (i, 0, 0, 0))] * NX,
-        out_shape=[jax.ShapeDtypeStruct((steps, NX, 2 * A, Q), BF16)] * NX,
+        out_specs=[pl.BlockSpec((1, NX, 2 * A, Q), lambda i: (i, 0, 0, 0))] * 3
+        + [pl.BlockSpec((1, NX // 2, 2 * A, Q), lambda i: (i, 0, 0, 0))] * 2,
+        out_shape=[jax.ShapeDtypeStruct((steps, NX, 2 * A, Q), BF16)] * 3
+        + [jax.ShapeDtypeStruct((steps, NX // 2, 2 * A, Q), BF16)] * 2,
         scratch_shapes=[pltpu.VMEM((NX, 2 * A, NE), BF16)],
         compiler_params=params("arbitrary"),
         name="pattern",
     )(keep, recv, fac)
 
 
+def forward_kernel(ahead, behind, from_behind, from_ahead, to_ahead, to_behind):
+    h = NX // 2
+    for z in range(NZ // CHUNKS):
+        to_ahead[z, :h] = (ahead[z, :h].astype(F32) + from_behind[z].astype(F32)).astype(BF16)
+        to_ahead[z, h:] = ahead[z, h:]
+        to_behind[z, :h] = behind[z, :h]
+        to_behind[z, h:] = (behind[z, h:].astype(F32) + from_ahead[z].astype(F32)).astype(BF16)
+
+
+def forward(*pieces):
+    return pl.pallas_call(
+        forward_kernel,
+        out_shape=[jax.ShapeDtypeStruct(pieces[0].shape, BF16)] * 2,
+        compiler_params=params(mb=10),
+        name="forward",
+    )(*pieces)
+
+
 def second_kernel(*refs):
-    parts, pieces = refs[:NX], refs[-NX:]
-    own = jnp.where(lax.axis_index("c") == 0, lax.axis_index("y"), lax.axis_index("x"))
+    parts, pieces = refs[:3], refs[-NX:]
+    own = jnp.where(lax.axis_index("c") == 1, lax.axis_index("y"), lax.axis_index("x"))
     for k in range(NX):
         at = lax.rem(own + k, NX)
         for z in range(NZ // CHUNKS):
@@ -206,11 +232,11 @@
     return pl.pallas_call(
         second_kernel,
         grid=(1,),
-        in_specs=[pl.BlockSpec((rows, NX, 2 * A, Q), lambda i: (0, 0, 0, 0))] * NX
+        in_specs=[pl.BlockSpec((rows, NX, 2 * A, Q), lambda i: (0, 0, 0, 0))] * 3
         + [pl.BlockSpec(memory_space=pl.ANY)] * len(earlier),
         out_specs=[pl.BlockSpec((rows, 2 * A, Q), lambda i: (chunk, 0, 0))] * NX,
         out_shape=[jax.ShapeDtypeStruct((NZ, 2 * A, Q), BF16)] * NX,
-        input_output_aliases={NX + i: i for i in range(len(earlier))},
+        input_output_aliases={3 + i: i for i in range(len(earlier))},
         compiler_params=params("arbitrary"),
         name="second",
     )(*parts, *earlier)
@@ -253,6 +279,12 @@
     for k in order:
         parts[k] = shift(pieces[k], x_core, k)
     return parts
+
+
+def both_ways(ahead, behind):
+    ahead = shift(ahead, 1, 1)
+    behind = shift(behind, 1, NX - 1)
+    return ahead, behind
 
 
 def body(currents, leaf_basis, leaf_box, box_count, merge_factor, angle_factor):
@@ -264,14 +296,17 @@
     keep, send = source(box_count, box, leaf_basis, currents, coefs)
     fac = spread.reshape(NX, NZ, NC * R, 2 * A)
     recv = other_core(send)
-    sent = []
+    made, sums = [], []
     for chunk in range(CHUNKS):
         pieces = pattern(keep, recv, fac, chunk)
-        sent.append(exchange(pieces, 0, NEAR))
+        made.append((pieces, both_ways(*pieces[3:])))
+    for pieces, halves in made:
+        ahead, behind = forward(*pieces[1:3], *halves)
+        sums.append([pieces[0], *both_ways(ahead, behind)])
     pieces = []
     for chunk in range(CHUNKS):
-        pieces = second(sent[chunk], chunk, pieces)
-    parts = third(exchange(pieces, 1, FAR))
+        pieces = second(sums[chunk], chunk, pieces)
+    parts = third(exchange(pieces, 0, FAR))
     parts = lax.all_to_all(parts, "z", 0, 0, tiled=True)
     intensity, tops = last(parts)
     tops = lax.all_to_all(tops, ("x", "z", "c"), 0, 0, tiled=True)

time: 120 us -> 119 us (level)
  waiting for transfers between devices: 23.3 us -> 16 us
  starting transfers between devices: 15.1 us -> 18.7 us
  blocking collectives: 59.5 us -> 62.7 us
    ppermute x9 -> x11, waiting for transfers between devices: 23.3 us -> 16 us  [shift(): return lax.ppermute(v, ('x', 'c', 'y'), pairs)]
    ppermute x9 -> x11, starting transfers between devices: 11.8 us -> 15.4 us  [shift(): return lax.ppermute(v, ('x', 'c', 'y'), pairs)]
    all_to_all x1, blocking collectives: 18.9 us -> 22.4 us  [body(): tops = lax.all_to_all(tops, ('x', 'z', 'c'), 0, 0, tiled=True)]
  transfers between devices with their start and end apart: 10 -> 12, of which waited for: 7 -> 6; matrix products, arithmetic and copies ran while one was open for 0% -> 0% of each run, Pallas kernels for 4% -> 4%
where the time goes in v4:
time: 119 us
  blocking collectives  62.7 us (53%)
  starting transfers between devices  18.7 us (16%)
  Pallas kernels  18.4 us (15%)
  waiting for transfers between devices  16 us (13%)
  local copies, waits for them, and re-layouts  1.35 us (1%)
    all_to_all x1, blocking collectives, body(): spread = lax.all_to_all(own, ('x', 'z'), 0, 0, tiled=True)  26.2 us
    all_to_all x1, blocking collectives, body(): tops = lax.all_to_all(tops, ('x', 'z', 'c'), 0, 0, tiled=True)  22.4 us
    ppermute x11, waiting for transfers between devices, shift(): return lax.ppermute(v, ('x', 'c', 'y'), pairs)  16 us
    ppermute x11, starting transfers between devices, shift(): return lax.ppermute(v, ('x', 'c', 'y'), pairs)  15.4 us
    all_to_all x1, blocking collectives, body(): parts = lax.all_to_all(parts, 'z', 0, 0, tiled=True)  14.1 us
    pallas_call x1, Pallas kernels, source(): pl.pallas_call(source_kernel, grid_spec=pltpu.PrefetchScalarGridSpec(num_...  11.5 us
    pallas_call x2, Pallas kernels, pattern(): pl.pallas_call(pattern_kernel, grid=(steps,), in_specs=[pl.BlockSpec((NX,...  4.47 us
    ppermute x1, starting transfers between devices, other_core(): return lax.ppermute(v, 'c', [(0, 1), (1, 0)])  3.28 us
  transfers between devices with their start and end apart: 12, of which 6 were waited for; matrix products, arithmetic and copies ran while one was open for 0% of the time, Pallas kernels for 4%

profile of v4, /device:TPU:1, one launch (start us, length us, event | category | flops | bytes accessed | tf_op | source)
XLA Modules:
  0.0 118.6 jit_solution(2259264792407232416)
XLA Ops:
  0.6 0.0 copy-start
  0.6 0.7 copy-done
  1.3 0.0 copy-start.1
  1.3 0.7 copy-done.1
  2.0 11.5 %source.1 = (bf16[4,8,80,512]{3,2,1,0:T(8,128)(2,1)S(1)}, bf16[4,8,80,512]{3,2,1,0:T(8,128)(2,1)S(1)}) custom-call(s32[8]{0:T(128)S(1)} %copy-done.1, s32[1,2048]{1,0:T(1,128)S(1)} %bitcast.7, bf16[2,40,2048]{2,1,0:T(8,128)(2,1)} %basis.1, bf16[2048,1024]{1,0:T(8,128)(2,1)} %x_im.1, bf16[2048,1024]{1,0:T(8,128)(2,1)} %x_im.1, bf16[2,320,2560]{2,1,0:T(8,128)(2,1)} %bitcast.8), custom_call_target="tpu_custom_call" | custom-call | tf_op jit(solution)/shard_map/source/pallas_call | solution.py:100
  13.4 3.3 %collective-permute-start = (bf16[4,8,80,512]{3,2,1,0:T(8,128)(2,1)S(1)}, bf16[4,8,80,512]{3,2,1,0:T(8,128)(2,1)S(1)}, u32[]{:S(2)}, u32[]{:S(2)}) collective-permute-start(bf16[4,8,80,512]{3,2,1,0:T(8,128)(2,1)S(1)} %get-tuple-element.29), channel_id=1, source_target_pairs={{0,4},{4,0},{1,5},{5,1},{2,6},{6,2},{3,7},{7,3},{8,12},{12,8},{9,1... | collective-permute-start | bytes 7864328 | tf_op jit(solution)/shard_map/ppermute | solution.py:21
  16.7 1.6 %turn.1 = bf16[2560,128]{1,0:T(8,128)(2,1)S(1)} custom-call(bf16[64,4,2,2560]{3,2,1,0:T(2,128)(2,1)} %f.1), custom_call_target="tpu_custom_call" | custom-call | tf_op jit(solution)/shard_map/turn/pallas_call | solution.py:132
  18.4 26.2 %all_to_all.15 = bf16[32,80,128]{2,1,0:T(8,128)(2,1)S(1)} all-to-all(bf16[32,80,128]{2,1,0:T(8,128)(2,1)S(1)} %bitcast.6), channel_id=1, replica_groups=mesh['x'=4,'z'=8,'c'=2,'y'=4] {'x','z'}, dimensions={0} | all-to-all | bytes 1310720 | tf_op jit(solution)/shard_map/all_to_all | solution.py:293
  44.6 0.0 collective-permute-done.recv
  44.6 2.2 %pattern.3 = (bf16[4,4,128,128]{3,2,1,0:T(8,128)(2,1)S(1)}, bf16[4,4,128,128]{3,2,1,0:T(8,128)(2,1)S(1)}, bf16[4,4,128,128]{3,2,1,0:T(8,128)(2,1)S(1)}, bf16[4,2...) custom-call(bf16[4,8,80,512]{3,2,1,0:T(8,128)(2,1)S(1)} %get-tuple-element.28.keep, ...), custom_call_target="tpu_custom_call" | custom-call | tf_op jit(solution)/shard_map/pattern/pallas_call | solution.py:185
  46.8 0.7 collective-permute-start.5
  47.5 2.0 %collective-permute-start.6 = (bf16[4,2,128,128]{3,2,1,0:T(8,128)(2,1)S(1)}, bf16[4,2,128,128]{3,2,1,0:T(8,128)(2,1)S(1)}, u32[]{:S(2)}, u32[]{:S(2)}) collective-permute-start(bf16[4,2,128,128]{3,2,1,0:T(8,128)(2,1)S(1)} %get-tuple-element.41), channel_id=1, source_target_pairs={{0,3},{1,0},{2,1},{3,2},{4,196},{5,197},{6,198},{7,199},{64,67},{6... | collective-permute-start | bytes 786440 | tf_op jit(solution)/shard_map/ppermute | solution.py:31
  49.6 2.2 %pattern.2 = (bf16[4,4,128,128]{3,2,1,0:T(8,128)(2,1)S(1)}, bf16[4,4,128,128]{3,2,1,0:T(8,128)(2,1)S(1)}, bf16[4,4,128,128]{3,2,1,0:T(8,128)(2,1)S(1)}, bf16[4,2...) custom-call(bf16[4,8,80,512]{3,2,1,0:T(8,128)(2,1)S(1)} %get-tuple-element.28.keep, ...), custom_call_target="tpu_custom_call" | custom-call | tf_op jit(solution)/shard_map/pattern/pallas_call | solution.py:185
  51.8 0.1 collective-permute-start.1
  51.9 2.7 %collective-permute-start.2 = (bf16[4,2,128,128]{3,2,1,0:T(8,128)(2,1)S(1)}, bf16[4,2,128,128]{3,2,1,0:T(8,128)(2,1)S(1)}, u32[]{:S(2)}, u32[]{:S(2)}) collective-permute-start(bf16[4,2,128,128]{3,2,1,0:T(8,128)(2,1)S(1)} %get-tuple-element.34), channel_id=1, source_target_pairs={{0,3},{1,0},{2,1},{3,2},{4,196},{5,197},{6,198},{7,199},{64,67},{6... | collective-permute-start | bytes 786440 | tf_op jit(solution)/shard_map/ppermute | solution.py:31
  54.6 0.0 collective-permute-done.5.from_behind
  54.6 0.0 collective-permute-done.6.from_ahead
  54.6 0.1 forward.3
  54.7 0.1 collective-permute-start.7
  54.8 2.7 %collective-permute-start.8 = (bf16[4,4,128,128]{3,2,1,0:T(8,128)(2,1)S(1)}, bf16[4,4,128,128]{3,2,1,0:T(8,128)(2,1)S(1)}, u32[]{:S(2)}, u32[]{:S(2)}) collective-permute-start(bf16[4,4,128,128]{3,2,1,0:T(8,128)(2,1)S(1)} %get-tuple-element.43), channel_id=1, source_target_pairs={{0,3},{1,0},{2,1},{3,2},{4,196},{5,197},{6,198},{7,199},{64,67},{6... | collective-permute-start | bytes 1572872 | tf_op jit(solution)/shard_map/ppermute | solution.py:31
  57.5 0.9 collective-permute-done.1.from_behind
  58.3 0.0 collective-permute-done.2.from_ahead
  58.3 0.1 forward.2
  58.5 0.1 collective-permute-start.3
  58.5 2.9 %collective-permute-start.4 = (bf16[4,4,128,128]{3,2,1,0:T(8,128)(2,1)S(1)}, bf16[4,4,128,128]{3,2,1,0:T(8,128)(2,1)S(1)}, u32[]{:S(2)}, u32[]{:S(2)}) collective-permute-start(bf16[4,4,128,128]{3,2,1,0:T(8,128)(2,1)S(1)} %get-tuple-element.36), channel_id=1, source_target_pairs={{0,3},{1,0},{2,1},{3,2},{4,196},{5,197},{6,198},{7,199},{64,67},{6... | collective-permute-start | bytes 1572872 | tf_op jit(solution)/shard_map/ppermute | solution.py:31
  61.5 2.5 %collective-permute-done.7.refs_1_ = bf16[4,4,128,128]{3,2,1,0:T(8,128)(2,1)S(1)} collective-permute-done((bf16[4,4,128,128]{3,2,1,0:T(8,128)(2,1)S(1)}, bf16[4,4,128,128]{3,2,1,0:T(8,128)(2,1)S(1)}, u32[]{:S(2)}, u32[]{:S(2)}) %collective-permute-start.7) | collective-permute-done | bytes 524320 | tf_op jit(solution)/shard_map/ppermute | solution.py:31
  64.0 0.0 collective-permute-done.8.refs_2_
  64.0 0.2 second.2
  64.2 5.7 %collective-permute-done.3.refs_1_ = bf16[4,4,128,128]{3,2,1,0:T(8,128)(2,1)S(1)} collective-permute-done((bf16[4,4,128,128]{3,2,1,0:T(8,128)(2,1)S(1)}, bf16[4,4,128,128]{3,2,1,0:T(8,128)(2,1)S(1)}, u32[]{:S(2)}, u32[]{:S(2)}) %collective-permute-start.3) | collective-permute-done | bytes 524320 | tf_op jit(solution)/shard_map/ppermute | solution.py:31
  69.9 0.0 collective-permute-done.4.refs_2_
  69.9 0.2 second.3
  70.1 2.7 %collective-permute-start.10 = (bf16[8,128,128]{2,1,0:T(8,128)(2,1)S(1)}, bf16[8,128,128]{2,1,0:T(8,128)(2,1)S(1)}, u32[]{:S(2)}, u32[]{:S(2)}) collective-permute-start(bf16[8,128,128]{2,1,0:T(8,128)(2,1)S(1)} %get-tuple-element.50), channel_id=1, source_target_pairs={{0,128},{1,129},{2,130},{3,131},{4,6},{5,7},{6,4},{7,5},{64,192},{... | collective-permute-start | bytes 786440 | tf_op jit(solution)/shard_map/ppermute | solution.py:31
  72.8 0.8 collective-permute-start.11
  73.6 0.7 collective-permute-start.9
  74.3 4.2 %collective-permute-done.10.refs_2_ = bf16[8,128,128]{2,1,0:T(8,128)(2,1)S(1)} collective-permute-done((bf16[8,128,128]{2,1,0:T(8,128)(2,1)S(1)}, bf16[8,128,128]{2,1,0:T(8,128)(2,1)S(1)}, u32[]{:S(2)}, u32[]{:S(2)}) %collective-permute-start.10) | collective-permute-done | bytes 262176 | tf_op jit(solution)/shard_map/ppermute | solution.py:31
  78.5 2.4 %collective-permute-done.11.refs_3_ = bf16[8,128,128]{2,1,0:T(8,128)(2,1)S(1)} collective-permute-done((bf16[8,128,128]{2,1,0:T(8,128)(2,1)S(1)}, bf16[8,128,128]{2,1,0:T(8,128)(2,1)S(1)}, u32[]{:S(2)}, u32[]{:S(2)}) %collective-permute-start.11) | collective-permute-done | bytes 262176 | tf_op jit(solution)/shard_map/ppermute | solution.py:31
  80.9 0.3 collective-permute-done.9.refs_1_
  81.2 0.1 third.1
  81.3 14.1 %all_to_all.16.parts = bf16[8,128,128]{2,1,0:T(8,128)(2,1)S(1)} all-to-all(bf16[8,128,128]{2,1,0:T(8,128)(2,1)S(1)} %third.1), channel_id=1, replica_groups=mesh['x'=4,'z'=8,'c'=2,'y'=4] {'z'}, dimensions={0} | all-to-all | bytes 524288 | tf_op jit(solution)/shard_map/all_to_all | solution.py:310
  95.4 0.1 last.1
  95.5 22.4 %all_to_all.17 = f32[64,1,128]{2,1,0:T(1,128)S(1)} all-to-all(f32[64,1,128]{2,1,0:T(1,128)S(1)} %get-tuple-element.53), channel_id=1, replica_groups=mesh['x'=4,'z'=8,'c'=2,'y'=4] {'x','z','c'}, dimensions={0} | all-to-all | bytes 65536 | tf_op jit(solution)/shard_map/all_to_all | solution.py:312
  117.9 0.1 reduce_max.9
  118.0 0.0 copy-start.2
  118.0 0.6 broadcast_divide_fusion
  118.6 0.0 copy-done.2
  (1 shorter events, 0.0 us)
Async XLA Ops:
  0.6 0.7 copy-start
  1.3 0.7 copy-start.1
  13.4 31.1 %collective-permute-start = (bf16[4,8,80,512]{3,2,1,0:T(8,128)(2,1)S(1)}, bf16[4,8,80,512]{3,2,1,0:T(8,128)(2,1)S(1)}, u32[]{:S(2)}, u32[]{:S(2)}) collective-permute-start(bf16[4,8,80,512]{3,2,1,0:T(8,128)(2,1)S(1)} %get-tuple-element.29), channel_id=1, source_target_pairs={{0,4},{4,0},{1,5},{5,1},{2,6},{6,2},{3,7},{7,3},{8,12},{12,8},{9,1... | collective-permute-start | bytes 7864328 | tf_op jit(solution)/shard_map/ppermute | solution.py:21
  46.8 7.8 %collective-permute-start.5 = (bf16[4,2,128,128]{3,2,1,0:T(8,128)(2,1)S(1)}, bf16[4,2,128,128]{3,2,1,0:T(8,128)(2,1)S(1)}, u32[]{:S(2)}, u32[]{:S(2)}) collective-permute-start(bf16[4,2,128,128]{3,2,1,0:T(8,128)(2,1)S(1)} %get-tuple-element.40), channel_id=1, source_target_pairs={{0,1},{1,2},{2,3},{3,0},{4,68},{5,69},{6,70},{7,71},{64,65},{65,66... | collective-permute-start | bytes 786440 | tf_op jit(solution)/shard_map/ppermute | solution.py:31
  47.5 7.0 %collective-permute-start.6 = (bf16[4,2,128,128]{3,2,1,0:T(8,128)(2,1)S(1)}, bf16[4,2,128,128]{3,2,1,0:T(8,128)(2,1)S(1)}, u32[]{:S(2)}, u32[]{:S(2)}) collective-permute-start(bf16[4,2,128,128]{3,2,1,0:T(8,128)(2,1)S(1)} %get-tuple-element.41), channel_id=1, source_target_pairs={{0,3},{1,0},{2,1},{3,2},{4,196},{5,197},{6,198},{7,199},{64,67},{6... | collective-permute-start | bytes 786440 | tf_op jit(solution)/shard_map/ppermute | solution.py:31
  51.8 6.5 %collective-permute-start.1 = (bf16[4,2,128,128]{3,2,1,0:T(8,128)(2,1)S(1)}, bf16[4,2,128,128]{3,2,1,0:T(8,128)(2,1)S(1)}, u32[]{:S(2)}, u32[]{:S(2)}) collective-permute-start(bf16[4,2,128,128]{3,2,1,0:T(8,128)(2,1)S(1)} %get-tuple-element.33), channel_id=1, source_target_pairs={{0,1},{1,2},{2,3},{3,0},{4,68},{5,69},{6,70},{7,71},{64,65},{65,66... | collective-permute-start | bytes 786440 | tf_op jit(solution)/shard_map/ppermute | solution.py:31
  51.9 6.4 %collective-permute-start.2 = (bf16[4,2,128,128]{3,2,1,0:T(8,128)(2,1)S(1)}, bf16[4,2,128,128]{3,2,1,0:T(8,128)(2,1)S(1)}, u32[]{:S(2)}, u32[]{:S(2)}) collective-permute-start(bf16[4,2,128,128]{3,2,1,0:T(8,128)(2,1)S(1)} %get-tuple-element.34), channel_id=1, source_target_pairs={{0,3},{1,0},{2,1},{3,2},{4,196},{5,197},{6,198},{7,199},{64,67},{6... | collective-permute-start | bytes 786440 | tf_op jit(solution)/shard_map/ppermute | solution.py:31
  54.7 9.3 %collective-permute-start.7 = (bf16[4,4,128,128]{3,2,1,0:T(8,128)(2,1)S(1)}, bf16[4,4,128,128]{3,2,1,0:T(8,128)(2,1)S(1)}, u32[]{:S(2)}, u32[]{:S(2)}) collective-permute-start(bf16[4,4,128,128]{3,2,1,0:T(8,128)(2,1)S(1)} %get-tuple-element.42), channel_id=1, source_target_pairs={{0,1},{1,2},{2,3},{3,0},{4,68},{5,69},{6,70},{7,71},{64,65},{65,66... | collective-permute-start | bytes 1572872 | tf_op jit(solution)/shard_map/ppermute | solution.py:31
  54.8 9.2 %collective-permute-start.8 = (bf16[4,4,128,128]{3,2,1,0:T(8,128)(2,1)S(1)}, bf16[4,4,128,128]{3,2,1,0:T(8,128)(2,1)S(1)}, u32[]{:S(2)}, u32[]{:S(2)}) collective-permute-start(bf16[4,4,128,128]{3,2,1,0:T(8,128)(2,1)S(1)} %get-tuple-element.43), channel_id=1, source_target_pairs={{0,3},{1,0},{2,1},{3,2},{4,196},{5,197},{6,198},{7,199},{64,67},{6... | collective-permute-start | bytes 1572872 | tf_op jit(solution)/shard_map/ppermute | solution.py:31
  58.5 11.5 %collective-permute-start.3 = (bf16[4,4,128,128]{3,2,1,0:T(8,128)(2,1)S(1)}, bf16[4,4,128,128]{3,2,1,0:T(8,128)(2,1)S(1)}, u32[]{:S(2)}, u32[]{:S(2)}) collective-permute-start(bf16[4,4,128,128]{3,2,1,0:T(8,128)(2,1)S(1)} %get-tuple-element.35), channel_id=1, source_target_pairs={{0,1},{1,2},{2,3},{3,0},{4,68},{5,69},{6,70},{7,71},{64,65},{65,66... | collective-permute-start | bytes 1572872 | tf_op jit(solution)/shard_map/ppermute | solution.py:31
  58.5 11.4 %collective-permute-start.4 = (bf16[4,4,128,128]{3,2,1,0:T(8,128)(2,1)S(1)}, bf16[4,4,128,128]{3,2,1,0:T(8,128)(2,1)S(1)}, u32[]{:S(2)}, u32[]{:S(2)}) collective-permute-start(bf16[4,4,128,128]{3,2,1,0:T(8,128)(2,1)S(1)} %get-tuple-element.36), channel_id=1, source_target_pairs={{0,3},{1,0},{2,1},{3,2},{4,196},{5,197},{6,198},{7,199},{64,67},{6... | collective-permute-start | bytes 1572872 | tf_op jit(solution)/shard_map/ppermute | solution.py:31
  70.1 8.4 %collective-permute-start.10 = (bf16[8,128,128]{2,1,0:T(8,128)(2,1)S(1)}, bf16[8,128,128]{2,1,0:T(8,128)(2,1)S(1)}, u32[]{:S(2)}, u32[]{:S(2)}) collective-permute-start(bf16[8,128,128]{2,1,0:T(8,128)(2,1)S(1)} %get-tuple-element.50), channel_id=1, source_target_pairs={{0,128},{1,129},{2,130},{3,131},{4,6},{5,7},{6,4},{7,5},{64,192},{... | collective-permute-start | bytes 786440 | tf_op jit(solution)/shard_map/ppermute | solution.py:31
  72.8 8.0 %collective-permute-start.11 = (bf16[8,128,128]{2,1,0:T(8,128)(2,1)S(1)}, bf16[8,128,128]{2,1,0:T(8,128)(2,1)S(1)}, u32[]{:S(2)}, u32[]{:S(2)}) collective-permute-start(bf16[8,128,128]{2,1,0:T(8,128)(2,1)S(1)} %get-tuple-element.51), channel_id=1, source_target_pairs={{0,192},{1,193},{2,194},{3,195},{4,7},{5,4},{6,5},{7,6},{64,0},{65... | collective-permute-start | bytes 786440 | tf_op jit(solution)/shard_map/ppermute | solution.py:31
  73.6 7.6 %collective-permute-start.9 = (bf16[8,128,128]{2,1,0:T(8,128)(2,1)S(1)}, bf16[8,128,128]{2,1,0:T(8,128)(2,1)S(1)}, u32[]{:S(2)}, u32[]{:S(2)}) collective-permute-start(bf16[8,128,128]{2,1,0:T(8,128)(2,1)S(1)} %get-tuple-element.49), channel_id=1, source_target_pairs={{0,64},{1,65},{2,66},{3,67},{4,5},{5,6},{6,7},{7,4},{64,128},{65,1... | collective-permute-start | bytes 786440 | tf_op jit(solution)/shard_map/ppermute | solution.py:31
  118.0 0.6 copy-start.2

commit v5 on v4

--- a/solution.py
+++ b/solution.py
@@ -13,6 +13,7 @@
 Q = NE // NY
 LEAF_STEPS = 2
 CHUNKS = 2
+ZB = 2
 FAR = (2, 1, 3)
 PLACE = {0: 0, 1: 1, 3: 2}
 
@@ -123,7 +124,12 @@
 
 def turn_kernel(f, out):
     wide = f[:, 0].astype(F32)
-    out[...] = jnp.concatenate([wide[:, 0], wide[:, 1]], axis=0).astype(BF16).T
+    turned = jnp.concatenate([wide[:, 0], wide[:, 1]], axis=0).astype(BF16).T
+    rows = NC * R
+    for x in range(NX // 2):
+        for z in range(NZ):
+            at = (x * NZ + z) * rows
+            out[z, x] = turned[at : at + rows]
 
 
 def turn(factor):
@@ -133,8 +139,8 @@
         turn_kernel,
         grid=(steps,),
         in_specs=[pl.BlockSpec((A, 1, 2, width), lambda i: (0, lax.axis_index("y"), 0, i))],
-        out_specs=pl.BlockSpec((width, 2 * A), lambda i: (i, 0)),
-        out_shape=jax.ShapeDtypeStruct((columns, 2 * A), BF16),
+        out_specs=pl.BlockSpec((NZ, NX // steps, NC * R, 2 * A), lambda i: (0, i, 0, 0)),
+        out_shape=jax.ShapeDtypeStruct((NZ, NX, NC * R, 2 * A), BF16),
         compiler_params=params("arbitrary"),
         name="turn",
     )(in_hbm(factor))
@@ -145,11 +151,11 @@
     core, x_own, y_own = (lax.axis_index(a) for a in ("c", "x", "y"))
     first = core == 0
 
-    def product(x):
-        both = fac[x, 0].astype(F32)
+    def product(x, z):
+        both = fac[z, x].astype(F32)
         turned = jnp.concatenate([-both[:, A:], both[:, :A]], axis=1)
         left = jnp.concatenate([both[:R], turned[:R], both[R:], turned[R:]], axis=0).astype(BF16)
-        own, other = keep[x, 0], recv[x, 0]
+        own, other = keep[x, z], recv[x, z]
         right = jnp.concatenate(
             [jnp.where(first, own, other), jnp.where(first, other, own)], axis=0
         )
@@ -157,27 +163,30 @@
 
     @pl.when(core == 1)
     def _():
-        for k in range(NX):
-            piece = product(lax.rem(x_own + k, NX))
-            for y in range(NY):
-                to = halves[y // 2].at[0, y % 2] if k == 2 else pieces[PLACE[k]].at[0, y]
-                to[...] = piece[:, y * Q : (y + 1) * Q]
+        for z in range(ZB):
+            for k in range(NX):
+                piece = product(lax.rem(x_own + k, NX), z)
+                for y in range(NY):
+                    to = halves[y // 2].at[z, y % 2] if k == 2 else pieces[PLACE[k]].at[z, y]
+                    to[...] = piece[:, y * Q : (y + 1) * Q]
 
     @pl.when(core == 0)
     def _():
-        for x in range(NX):
-            row[x] = product(x)
+        for z in range(ZB):
+            for x in range(NX):
+                row[z, x] = product(x, z)
         for k in range(NY):
             at = pl.multiple_of(lax.rem(y_own + k, NY) * Q, Q)
             if k == 2:
                 for half in range(2):
-                    halves[half][0] = row[2 * half : 2 * half + 2, :, pl.ds(at, Q)]
+                    halves[half][...] = row[:, 2 * half : 2 * half + 2, :, pl.ds(at, Q)]
             else:
-                pieces[PLACE[k]][0] = row[:, :, pl.ds(at, Q)]
+                pieces[PLACE[k]][...] = row[:, :, :, pl.ds(at, Q)]
 
 
 def pattern(keep, recv, fac, chunk):
-    steps = NZ // CHUNKS
+    rows = NZ // CHUNKS
+    steps = rows // ZB
 
     def at(i):
         return (0, chunk * steps + i, 0, 0)
@@ -186,15 +195,15 @@
         pattern_kernel,
         grid=(steps,),
         in_specs=[
-            pl.BlockSpec((NX, 1, 2 * R, NE), at),
-            pl.BlockSpec((NX, 1, 2 * R, NE), at),
-            pl.BlockSpec((NX, 1, 2 * R, 2 * A), at),
+            pl.BlockSpec((NX, ZB, 2 * R, NE), at),
+            pl.BlockSpec((NX, ZB, 2 * R, NE), at),
+            pl.BlockSpec((ZB, NX, 2 * R, 2 * A), lambda i: (chunk * steps + i, 0, 0, 0)),
         ],
-        out_specs=[pl.BlockSpec((1, NX, 2 * A, Q), lambda i: (i, 0, 0, 0))] * 3
-        + [pl.BlockSpec((1, NX // 2, 2 * A, Q), lambda i: (i, 0, 0, 0))] * 2,
-        out_shape=[jax.ShapeDtypeStruct((steps, NX, 2 * A, Q), BF16)] * 3
-        + [jax.ShapeDtypeStruct((steps, NX // 2, 2 * A, Q), BF16)] * 2,
-        scratch_shapes=[pltpu.VMEM((NX, 2 * A, NE), BF16)],
+        out_specs=[pl.BlockSpec((ZB, NX, 2 * A, Q), lambda i: (i, 0, 0, 0))] * 3
+        + [pl.BlockSpec((ZB, NX // 2, 2 * A, Q), lambda i: (i, 0, 0, 0))] * 2,
+        out_shape=[jax.ShapeDtypeStruct((rows, NX, 2 * A, Q), BF16)] * 3
+        + [jax.ShapeDtypeStruct((rows, NX // 2, 2 * A, Q), BF16)] * 2,
+        scratch_shapes=[pltpu.VMEM((ZB, NX, 2 * A, NE), BF16)],
         compiler_params=params("arbitrary"),
         name="pattern",
     )(keep, recv, fac)
@@ -290,11 +299,11 @@
 def body(currents, leaf_basis, leaf_box, box_count, merge_factor, angle_factor):
     own = turn(angle_factor)
     own = own.reshape(NX * NZ, NC * R, 2 * A)
-    spread = lax.all_to_all(own, ("x", "z"), 0, 0, tiled=True)
+    spread = lax.all_to_all(own, ("z", "x"), 0, 0, tiled=True)
     box = leaf_box.reshape(1, S_DEV)
     coefs = merge_factor.swapaxes(1, 2)
     keep, send = source(box_count, box, leaf_basis, currents, coefs)
-    fac = spread.reshape(NX, NZ, NC * R, 2 * A)
+    fac = spread.reshape(NZ, NX, NC * R, 2 * A)
     recv = other_core(send)
     made, sums = [], []
     for chunk in range(CHUNKS):

time: 119 us -> 117 us (0.983)
    all_to_all x1, blocking collectives: 26.2 us -> 28.3 us  [body(): spread = lax.all_to_all(own, ('z', 'x'), 0, 0, tiled=True)]
  transfers between devices with their start and end apart: 12 -> 12, of which waited for: 6 -> 5; matrix products, arithmetic and copies ran while one was open for 0% -> 0% of each run, Pallas kernels for 4% -> 3%
where the time goes in v5:
time: 117 us
  blocking collectives  63.1 us (54%)
  starting transfers between devices  18.6 us (16%)
  Pallas kernels  17.5 us (15%)
  waiting for transfers between devices  15.2 us (13%)
  local copies, waits for them, and re-layouts  1.35 us (1%)
    all_to_all x1, blocking collectives, body(): spread = lax.all_to_all(own, ('z', 'x'), 0, 0, tiled=True)  28.3 us
    all_to_all x1, blocking collectives, body(): tops = lax.all_to_all(tops, ('x', 'z', 'c'), 0, 0, tiled=True)  21.7 us
    ppermute x11, starting transfers between devices, shift(): return lax.ppermute(v, ('x', 'c', 'y'), pairs)  15.3 us
    ppermute x11, waiting for transfers between devices, shift(): return lax.ppermute(v, ('x', 'c', 'y'), pairs)  15.2 us
    all_to_all x1, blocking collectives, body(): parts = lax.all_to_all(parts, 'z', 0, 0, tiled=True)  13.1 us
    pallas_call x1, Pallas kernels, source(): pl.pallas_call(source_kernel, grid_spec=pltpu.PrefetchScalarGridSpec(num_...  11.5 us
    pallas_call x2, Pallas kernels, pattern(): pl.pallas_call(pattern_kernel, grid=(steps,), in_specs=[pl.BlockSpec((NX,...  3.53 us
    ppermute x1, starting transfers between devices, other_core(): return lax.ppermute(v, 'c', [(0, 1), (1, 0)])  3.28 us
  transfers between devices with their start and end apart: 12, of which 5 were waited for; matrix products, arithmetic and copies ran while one was open for 0% of the time, Pallas kernels for 3%

profile of v5, /device:TPU:1, one launch (start us, length us, event | category | flops | bytes accessed | tf_op | source)
XLA Modules:
  0.0 117.2 jit_solution(1076201175397092514)
XLA Ops:
  0.6 0.0 copy-start
  0.6 0.7 copy-done
  1.3 0.0 copy-start.1
  1.3 0.7 copy-done.1
  2.0 11.5 %source.1 = (bf16[4,8,80,512]{3,2,1,0:T(8,128)(2,1)S(1)}, bf16[4,8,80,512]{3,2,1,0:T(8,128)(2,1)S(1)}) custom-call(s32[8]{0:T(128)S(1)} %copy-done.1, s32[1,2048]{1,0:T(1,128)S(1)} %bitcast.7, bf16[2,40,2048]{2,1,0:T(8,128)(2,1)} %basis.1, bf16[2048,1024]{1,0:T(8,128)(2,1)} %x_im.1, bf16[2048,1024]{1,0:T(8,128)(2,1)} %x_im.1, bf16[2,320,2560]{2,1,0:T(8,128)(2,1)} %bitcast.8), custom_call_target="tpu_custom_call" | custom-call | tf_op jit(solution)/shard_map/source/pallas_call | solution.py:101
  13.4 3.3 %collective-permute-start = (bf16[4,8,80,512]{3,2,1,0:T(8,128)(2,1)S(1)}, bf16[4,8,80,512]{3,2,1,0:T(8,128)(2,1)S(1)}, u32[]{:S(2)}, u32[]{:S(2)}) collective-permute-start(bf16[4,8,80,512]{3,2,1,0:T(8,128)(2,1)S(1)} %get-tuple-element.29), channel_id=1, source_target_pairs={{0,4},{4,0},{1,5},{5,1},{2,6},{6,2},{3,7},{7,3},{8,12},{12,8},{9,1... | collective-permute-start | bytes 7864328 | tf_op jit(solution)/shard_map/ppermute | solution.py:22
  16.7 1.7 %turn.1 = bf16[8,4,80,128]{3,2,1,0:T(8,128)(2,1)S(1)} custom-call(bf16[64,4,2,2560]{3,2,1,0:T(2,128)(2,1)} %f.1), custom_call_target="tpu_custom_call" | custom-call | tf_op jit(solution)/shard_map/turn/pallas_call | solution.py:138
  18.4 28.3 %all_to_all.15 = bf16[32,80,128]{2,1,0:T(8,128)(2,1)S(1)} all-to-all(bf16[32,80,128]{2,1,0:T(8,128)(2,1)S(1)} %bitcast.6), channel_id=1, replica_groups=mesh['x'=4,'z'=8,'c'=2,'y'=4] {'z','x'}, dimensions={0} | all-to-all | bytes 1310720 | tf_op jit(solution)/shard_map/all_to_all | solution.py:302
  46.7 0.0 collective-permute-done.recv
  46.7 1.8 %pattern.3 = (bf16[4,4,128,128]{3,2,1,0:T(8,128)(2,1)S(1)}, bf16[4,4,128,128]{3,2,1,0:T(8,128)(2,1)S(1)}, bf16[4,4,128,128]{3,2,1,0:T(8,128)(2,1)S(1)}, bf16[4,2...) custom-call(bf16[4,8,80,512]{3,2,1,0:T(8,128)(2,1)S(1)} %get-tuple-element.28.keep, ...), custom_call_target="tpu_custom_call" | custom-call | tf_op jit(solution)/shard_map/pattern/pallas_call | solution.py:194
  48.5 1.2 %collective-permute-start.5 = (bf16[4,2,128,128]{3,2,1,0:T(8,128)(2,1)S(1)}, bf16[4,2,128,128]{3,2,1,0:T(8,128)(2,1)S(1)}, u32[]{:S(2)}, u32[]{:S(2)}) collective-permute-start(bf16[4,2,128,128]{3,2,1,0:T(8,128)(2,1)S(1)} %get-tuple-element.40), channel_id=1, source_target_pairs={{0,1},{1,2},{2,3},{3,0},{4,68},{5,69},{6,70},{7,71},{64,65},{65,66... | collective-permute-start | bytes 786440 | tf_op jit(solution)/shard_map/ppermute | solution.py:32
  49.7 1.6 %collective-permute-start.6 = (bf16[4,2,128,128]{3,2,1,0:T(8,128)(2,1)S(1)}, bf16[4,2,128,128]{3,2,1,0:T(8,128)(2,1)S(1)}, u32[]{:S(2)}, u32[]{:S(2)}) collective-permute-start(bf16[4,2,128,128]{3,2,1,0:T(8,128)(2,1)S(1)} %get-tuple-element.41), channel_id=1, source_target_pairs={{0,3},{1,0},{2,1},{3,2},{4,196},{5,197},{6,198},{7,199},{64,67},{6... | collective-permute-start | bytes 786440 | tf_op jit(solution)/shard_map/ppermute | solution.py:32
  51.3 1.8 %pattern.2 = (bf16[4,4,128,128]{3,2,1,0:T(8,128)(2,1)S(1)}, bf16[4,4,128,128]{3,2,1,0:T(8,128)(2,1)S(1)}, bf16[4,4,128,128]{3,2,1,0:T(8,128)(2,1)S(1)}, bf16[4,2...) custom-call(bf16[4,8,80,512]{3,2,1,0:T(8,128)(2,1)S(1)} %get-tuple-element.28.keep, ...), custom_call_target="tpu_custom_call" | custom-call | tf_op jit(solution)/shard_map/pattern/pallas_call | solution.py:194
  53.1 0.1 collective-permute-start.1
  53.2 2.7 %collective-permute-start.2 = (bf16[4,2,128,128]{3,2,1,0:T(8,128)(2,1)S(1)}, bf16[4,2,128,128]{3,2,1,0:T(8,128)(2,1)S(1)}, u32[]{:S(2)}, u32[]{:S(2)}) collective-permute-start(bf16[4,2,128,128]{3,2,1,0:T(8,128)(2,1)S(1)} %get-tuple-element.34), channel_id=1, source_target_pairs={{0,3},{1,0},{2,1},{3,2},{4,196},{5,197},{6,198},{7,199},{64,67},{6... | collective-permute-start | bytes 786440 | tf_op jit(solution)/shard_map/ppermute | solution.py:32
  55.8 0.0 collective-permute-done.5.from_behind
  55.8 0.0 collective-permute-done.6.from_ahead
  55.8 0.1 forward.3
  56.0 1.0 collective-permute-start.7
  56.9 1.8 %collective-permute-start.8 = (bf16[4,4,128,128]{3,2,1,0:T(8,128)(2,1)S(1)}, bf16[4,4,128,128]{3,2,1,0:T(8,128)(2,1)S(1)}, u32[]{:S(2)}, u32[]{:S(2)}) collective-permute-start(bf16[4,4,128,128]{3,2,1,0:T(8,128)(2,1)S(1)} %get-tuple-element.43), channel_id=1, source_target_pairs={{0,3},{1,0},{2,1},{3,2},{4,196},{5,197},{6,198},{7,199},{64,67},{6... | collective-permute-start | bytes 1572872 | tf_op jit(solution)/shard_map/ppermute | solution.py:32
  58.7 0.9 collective-permute-done.1.from_behind
  59.6 0.0 collective-permute-done.2.from_ahead
  59.6 0.1 forward.2
  59.7 0.2 collective-permute-start.3
  59.9 2.6 %collective-permute-start.4 = (bf16[4,4,128,128]{3,2,1,0:T(8,128)(2,1)S(1)}, bf16[4,4,128,128]{3,2,1,0:T(8,128)(2,1)S(1)}, u32[]{:S(2)}, u32[]{:S(2)}) collective-permute-start(bf16[4,4,128,128]{3,2,1,0:T(8,128)(2,1)S(1)} %get-tuple-element.36), channel_id=1, source_target_pairs={{0,3},{1,0},{2,1},{3,2},{4,196},{5,197},{6,198},{7,199},{64,67},{6... | collective-permute-start | bytes 1572872 | tf_op jit(solution)/shard_map/ppermute | solution.py:32
  62.6 3.0 %collective-permute-done.7.refs_1_ = bf16[4,4,128,128]{3,2,1,0:T(8,128)(2,1)S(1)} collective-permute-done((bf16[4,4,128,128]{3,2,1,0:T(8,128)(2,1)S(1)}, bf16[4,4,128,128]{3,2,1,0:T(8,128)(2,1)S(1)}, u32[]{:S(2)}, u32[]{:S(2)}) %collective-permute-start.7) | collective-permute-done | bytes 524320 | tf_op jit(solution)/shard_map/ppermute | solution.py:32
  65.6 0.0 collective-permute-done.8.refs_2_
  65.6 0.2 second.2
  65.8 5.4 %collective-permute-done.3.refs_1_ = bf16[4,4,128,128]{3,2,1,0:T(8,128)(2,1)S(1)} collective-permute-done((bf16[4,4,128,128]{3,2,1,0:T(8,128)(2,1)S(1)}, bf16[4,4,128,128]{3,2,1,0:T(8,128)(2,1)S(1)}, u32[]{:S(2)}, u32[]{:S(2)}) %collective-permute-start.3) | collective-permute-done | bytes 524320 | tf_op jit(solution)/shard_map/ppermute | solution.py:32
  71.2 0.0 collective-permute-done.4.refs_2_
  71.2 0.2 second.3
  71.4 2.7 %collective-permute-start.10 = (bf16[8,128,128]{2,1,0:T(8,128)(2,1)S(1)}, bf16[8,128,128]{2,1,0:T(8,128)(2,1)S(1)}, u32[]{:S(2)}, u32[]{:S(2)}) collective-permute-start(bf16[8,128,128]{2,1,0:T(8,128)(2,1)S(1)} %get-tuple-element.50), channel_id=1, source_target_pairs={{0,128},{1,129},{2,130},{3,131},{4,6},{5,7},{6,4},{7,5},{64,192},{... | collective-permute-start | bytes 786440 | tf_op jit(solution)/shard_map/ppermute | solution.py:32
  74.1 0.8 collective-permute-start.11
  74.9 0.7 collective-permute-start.9
  75.6 3.0 %collective-permute-done.10.refs_2_ = bf16[8,128,128]{2,1,0:T(8,128)(2,1)S(1)} collective-permute-done((bf16[8,128,128]{2,1,0:T(8,128)(2,1)S(1)}, bf16[8,128,128]{2,1,0:T(8,128)(2,1)S(1)}, u32[]{:S(2)}, u32[]{:S(2)}) %collective-permute-start.10) | collective-permute-done | bytes 262176 | tf_op jit(solution)/shard_map/ppermute | solution.py:32
  78.5 2.9 %collective-permute-done.11.refs_3_ = bf16[8,128,128]{2,1,0:T(8,128)(2,1)S(1)} collective-permute-done((bf16[8,128,128]{2,1,0:T(8,128)(2,1)S(1)}, bf16[8,128,128]{2,1,0:T(8,128)(2,1)S(1)}, u32[]{:S(2)}, u32[]{:S(2)}) %collective-permute-start.11) | collective-permute-done | bytes 262176 | tf_op jit(solution)/shard_map/ppermute | solution.py:32
  81.4 0.0 collective-permute-done.9.refs_1_
  81.4 0.1 third.1
  81.5 13.1 %all_to_all.16.parts = bf16[8,128,128]{2,1,0:T(8,128)(2,1)S(1)} all-to-all(bf16[8,128,128]{2,1,0:T(8,128)(2,1)S(1)} %third.1), channel_id=1, replica_groups=mesh['x'=4,'z'=8,'c'=2,'y'=4] {'z'}, dimensions={0} | all-to-all | bytes 524288 | tf_op jit(solution)/shard_map/all_to_all | solution.py:319
  94.7 0.1 last.1
  94.7 21.7 %all_to_all.17 = f32[64,1,128]{2,1,0:T(1,128)S(1)} all-to-all(f32[64,1,128]{2,1,0:T(1,128)S(1)} %get-tuple-element.53), channel_id=1, replica_groups=mesh['x'=4,'z'=8,'c'=2,'y'=4] {'x','z','c'}, dimensions={0} | all-to-all | bytes 65536 | tf_op jit(solution)/shard_map/all_to_all | solution.py:321
  116.4 0.1 reduce_max.9
  116.5 0.0 copy-start.2
  116.5 0.6 broadcast_divide_fusion
  117.2 0.0 copy-done.2
  (1 shorter events, 0.0 us)
Async XLA Ops:
  0.6 0.7 copy-start
  1.3 0.7 copy-start.1
  13.4 33.2 %collective-permute-start = (bf16[4,8,80,512]{3,2,1,0:T(8,128)(2,1)S(1)}, bf16[4,8,80,512]{3,2,1,0:T(8,128)(2,1)S(1)}, u32[]{:S(2)}, u32[]{:S(2)}) collective-permute-start(bf16[4,8,80,512]{3,2,1,0:T(8,128)(2,1)S(1)} %get-tuple-element.29), channel_id=1, source_target_pairs={{0,4},{4,0},{1,5},{5,1},{2,6},{6,2},{3,7},{7,3},{8,12},{12,8},{9,1... | collective-permute-start | bytes 7864328 | tf_op jit(solution)/shard_map/ppermute | solution.py:22
  48.5 7.4 %collective-permute-start.5 = (bf16[4,2,128,128]{3,2,1,0:T(8,128)(2,1)S(1)}, bf16[4,2,128,128]{3,2,1,0:T(8,128)(2,1)S(1)}, u32[]{:S(2)}, u32[]{:S(2)}) collective-permute-start(bf16[4,2,128,128]{3,2,1,0:T(8,128)(2,1)S(1)} %get-tuple-element.40), channel_id=1, source_target_pairs={{0,1},{1,2},{2,3},{3,0},{4,68},{5,69},{6,70},{7,71},{64,65},{65,66... | collective-permute-start | bytes 786440 | tf_op jit(solution)/shard_map/ppermute | solution.py:32
  49.7 6.1 %collective-permute-start.6 = (bf16[4,2,128,128]{3,2,1,0:T(8,128)(2,1)S(1)}, bf16[4,2,128,128]{3,2,1,0:T(8,128)(2,1)S(1)}, u32[]{:S(2)}, u32[]{:S(2)}) collective-permute-start(bf16[4,2,128,128]{3,2,1,0:T(8,128)(2,1)S(1)} %get-tuple-element.41), channel_id=1, source_target_pairs={{0,3},{1,0},{2,1},{3,2},{4,196},{5,197},{6,198},{7,199},{64,67},{6... | collective-permute-start | bytes 786440 | tf_op jit(solution)/shard_map/ppermute | solution.py:32
  53.1 6.5 %collective-permute-start.1 = (bf16[4,2,128,128]{3,2,1,0:T(8,128)(2,1)S(1)}, bf16[4,2,128,128]{3,2,1,0:T(8,128)(2,1)S(1)}, u32[]{:S(2)}, u32[]{:S(2)}) collective-permute-start(bf16[4,2,128,128]{3,2,1,0:T(8,128)(2,1)S(1)} %get-tuple-element.33), channel_id=1, source_target_pairs={{0,1},{1,2},{2,3},{3,0},{4,68},{5,69},{6,70},{7,71},{64,65},{65,66... | collective-permute-start | bytes 786440 | tf_op jit(solution)/shard_map/ppermute | solution.py:32
  53.2 6.4 %collective-permute-start.2 = (bf16[4,2,128,128]{3,2,1,0:T(8,128)(2,1)S(1)}, bf16[4,2,128,128]{3,2,1,0:T(8,128)(2,1)S(1)}, u32[]{:S(2)}, u32[]{:S(2)}) collective-permute-start(bf16[4,2,128,128]{3,2,1,0:T(8,128)(2,1)S(1)} %get-tuple-element.34), channel_id=1, source_target_pairs={{0,3},{1,0},{2,1},{3,2},{4,196},{5,197},{6,198},{7,199},{64,67},{6... | collective-permute-start | bytes 786440 | tf_op jit(solution)/shard_map/ppermute | solution.py:32
  56.0 9.6 %collective-permute-start.7 = (bf16[4,4,128,128]{3,2,1,0:T(8,128)(2,1)S(1)}, bf16[4,4,128,128]{3,2,1,0:T(8,128)(2,1)S(1)}, u32[]{:S(2)}, u32[]{:S(2)}) collective-permute-start(bf16[4,4,128,128]{3,2,1,0:T(8,128)(2,1)S(1)} %get-tuple-element.42), channel_id=1, source_target_pairs={{0,1},{1,2},{2,3},{3,0},{4,68},{5,69},{6,70},{7,71},{64,65},{65,66... | collective-permute-start | bytes 1572872 | tf_op jit(solution)/shard_map/ppermute | solution.py:32
  56.9 8.7 %collective-permute-start.8 = (bf16[4,4,128,128]{3,2,1,0:T(8,128)(2,1)S(1)}, bf16[4,4,128,128]{3,2,1,0:T(8,128)(2,1)S(1)}, u32[]{:S(2)}, u32[]{:S(2)}) collective-permute-start(bf16[4,4,128,128]{3,2,1,0:T(8,128)(2,1)S(1)} %get-tuple-element.43), channel_id=1, source_target_pairs={{0,3},{1,0},{2,1},{3,2},{4,196},{5,197},{6,198},{7,199},{64,67},{6... | collective-permute-start | bytes 1572872 | tf_op jit(solution)/shard_map/ppermute | solution.py:32
  59.7 11.5 %collective-permute-start.3 = (bf16[4,4,128,128]{3,2,1,0:T(8,128)(2,1)S(1)}, bf16[4,4,128,128]{3,2,1,0:T(8,128)(2,1)S(1)}, u32[]{:S(2)}, u32[]{:S(2)}) collective-permute-start(bf16[4,4,128,128]{3,2,1,0:T(8,128)(2,1)S(1)} %get-tuple-element.35), channel_id=1, source_target_pairs={{0,1},{1,2},{2,3},{3,0},{4,68},{5,69},{6,70},{7,71},{64,65},{65,66... | collective-permute-start | bytes 1572872 | tf_op jit(solution)/shard_map/ppermute | solution.py:32
  59.9 11.3 %collective-permute-start.4 = (bf16[4,4,128,128]{3,2,1,0:T(8,128)(2,1)S(1)}, bf16[4,4,128,128]{3,2,1,0:T(8,128)(2,1)S(1)}, u32[]{:S(2)}, u32[]{:S(2)}) collective-permute-start(bf16[4,4,128,128]{3,2,1,0:T(8,128)(2,1)S(1)} %get-tuple-element.36), channel_id=1, source_target_pairs={{0,3},{1,0},{2,1},{3,2},{4,196},{5,197},{6,198},{7,199},{64,67},{6... | collective-permute-start | bytes 1572872 | tf_op jit(solution)/shard_map/ppermute | solution.py:32
  71.4 7.2 %collective-permute-start.10 = (bf16[8,128,128]{2,1,0:T(8,128)(2,1)S(1)}, bf16[8,128,128]{2,1,0:T(8,128)(2,1)S(1)}, u32[]{:S(2)}, u32[]{:S(2)}) collective-permute-start(bf16[8,128,128]{2,1,0:T(8,128)(2,1)S(1)} %get-tuple-element.50), channel_id=1, source_target_pairs={{0,128},{1,129},{2,130},{3,131},{4,6},{5,7},{6,4},{7,5},{64,192},{... | collective-permute-start | bytes 786440 | tf_op jit(solution)/shard_map/ppermute | solution.py:32
  74.1 7.3 %collective-permute-start.11 = (bf16[8,128,128]{2,1,0:T(8,128)(2,1)S(1)}, bf16[8,128,128]{2,1,0:T(8,128)(2,1)S(1)}, u32[]{:S(2)}, u32[]{:S(2)}) collective-permute-start(bf16[8,128,128]{2,1,0:T(8,128)(2,1)S(1)} %get-tuple-element.51), channel_id=1, source_target_pairs={{0,192},{1,193},{2,194},{3,195},{4,7},{5,4},{6,5},{7,6},{64,0},{65... | collective-permute-start | bytes 786440 | tf_op jit(solution)/shard_map/ppermute | solution.py:32
  74.9 6.5 %collective-permute-start.9 = (bf16[8,128,128]{2,1,0:T(8,128)(2,1)S(1)}, bf16[8,128,128]{2,1,0:T(8,128)(2,1)S(1)}, u32[]{:S(2)}, u32[]{:S(2)}) collective-permute-start(bf16[8,128,128]{2,1,0:T(8,128)(2,1)S(1)} %get-tuple-element.49), channel_id=1, source_target_pairs={{0,64},{1,65},{2,66},{3,67},{4,5},{5,6},{6,7},{7,4},{64,128},{65,1... | collective-permute-start | bytes 786440 | tf_op jit(solution)/shard_map/ppermute | solution.py:32
  116.5 0.6 copy-start.2
